TPU v7x, 32 devices: a whole 2x2x4 slice. The times are simulated.
32 devices in a mesh: wave: 16 (over z, y, core), lev: 2 (over x).
Axes of the slice: x: 2, y: 2, z: 4, core: 2. Of those that a mesh axis runs over, the one named last changes fastest.
Arguments:
- control: bfloat16 [2, 256, 256, 2, 512], P(None, 'wave', 'lev'), may hold values from -6 to 6
- wave_of_slot: int32 [256], replicated, may hold values from 0 to 255, each once
- legendre: bfloat16 [256, 256, 256], P('wave', 'lev'), may hold values from -0.375 to 0.375
- vertical: bfloat16 [4, 4, 128, 128], replicated, may hold values from -0.5 to 0.5
- points: int32 [256], P('wave'), may hold values from 128 to 512
- lat_band: int32 [256], P('wave'), may hold values from 0 to 7, never falling along the last dimension, each value on 1 to 64 neighbouring positions
- grid_scale: float32 [8, 512], P(None, 'lev'), may hold values from 0.5 to 2
- obs_weight: bfloat16 [256, 512, 512], P('wave', 'lev'), may hold values from 0.19921875 to 1
Outputs:
- increment: bfloat16 [2, 256, 512, 512], P(None, 'wave', 'lev')
- gradient: bfloat16 [2, 256, 256, 2, 512], P(None, 'wave', 'lev')
Inputs may be any that keep to these rules, and one draw needn't show every extreme that they name: `wave_of_slot`: each zonal wavenumber 0 to 255 stands in exactly one slot. `lat_band`: band numbers never fall from one latitude to the next, and each band covers 1 to 64 latitudes.
All inputs are finite; a program needn't handle non-finite values.
Results may differ from a plain program's by a relative error of at most 0.007.
Values may be sent and summed in bfloat16 or wider, within the bound.
No kernel may reach another device: no remote copies, remote signals or barrier semaphores. Data moves between devices by JAX's collectives and lax.ppermute only.
A program may use at most 192 MiB of HBM per device.

v0:
```python
import math

import jax
import jax.numpy as jnp
from jax import lax
from jax.sharding import PartitionSpec as P

WAVES = 256
LONGITUDES = 512
LEVELS = 128
VARIABLES = 4
COV_BANDS = 4


def fourier_table(wave_ids, lat_points):
    lon_index = jnp.arange(LONGITUDES, dtype=jnp.int32)
    remainder = wave_ids[None, :, None] * lon_index[None, None, :] % lat_points[:, None, None]
    angles = (
        2.0
        * math.pi
        * remainder.astype(jnp.float32)
        / lat_points.astype(jnp.float32)[:, None, None]
    )
    factor = jnp.where(wave_ids == 0, 1.0, 2.0).astype(jnp.float32) / math.sqrt(4.0 * WAVES)
    inside = lon_index[None, None, :] < lat_points[:, None, None]
    cosine = jnp.where(inside, factor[None, :, None] * jnp.cos(angles), 0.0)
    sine = jnp.where(inside, -factor[None, :, None] * jnp.sin(angles), 0.0)
    return jnp.stack([cosine, sine], axis=2).astype(jnp.bfloat16)


def vertical_apply(field, vertical, live_rows, band_of, forward):
    members, slots, rows_dev = (field.shape[0], field.shape[1], field.shape[2])
    shaped = field.reshape(members, slots, rows_dev, 2, VARIABLES, LEVELS)
    form = "eskpam,alm->eskpal" if forward else "eskpal,alm->eskpam"
    summed = jnp.zeros(shaped.shape, jnp.float32)
    for index_band in range(COV_BANDS):
        partial_value = jnp.einsum(
            form, shaped, vertical[index_band], preferred_element_type=jnp.float32
        )
        chosen = live_rows & (band_of == index_band)
        summed = summed + jnp.where(chosen[None, :, :, None, None, None], partial_value, 0.0)
    return summed.reshape(field.shape).astype(jnp.bfloat16)


def to_bands(values):
    return lax.all_to_all(values, "wave", split_axis=2, concat_axis=1, tiled=True)


def shards(control, wave_of_slot, legendre, vertical, points, lat_band, grid_scale, obs_weight):
    members, slots, rows_dev = (control.shape[0], control.shape[1], control.shape[2])
    slot_start = lax.axis_index("wave") * slots
    row_start = lax.axis_index("lev") * rows_dev
    own_waves = lax.dynamic_slice_in_dim(wave_of_slot, slot_start, slots)
    row_index = row_start + jnp.arange(rows_dev, dtype=jnp.int32)
    totals_n = own_waves[:, None] + row_index[None, :]
    live_rows = totals_n <= WAVES - 1
    band_of = jnp.minimum(totals_n * COV_BANDS // WAVES, COV_BANDS - 1)
    spectral = vertical_apply(control, vertical, live_rows, band_of, True)
    columns = lax.all_to_all(spectral, "lev", split_axis=4, concat_axis=2, tiled=True)
    col_dev = columns.shape[4]
    width = 2 * col_dev
    all_rows = columns.shape[2]
    columns = columns.reshape(members, slots, all_rows, width)
    coeffs = jnp.einsum(
        "skt,eskq->estq",
        lax.all_gather(legendre, "lev", axis=1, tiled=True),
        columns,
        preferred_element_type=jnp.float32,
    )
    coeffs = coeffs.astype(jnp.bfloat16)
    by_lat = to_bands(coeffs)
    wave_count = by_lat.shape[1]
    lat_dev = by_lat.shape[2]
    by_lat = by_lat.reshape(members, wave_count, lat_dev, 2, col_dev)
    fourier = fourier_table(wave_of_slot, points)
    synthesis = jnp.einsum("tspj,estpc->etcj", fourier, by_lat, preferred_element_type=jnp.float32)
    chooser = (
        lat_band[:, None] == jnp.arange(grid_scale.shape[0], dtype=jnp.int32)[None, :]
    ).astype(jnp.float32)
    lat_scale = jnp.dot(chooser, grid_scale, precision=lax.Precision.HIGHEST)
    increment = (synthesis * lat_scale[None, :, :, None]).astype(jnp.bfloat16)
    weighted = (
        increment.astype(jnp.float32) * obs_weight.astype(jnp.float32) * lat_scale[None, :, :, None]
    ).astype(jnp.bfloat16)
    adjoint_fourier = jnp.einsum(
        "tspj,etcj->etspc", fourier, weighted, preferred_element_type=jnp.float32
    )
    adjoint_fourier = adjoint_fourier.astype(jnp.bfloat16).reshape(
        members, lat_dev, wave_count, width
    )
    band_rows = to_bands(adjoint_fourier)
    adjoint_coeffs = jnp.einsum(
        "skt,etsq->eskq",
        lax.all_gather(legendre, "lev", axis=1, tiled=True),
        band_rows,
        preferred_element_type=jnp.float32,
    )
    adjoint_coeffs = adjoint_coeffs.astype(jnp.bfloat16).reshape(
        members, slots, all_rows, 2, col_dev
    )
    rows_back = lax.all_to_all(adjoint_coeffs, "lev", split_axis=2, concat_axis=4, tiled=True)
    gradient = vertical_apply(rows_back, vertical, live_rows, band_of, False)
    return (increment, gradient)


def solution(mesh):
    in_specs = (
        P(None, "wave", "lev", None, None),
        P(),
        P("wave", "lev", None),
        P(),
        P("wave"),
        P("wave"),
        P(None, "lev"),
        P("wave", "lev", None),
    )
    out_specs = (P(None, "wave", "lev", None), P(None, "wave", "lev", None, None))
    return jax.shard_map(shards, mesh=mesh, in_specs=in_specs, out_specs=out_specs, check_vma=False)
```

profile of v0, /device:TPU:13, one launch (start us, length us, event | category | flops | bytes accessed | tf_op | source)
XLA Modules:
  0.0 1021.0 jit_solution(5257670310123423608)
XLA Ops:
  7.2 0.0 copy-start
  7.2 0.0 copy-start.4
  7.2 14.1 %reshape.273 = bf16[2,16,128,2,4,128]{5,4,3,2,1,0:T(4,128)(2,1)} reshape(bf16[2,16,128,2,512]{4,3,2,1,0:T(2,128)(2,1)} %param.8) | data formatting | bytes 16777216 | tf_op jit(solution)/shard_map/reshape | solution.py:33
  21.3 0.0 copy-done.4
  21.3 11.6 %fusion.28 = f32[4,128,2,16,128,2]{4,1,5,3,2,0:T(8,128)} fusion(bf16[2,16,128,2,4,128]{5,4,3,2,1,0:T(4,128)(2,1)} %reshape.273, bf16[4,4,128,128]{3,2,1,0:T(8,128)(2,1)S(1)} %copy-done.4), kind=kOutput, calls=%fused_computation.35 | convolution fusion | flops 1073741824 | bytes 25296896 | tf_op jit(solution)/shard_map/eskpam,alm->eskpal/dot_general | solution.py:37
  32.9 0.0 copy-done.2
  32.9 8.1 fusion.30
  41.0 8.1 fusion.32
  49.1 0.0 copy-done.13
  49.1 0.1 dynamic_slice.3
  49.2 0.1 fusion.68
  49.3 0.0 copy-start.5
  49.3 0.0 copy-start.7
  49.3 0.0 copy-start.9
  49.3 0.0 copy-start.11
  49.3 0.6 copy-done.5
  49.8 0.0 copy-done.7
  49.8 0.0 copy-done.9
  49.8 0.0 copy-done.11
  49.9 23.9 %fusion.34 = bf16[2,16,128,2,4,128]{2,5,3,1,0,4:T(8,128)(2,1)} fusion(bf16[2,16,128,2,4,128]{5,4,3,2,1,0:T(4,128)(2,1)} %reshape.273, pred[16,128]{1,0:T(8,128)(4,1)S(1)} %get-tuple-element.14, f32[4,128,2,16,128,2]{4,1,5,3,2,0:T(8,128)} %fusion.28, pred[16,128]{1,0:T(8,128)(4,1)S(1)} %get-tuple-element.15, f32[4,128,2,16,128,2]{4,1,5,3,2,0:T(8,128)} %fusion.30, ...), kind=kOutput, calls=%fused_computation.41 | convolution fusion | flops 1107296256 | bytes 67248128 | tf_op jit(solution)/shard_map/eskpam,alm->eskpal/dot_general | solution.py:37
  73.8 10.5 %copy.73 = bf16[2,16,128,2,4,128]{2,5,4,3,1,0:T(8,128)(2,1)} copy(bf16[2,16,128,2,4,128]{2,5,3,1,0,4:T(8,128)(2,1)} %fusion.34) | data formatting | bytes 16777216 | tf_op jit(solution)/shard_map/add | solution.py:41
  84.3 13.1 %copy.74 = bf16[2,16,128,2,512]{2,3,1,0,4:T(2,128)(2,1)} copy(bf16[2,16,128,2,512]{2,4,3,1,0:T(8,128)(2,1)} %bitcast.123) | data formatting | bytes 16777216 | tf_op jit(solution)/shard_map/convert_element_type | solution.py:42
  97.4 6.9 all-to-all-start
  104.4 0.0 all-gather.2.cloned.1.call-start
  104.5 0.7 all-gather.2.cloned.1.call-update
  105.1 113.5 %all-to-all-done = bf16[2,16,128,2,512]{2,3,1,0,4:T(2,128)(2,1)} async-done(((bf16[2,16,128,2,512]{2,3,1,0,4:T(2,128)(2,1)}), bf16[2,16,128,2,512]{2,3,1,0,4:T(2,128)(2,1)}, u32[]{:S(2)}, u32[]{:S(2)}) %all-to-all-start) | async-done | bytes 8388640 | tf_op jit(solution)/shard_map/all_to_all | solution.py:59
  218.6 16.5 %copy.75 = bf16[2,16,128,2,512]{2,4,3,1,0:T(8,128)(2,1)} copy(bf16[2,16,128,2,512]{2,3,1,0,4:T(2,128)(2,1)} %all-to-all-done) | data formatting | bytes 16777216 | tf_op jit(solution)/shard_map/all_to_all | solution.py:59
  235.1 16.8 %copy.76 = bf16[2,16,2,128,2,256]{3,2,5,4,0,1:T(2,128)(2,1)} copy(bf16[2,16,2,128,2,256]{3,5,2,4,1,0:T(8,128)(2,1)} %bitcast.124) | data formatting | bytes 16777216 | tf_op jit(solution)/shard_map/all_to_all | solution.py:59
  251.9 14.0 %reshape.274 = bf16[2,16,256,512]{2,3,0,1:T(8,128)(2,1)} reshape(bf16[2,16,2,128,2,256]{3,2,5,4,0,1:T(2,128)(2,1)} %copy.76) | data formatting | bytes 16777216 | tf_op jit(solution)/shard_map/reshape | solution.py:63
  265.9 9.7 convert_bitcast_fusion
  275.6 21.1 %copy.77 = bf16[2,16,256,512]{3,0,1,2:T(2,128)(2,1)} copy(bf16[2,16,256,512]{2,3,0,1:T(8,128)(2,1)} %convert_bitcast_fusion) | data formatting | bytes 16777216 | tf_op jit(solution)/shard_map/convert_element_type | solution.py:70
  296.7 7.4 all-to-all-start.1
  304.1 0.0 copy-start.15
  304.1 6.6 convert_element_type.68
  310.6 0.0 copy-done.14
  310.7 0.1 iota_compare_fusion
  310.8 0.0 copy-done.15
  310.8 0.2 fusion.73
  311.0 0.1 iota_multiply_fusion
  311.1 121.6 %select_convert_fusion.1 = (bf16[16,256,1,512]{3,1,2,0:T(8,128)(2,1)}, bf16[16,256,1,512]{3,1,2,0:T(8,128)(2,1)}) fusion(f32[256]{0:T(256)S(1)} %get-tuple-element.16, f32[16]{0:T(128)S(1)} %get-tuple-element.19, pred[16]{0:T(512)(128)(4,1)S(1)} %broadcast_compare_fusion, s32[16]{0:T(128)S(1)} %get-tuple-element.18, s32[256,512]{1,0:T(8,128)S(1)} %iota_multiply_fusion, ...), kind=kLoop, calls=%fused_computation.21 | loop fusion | flops 33554432 | bytes 8923280 | tf_op jit(solution)/shard_map/convert.1
  432.7 53.7 %all-to-all-done.1 = bf16[2,16,256,512]{3,0,1,2:T(2,128)(2,1)} async-done(((bf16[2,16,256,512]{3,0,1,2:T(2,128)(2,1)}), bf16[2,16,256,512]{3,0,1,2:T(2,128)(2,1)}, u32[]{:S(2)}, u32[]{:S(2)}) %all-to-all-start.1) | async-done | bytes 8388640 | tf_op jit(solution)/shard_map/all_to_all | solution.py:46
  486.4 11.5 %copy.78 = bf16[2,16,256,512]{3,2,1,0:T(8,128)(2,1)} copy(bf16[2,16,256,512]{3,0,1,2:T(2,128)(2,1)} %all-to-all-done.1) | data formatting | bytes 16777216 | tf_op jit(solution)/shard_map/all_to_all | solution.py:46
  497.9 8.2 copy.79
  506.1 12.5 %reshape.275 = bf16[2,256,16,2,256]{4,3,2,1,0:T(2,128)(2,1)} reshape(bf16[2,16,16,16,512]{4,3,2,1,0:T(8,128)(2,1)} %copy.79) | data formatting | bytes 16777216 | tf_op jit(solution)/shard_map/reshape | solution.py:74
  518.6 17.3 %fusion.40 = bf16[2,16,256,512]{3,2,0,1:T(8,128)(2,1)} fusion(f32[16,256]{1,0:T(8,128)S(1)} %fusion.73, bf16[16,256,1,512]{3,1,2,0:T(8,128)(2,1)} %get-tuple-element.11, bf16[16,256,1,512]{3,1,2,0:T(8,128)(2,1)} %get-tuple-element.10, bf16[2,256,16,2,256]{4,3,2,1,0:T(2,128)(2,1)} %reshape.275), kind=kOutput, calls=%fused_computation.43 | convolution fusion | flops 4307550208 | bytes 25182208 | tf_op jit(solution)/shard_map/tspj,estpc->etcj/dot_general | solution.py:76
  535.9 13.4 %fusion.17 = bf16[16,2,256,256,2]{3,2,4,1,0:T(8,128)(2,1)} fusion(bf16[2,16,256,512]{3,2,0,1:T(8,128)(2,1)} %fusion.40, f32[16,256]{1,0:T(8,128)S(1)} %fusion.73, f32[16,256,512]{2,1,0:T(8,128)} %convert_element_type.68, bf16[16,256,1,512]{3,1,2,0:T(8,128)(2,1)} %get-tuple-element.11, bf16[16,256,1,512]{3,1,2,0:T(8,128)(2,1)} %get-tuple-element.10), kind=kOutput, calls=%fused_computation.26 | convolution fusion | flops 4332716032 | bytes 33570816 | tf_op jit(solution)/shard_map/tspj,etcj->etspc/dot_general | solution.py:85
  549.3 14.6 %copy.81 = bf16[2,16,256,512]{3,1,0,2:T(8,128)(2,1)} copy(bf16[2,16,256,512]{2,3,0,1:T(8,128)(2,1)} %bitcast.129) | data formatting | bytes 16777216 | tf_op jit(solution)/shard_map/reshape | solution.py:88
  563.8 187.0 %all_to_all.63 = bf16[2,16,256,512]{3,1,0,2:T(8,128)(2,1)} all-to-all(bf16[2,16,256,512]{3,1,0,2:T(8,128)(2,1)} %copy.81), channel_id=1, replica_groups=mesh['wave'=16,'lev'=2] {'wave'}, dimensions={2} | all-to-all | bytes 16777216 | tf_op jit(solution)/shard_map/all_to_all | solution.py:46
  750.8 15.5 %copy.83 = bf16[2,16,16,16,512]{4,3,2,1,0:T(8,128)(2,1)} copy(bf16[2,16,16,16,512]{4,2,0,3,1:T(8,128)(2,1)} %bitcast.126) | data formatting | bytes 16777216 | tf_op jit(solution)/shard_map/all_to_all | solution.py:46
  766.3 12.7 %fusion.14 = bf16[16,2,512,256]{3,2,1,0:T(8,128)(2,1)} fusion(bf16[2,256,16,512]{3,2,1,0:T(8,128)(2,1)} %bitcast.121, bf16[16,256,256]{2,1,0:T(8,128)(2,1)S(1)} %copy-done.3), kind=kOutput, calls=%fused_computation.25 | convolution fusion | flops 2151677952 | bytes 18874368 | tf_op jit(solution)/shard_map/skt,etsq->eskq/dot_general | solution.py:92
  778.9 21.1 %copy.85 = bf16[2,16,256,2,256]{4,3,1,0,2:T(2,128)(2,1)} copy(bf16[2,16,256,2,256]{2,4,3,0,1:T(8,128)(2,1)} %bitcast.122) | data formatting | bytes 16777216 | tf_op jit(solution)/shard_map/reshape | solution.py:98
  800.0 7.0 all-to-all-start.3
  807.0 7.7 copy.97
  814.7 84.7 %all-to-all-done.3 = bf16[2,16,256,2,256]{4,3,1,0,2:T(2,128)(2,1)} async-done(((bf16[2,16,256,2,256]{4,3,1,0,2:T(2,128)(2,1)}), bf16[2,16,256,2,256]{4,3,1,0,2:T(2,128)(2,1)}, u32[]{:S(2)}, u32[]{:S(2)}) %all-to-all-start.3) | async-done | bytes 8388640 | tf_op jit(solution)/shard_map/all_to_all | solution.py:101
  899.3 13.6 %copy.86 = bf16[2,16,256,2,256]{4,2,3,1,0:T(8,128)(2,1)} copy(bf16[2,16,256,2,256]{4,3,1,0,2:T(2,128)(2,1)} %all-to-all-done.3) | data formatting | bytes 16777216 | tf_op jit(solution)/shard_map/all_to_all | solution.py:101
  913.0 12.1 %copy.87 = bf16[2,16,128,2,2,256]{2,5,4,3,1,0:T(8,128)(2,1)} copy(bf16[2,16,128,2,2,256]{5,2,4,3,1,0:T(8,128)(2,1)} %bitcast.127) | data formatting | bytes 16777216 | tf_op jit(solution)/shard_map/all_to_all | solution.py:101
  925.0 11.5 %fusion.21 = f32[4,2,16,128,2,128]{3,5,4,2,1,0:T(8,128)} fusion(bf16[2,16,128,2,4,128]{2,5,4,3,1,0:T(8,128)(2,1)} %bitcast.117, bf16[4,4,128,128]{3,2,1,0:T(8,128)(2,1)S(1)} %copy-done.4), kind=kOutput, calls=%fused_computation.28 | convolution fusion | flops 1073741824 | bytes 25296896 | tf_op jit(solution)/shard_map/eskpal,alm->eskpam/dot_general | solution.py:37
  936.5 11.5 %fusion.23 = f32[4,2,16,128,2,128]{3,5,4,2,1,0:T(8,128)} fusion(bf16[2,16,128,2,4,128]{2,5,4,3,1,0:T(8,128)(2,1)} %bitcast.118, bf16[4,4,128,128]{3,2,1,0:T(8,128)(2,1)S(1)} %copy-done.4), kind=kOutput, calls=%fused_computation.30 | convolution fusion | flops 1073741824 | bytes 25296896 | tf_op jit(solution)/shard_map/eskpal,alm->eskpam/dot_general | solution.py:37
  948.0 11.5 %fusion.25 = f32[4,2,16,128,2,128]{3,5,4,2,1,0:T(8,128)} fusion(bf16[2,16,128,2,4,128]{2,5,4,3,1,0:T(8,128)(2,1)} %bitcast.119, bf16[4,4,128,128]{3,2,1,0:T(8,128)(2,1)S(1)} %copy-done.4), kind=kOutput, calls=%fused_computation.32 | convolution fusion | flops 1073741824 | bytes 25296896 | tf_op jit(solution)/shard_map/eskpal,alm->eskpam/dot_general | solution.py:37
  959.5 0.0 copy-done.12
  959.5 23.0 %fusion.37 = bf16[2,16,128,2,4,128]{2,5,3,1,0,4:T(8,128)(2,1)} fusion(bf16[2,16,128,2,4,128]{2,5,4,3,1,0:T(8,128)(2,1)} %bitcast.120, pred[16,128]{1,0:T(8,128)(4,1)S(1)} %copy-done.10, f32[4,2,16,128,2,128]{3,5,4,2,1,0:T(8,128)} %fusion.21, pred[16,128]{1,0:T(8,128)(4,1)S(1)} %copy-done.12, f32[4,2,16,128,2,128]{3,5,4,2,1,0:T(8,128)} %fusion.23, ...), kind=kOutput, calls=%fused_computation.42 | convolution fusion | flops 1107296256 | bytes 67248128 | tf_op jit(solution)/shard_map/eskpal,alm->eskpam/dot_general | solution.py:37
  982.5 10.4 %copy.96 = bf16[2,16,128,2,4,128]{2,5,4,3,1,0:T(8,128)(2,1)} copy(bf16[2,16,128,2,4,128]{2,5,3,1,0,4:T(8,128)(2,1)} %fusion.37) | data formatting | bytes 16777216 | tf_op jit(solution)/shard_map/add | solution.py:41
  992.9 21.1 %copy.98 = bf16[2,16,128,2,512]{4,3,2,1,0:T(2,128)(2,1)} copy(bf16[2,16,128,2,512]{2,4,3,1,0:T(8,128)(2,1)} %bitcast.128) | data formatting | bytes 16777216
  1014.0 0.0 copy-done.1
  (19 shorter events, 0.0 us)
Async XLA Ops:
  7.2 303.6 %copy-start = (f32[8,256]{1,0:T(8,128)S(1)}, f32[8,256]{1,0:T(8,128)}, u32[]{:S(2)}) copy-start(f32[8,256]{1,0:T(8,128)} %param.14) | copy-start | bytes 24580
  7.2 14.1 %copy-start.4 = (bf16[4,4,128,128]{3,2,1,0:T(8,128)(2,1)S(1)}, bf16[4,4,128,128]{3,2,1,0:T(8,128)(2,1)}, u32[]{:S(2)}) copy-start(bf16[4,4,128,128]{3,2,1,0:T(8,128)(2,1)} %param.11) | copy-start | bytes 1572868
  21.3 11.6 %copy-start.2 = (bf16[2,16,128,2,4,128]{5,4,3,2,1,0:T(4,128)(2,1)S(1)}, bf16[2,16,128,2,4,128]{5,4,3,2,1,0:T(4,128)(2,1)}, u32[]{:S(2)}) copy-start(bf16[2,16,128,2,4,128]{5,4,3,2,1,0:T(4,128)(2,1)} %reshape.273) | copy-start | bytes 25165828
  41.0 8.1 copy-start.13
  49.3 0.6 copy-start.5
  49.3 0.6 copy-start.7
  49.3 0.6 copy-start.9
  49.3 0.6 copy-start.11
  97.4 121.2 %all-to-all-start = ((bf16[2,16,128,2,512]{2,3,1,0,4:T(2,128)(2,1)}), bf16[2,16,128,2,512]{2,3,1,0,4:T(2,128)(2,1)}, u32[]{:S(2)}, u32[]{:S(2)}) async-start(bf16[2,16,128,2,512]{2,3,1,0,4:T(2,128)(2,1)} %copy.74), calls=%async_computation | async-start | bytes 16777216 | tf_op jit(solution)/shard_map/all_to_all | solution.py:59
  104.4 161.5 %all-gather.2.cloned.1.call-start = ((), (), s32[]{:S(2)}) async-start(), calls=%async_computation.4 | async-start | bytes 3145728 | tf_op jit(solution)/shard_map/all_gather | solution.py:66
  296.7 189.7 %all-to-all-start.1 = ((bf16[2,16,256,512]{3,0,1,2:T(2,128)(2,1)}), bf16[2,16,256,512]{3,0,1,2:T(2,128)(2,1)}, u32[]{:S(2)}, u32[]{:S(2)}) async-start(bf16[2,16,256,512]{3,0,1,2:T(2,128)(2,1)} %copy.77), calls=%async_computation.1 | async-start | bytes 16777216 | tf_op jit(solution)/shard_map/all_to_all | solution.py:46
  304.1 6.6 copy-start.14
  304.1 6.7 copy-start.15
  750.8 15.5 %copy-start.3 = (bf16[16,256,256]{2,1,0:T(8,128)(2,1)S(1)}, bf16[16,256,256]{2,1,0:T(8,128)(2,1)}, u32[]{:S(2)}) copy-start(bf16[16,256,256]{2,1,0:T(8,128)(2,1)} %all-gather.2.cloned.1.call-done) | copy-start | bytes 6291460
  800.0 99.3 %all-to-all-start.3 = ((bf16[2,16,256,2,256]{4,3,1,0,2:T(2,128)(2,1)}), bf16[2,16,256,2,256]{4,3,1,0,2:T(2,128)(2,1)}, u32[]{:S(2)}, u32[]{:S(2)}) async-start(bf16[2,16,256,2,256]{4,3,1,0,2:T(2,128)(2,1)} %copy.85), calls=%async_computation.3 | async-start | bytes 16777216 | tf_op jit(solution)/shard_map/all_to_all | solution.py:101
  948.0 11.5 %copy-start.6 = (pred[16,128]{1,0:T(8,128)(4,1)S(1)}, pred[16,128]{1,0:T(8,128)(4,1)}, u32[]{:S(2)}) copy-start(pred[16,128]{1,0:T(8,128)(4,1)} %copy-done.5) | copy-start | bytes 6148
  948.0 11.5 %copy-start.8 = (pred[16,128]{1,0:T(8,128)(4,1)S(1)}, pred[16,128]{1,0:T(8,128)(4,1)}, u32[]{:S(2)}) copy-start(pred[16,128]{1,0:T(8,128)(4,1)} %copy-done.7) | copy-start | bytes 6148
  948.0 11.5 %copy-start.10 = (pred[16,128]{1,0:T(8,128)(4,1)S(1)}, pred[16,128]{1,0:T(8,128)(4,1)}, u32[]{:S(2)}) copy-start(pred[16,128]{1,0:T(8,128)(4,1)} %copy-done.9) | copy-start | bytes 6148
  948.0 11.5 %copy-start.12 = (pred[16,128]{1,0:T(8,128)(4,1)S(1)}, pred[16,128]{1,0:T(8,128)(4,1)}, u32[]{:S(2)}) copy-start(pred[16,128]{1,0:T(8,128)(4,1)} %copy-done.11) | copy-start | bytes 6148
  992.9 21.1 %copy-start.1 = (f32[8,256]{1,0:T(8,128)S(1)}, f32[8,256]{1,0:T(8,128)}, u32[]{:S(2)}) copy-start(f32[8,256]{1,0:T(8,128)} %param.14) | copy-start | bytes 24580
Sparse Core Ops, SparseCore 0:
  106.8 57.2 all-gather.1
where the time goes:
time: 1030 us; the launch traced here: 1020 us
  local copies, waits for them, and re-layouts  255 us (25%)
  waiting for transfers between devices  253 us (25%)
  blocking collectives  187 us (18%)
  matrix products  162 us (16%)
  other arithmetic  128 us (12%)
  starting transfers between devices  21.4 us (2%)
  between operations  14.4 us (1%)
    all_to_all x1, blocking collectives, to_bands(): lax.all_to_all(values, 'wave', split_axis=2, concat_axis=1, tiled=True)  187 us
    another operation x1, other arithmetic  122 us
    all_to_all x1, waiting for transfers between devices, shards(): lax.all_to_all(spectral, 'lev', split_axis=4, concat_axis=2, tiled=True)  113 us
    dot_general x8, matrix products, vertical_apply(): jnp.einsum(form, shaped, vertical[index_band], preferred_element_type=jnp...  109 us
    all_to_all x1, waiting for transfers between devices, shards(): lax.all_to_all(adjoint_coeffs, 'lev', split_axis=2, concat_axis=4, tiled=...  84.7 us
    all_to_all x1, waiting for transfers between devices, to_bands(): lax.all_to_all(values, 'wave', split_axis=2, concat_axis=1, tiled=True)  53.7 us
    all_to_all x3, local copies, waits for them, and re-layouts, to_bands(): lax.all_to_all(values, 'wave', split_axis=2, concat_axis=1, tiled=True)  35.2 us
    all_to_all x2, local copies, waits for them, and re-layouts, shards(): lax.all_to_all(spectral, 'lev', split_axis=4, concat_axis=2, tiled=True)  33.2 us
  transfers between devices with their start and end apart: 4, of which 3 were waited for; matrix products, arithmetic and copies ran while one was open for 18% of the time, Pallas kernels for 0%

commit v1 on v0

--- a/solution.py
+++ b/solution.py
@@ -1,8 +1,11 @@
+import functools
 import math
 
 import jax
 import jax.numpy as jnp
 from jax import lax
+from jax.experimental import pallas as pl
+from jax.experimental.pallas import tpu as pltpu
 from jax.sharding import PartitionSpec as P
 
 WAVES = 256
@@ -10,6 +13,340 @@
 LEVELS = 128
 VARIABLES = 4
 COV_BANDS = 4
+LANES = 128
+
+BF16 = jnp.bfloat16
+F32 = jnp.float32
+
+
+def params(*semantics):
+    return pltpu.CompilerParams(dimension_semantics=semantics, vmem_limit_bytes=56 << 20)
+
+
+def cost(flops, nbytes):
+    return pl.CostEstimate(flops=int(flops), bytes_accessed=int(nbytes), transcendentals=0)
+
+
+def dot(a, b, contract):
+    return lax.dot_general(a, b, (contract, ((), ())), preferred_element_type=F32)
+
+
+def band_masked(rows, first_total):
+    row_total = first_total + lax.broadcasted_iota(jnp.int32, rows.shape, 0) // 2
+    width = WAVES // COV_BANDS
+    parts = []
+    for band in range(COV_BANDS):
+        inside = (row_total >= band * width) & (row_total < (band + 1) * width)
+        parts.append(jnp.where(inside, rows, jnp.zeros_like(rows)))
+    return jnp.concatenate(parts, axis=1)
+
+
+def vertical_fwd_body(info, waves, xo, xs, vo, vs, own, send, scratch):
+    rows_dev = own.shape[1]
+    first_total = waves[pl.program_id(0)] + info[0] * rows_dev
+    for x, v, out in ((xo, vo, own), (xs, vs, send)):
+        rows = x[0, 0].reshape(2 * rows_dev, LEVELS)
+        matrix = jnp.concatenate([v[band, 0] for band in range(COV_BANDS)], axis=1)
+        scratch[...] = dot(band_masked(rows, first_total), matrix, ((1,), (1,)))
+        for part in range(2):
+            out[0, :, part * LEVELS : (part + 1) * LEVELS] = scratch[
+                pl.ds(part, rows_dev, stride=2), :
+            ].astype(BF16)
+
+
+def vertical_fwd(control, vertical, info, waves, member, sub, subs):
+    _, slots, rows_dev, _, _ = control.shape
+    block = (1, 1, rows_dev, 2, LEVELS)
+    vblock = (COV_BANDS, 1, LEVELS, LEVELS)
+    oblock = (1, rows_dev, 2 * LEVELS)
+    mine = lambda info: info[0] * subs + sub
+    other = lambda info: (1 - info[0]) * subs + sub
+    shape = jax.ShapeDtypeStruct((slots, rows_dev, 2 * LEVELS), BF16)
+    return pl.pallas_call(
+        vertical_fwd_body,
+        grid_spec=pltpu.PrefetchScalarGridSpec(
+            num_scalar_prefetch=2,
+            grid=(slots,),
+            in_specs=[
+                pl.BlockSpec(block, lambda s, info, w: (member, s, 0, 0, mine(info))),
+                pl.BlockSpec(block, lambda s, info, w: (member, s, 0, 0, other(info))),
+                pl.BlockSpec(vblock, lambda s, info, w: (0, mine(info), 0, 0)),
+                pl.BlockSpec(vblock, lambda s, info, w: (0, other(info), 0, 0)),
+            ],
+            out_specs=[
+                pl.BlockSpec(oblock, lambda s, info, w: (s, 0, 0)),
+                pl.BlockSpec(oblock, lambda s, info, w: (s, 0, 0)),
+            ],
+            scratch_shapes=[pltpu.VMEM((2 * rows_dev, LEVELS), F32)],
+        ),
+        out_shape=[shape, shape],
+        compiler_params=params("arbitrary"),
+        cost_estimate=cost(16 * slots * rows_dev * COV_BANDS * LEVELS * LEVELS, 8 * slots * rows_dev * 256),
+        name="vertical_fwd",
+    )(info, waves, control, control, vertical, vertical)
+
+
+def vertical_adj_body(info, waves, own, other, v, *rest):
+    out, scratch = rest[-2:]
+    rows_dev = own.shape[1]
+    first_total = waves[pl.program_id(0)] + info[0] * rows_dev
+
+    def run(block):
+        for part in range(2):
+            scratch[pl.ds(part, rows_dev, stride=2), :] = block[
+                0, :, part * LEVELS : (part + 1) * LEVELS
+            ].astype(F32)
+        rows = scratch[...].astype(BF16)
+        matrix = v[:, 0].reshape(COV_BANDS * LEVELS, LEVELS)
+        total = dot(band_masked(rows, first_total), matrix, ((1,), (0,)))
+        out[0, 0] = total.astype(BF16).reshape(rows_dev, 2, LEVELS)
+
+    pl.when(pl.program_id(1) == 0)(lambda: run(own))
+    pl.when(pl.program_id(1) == 1)(lambda: run(other))
+
+
+def vertical_adj(own, other, vertical, info, waves, member, sub, subs, shape, into):
+    _, slots, rows_dev, _, _ = shape
+    block = (1, 1, rows_dev, 2, LEVELS)
+    iblock = (1, rows_dev, 2 * LEVELS)
+    column = lambda r, info: (info[0] + r - 2 * info[0] * r) * subs + sub
+    in_specs = [
+        pl.BlockSpec(iblock, lambda s, r, info, w: (s, 0, 0)),
+        pl.BlockSpec(iblock, lambda s, r, info, w: (s, 0, 0)),
+        pl.BlockSpec((COV_BANDS, 1, LEVELS, LEVELS), lambda s, r, info, w: (0, column(r, info), 0, 0)),
+    ]
+    operands = [info, waves, own, other, vertical]
+    aliases = {}
+    if into is not None:
+        in_specs.append(pl.BlockSpec(memory_space=pl.ANY))
+        operands.append(into)
+        aliases = {5: 0}
+    return pl.pallas_call(
+        vertical_adj_body,
+        grid_spec=pltpu.PrefetchScalarGridSpec(
+            num_scalar_prefetch=2,
+            grid=(slots, 2),
+            in_specs=in_specs,
+            out_specs=pl.BlockSpec(block, lambda s, r, info, w: (member, s, 0, 0, column(r, info))),
+            scratch_shapes=[pltpu.VMEM((2 * rows_dev, LEVELS), F32)],
+        ),
+        out_shape=jax.ShapeDtypeStruct(shape, BF16),
+        input_output_aliases=aliases,
+        compiler_params=params("arbitrary", "arbitrary"),
+        cost_estimate=cost(16 * slots * rows_dev * COV_BANDS * LEVELS * LEVELS, 8 * slots * rows_dev * 256),
+        name="vertical_adj",
+    )(*operands)
+
+
+def legendre_fwd_body(lo, lx, own, recv, out, scratch):
+    slot = pl.program_id(0)
+    groups, lats, slots, width = out.shape
+    total = dot(lo[0], own[0], ((0,), (0,))) + dot(lx[0], recv[0], ((0,), (0,)))
+    for tile in range(width // LANES):
+        scratch[tile, pl.ds(slot, groups * lats, stride=slots), :] = total[:, tile * LANES : (tile + 1) * LANES]
+
+    @pl.when(slot == slots - 1)
+    def _():
+        for group in range(groups):
+            for tile in range(width // LANES):
+                rows = scratch[tile, group * lats * slots : (group + 1) * lats * slots, :]
+                out[group, :, :, tile * LANES : (tile + 1) * LANES] = rows.astype(BF16).reshape(lats, slots, LANES)
+
+
+def legendre_fwd(leg_own, leg_other, own, recv, groups):
+    slots, rows_dev, latitudes = leg_own.shape
+    width = own.shape[2]
+    lats = latitudes // groups
+    row = pl.BlockSpec((1, rows_dev, latitudes), lambda s: (s, 0, 0))
+    col = pl.BlockSpec((1, rows_dev, width), lambda s: (s, 0, 0))
+    shape = (groups, lats, slots, width)
+    return pl.pallas_call(
+        legendre_fwd_body,
+        grid=(slots,),
+        in_specs=[row, row, col, col],
+        out_specs=pl.BlockSpec(shape, lambda s: (0, 0, 0, 0)),
+        out_shape=jax.ShapeDtypeStruct(shape, BF16),
+        scratch_shapes=[pltpu.VMEM((width // LANES, latitudes * slots, LANES), F32)],
+        compiler_params=params("arbitrary"),
+        cost_estimate=cost(4 * slots * rows_dev * latitudes * width, 8 * slots * rows_dev * width),
+        name="legendre_fwd",
+    )(leg_own, leg_other, own, recv)
+
+
+def legendre_adj_body(lo, lx, band, own, send, scratch):
+    slot = pl.program_id(0)
+    groups, lats, slots, width = band.shape
+
+    @pl.when(slot == 0)
+    def _():
+        for group in range(groups):
+            for tile in range(width // LANES):
+                rows = band[group, :, :, tile * LANES : (tile + 1) * LANES].reshape(lats * slots, LANES)
+                scratch[tile, group * lats * slots : (group + 1) * lats * slots, :] = rows.astype(F32)
+
+    rows = jnp.concatenate(
+        [scratch[tile, pl.ds(slot, groups * lats, stride=slots), :] for tile in range(width // LANES)], axis=1
+    ).astype(BF16)
+    own[0] = dot(lo[0], rows, ((1,), (0,))).astype(BF16)
+    send[0] = dot(lx[0], rows, ((1,), (0,))).astype(BF16)
+
+
+def legendre_adj(leg_own, leg_other, band_rows):
+    slots, rows_dev, latitudes = leg_own.shape
+    width = band_rows.shape[3]
+    row = pl.BlockSpec((1, rows_dev, latitudes), lambda s: (s, 0, 0))
+    col = pl.BlockSpec((1, rows_dev, width), lambda s: (s, 0, 0))
+    shape = jax.ShapeDtypeStruct((slots, rows_dev, width), BF16)
+    return pl.pallas_call(
+        legendre_adj_body,
+        grid=(slots,),
+        in_specs=[row, row, pl.BlockSpec(band_rows.shape, lambda s: (0, 0, 0, 0))],
+        out_specs=[col, col],
+        out_shape=[shape, shape],
+        scratch_shapes=[pltpu.VMEM((width // LANES, latitudes * slots, LANES), F32)],
+        compiler_params=params("arbitrary"),
+        cost_estimate=cost(4 * slots * rows_dev * latitudes * width, 8 * slots * rows_dev * width),
+        name="legendre_adj",
+    )(leg_own, leg_other, band_rows)
+
+
+def table_body(points, waves, cosine, sine):
+    count_i = points[pl.program_id(0)]
+    count = jnp.full((1, 1), count_i, jnp.int32).astype(F32)
+    inverse = 1.0 / count
+    wave = waves[...]
+    lon_i = lax.broadcasted_iota(jnp.int32, cosine.shape[1:], 1)
+    product = wave * lon_i.astype(F32)
+    rest = product - jnp.floor(product * inverse) * count
+    rest = jnp.where(rest < 0.0, rest + count, rest)
+    rest = jnp.where(rest >= count, rest - count, rest)
+    quarters = rest * (4.0 * inverse)
+    whole = jnp.floor(quarters + 0.5)
+    x = (quarters - whole) * (0.5 * math.pi)
+    y = x * x
+    s = x * (1.0 + y * (-1.0 / 6 + y * (1.0 / 120 + y * (-1.0 / 5040 + y * (1.0 / 362880)))))
+    c = 1.0 + y * (-0.5 + y * (1.0 / 24 + y * (-1.0 / 720 + y * (1.0 / 40320))))
+    turn = whole.astype(jnp.int32)
+    odd = (turn & 1) != 0
+    factor = jnp.where(wave == 0.0, 1.0, 2.0) / math.sqrt(4.0 * WAVES)
+    factor = jnp.where(lon_i < count_i, factor, 0.0)
+    cos_factor = jnp.where(((turn + 1) & 2) != 0, -factor, factor)
+    sin_factor = jnp.where((turn & 2) != 0, factor, -factor)
+    cosine[0] = (cos_factor * jnp.where(odd, s, c)).astype(BF16)
+    sine[0] = (sin_factor * jnp.where(odd, c, s)).astype(BF16)
+
+
+def fourier_tables(points, wave_of_slot):
+    lats, count = points.shape[0], wave_of_slot.shape[0]
+    shape = jax.ShapeDtypeStruct((lats, count, LONGITUDES), BF16)
+    block = pl.BlockSpec((1, count, LONGITUDES), lambda t, n: (t, 0, 0))
+    return pl.pallas_call(
+        table_body,
+        grid_spec=pltpu.PrefetchScalarGridSpec(
+            num_scalar_prefetch=1,
+            grid=(lats,),
+            in_specs=[pl.BlockSpec((count, 1), lambda t, n: (0, 0))],
+            out_specs=[block, block],
+        ),
+        out_shape=[shape, shape],
+        compiler_params=params("arbitrary"),
+        cost_estimate=cost(40 * lats * count * LONGITUDES, 4 * lats * count * LONGITUDES),
+        name="fourier_tables",
+    )(points, wave_of_slot.astype(F32)[:, None])
+
+
+def grid_body(by_lat, cosine, sine, scale, weight, *rest):
+    increment, adjoint = rest[-2:]
+    groups, _, slots, width = by_lat.shape
+    half = width // 2
+    rows = by_lat[:, 0].reshape(groups * slots, width)
+    synthesis = dot(rows[:, :half], cosine[0], ((0,), (0,)))
+    synthesis = synthesis + dot(rows[:, half:], sine[0], ((0,), (0,)))
+    lat_scale = scale[0]
+    inc = (synthesis * lat_scale).astype(BF16)
+    increment[0, 0] = inc
+    weighted = (inc.astype(F32) * weight[0].astype(F32) * lat_scale).astype(BF16)
+    for part, table in ((0, cosine), (1, sine)):
+        total = dot(table[0], weighted, ((1,), (1,))).astype(BF16)
+        adjoint[:, 0, :, part * half : (part + 1) * half] = total.reshape(groups, slots, half)
+
+
+def grid_stage(by_lat, tables, lat_scale, obs_weight, member, sub, shape, into):
+    groups, lats, slots, width = by_lat.shape
+    half = width // 2
+    count = groups * slots
+    table = pl.BlockSpec((1, count, LONGITUDES), lambda t: (t, 0, 0))
+    lat_rows = pl.BlockSpec((groups, 1, slots, width), lambda t: (0, t, 0, 0))
+    in_specs = [
+        lat_rows,
+        table,
+        table,
+        pl.BlockSpec((1, half, 1), lambda t: (t, sub, 0)),
+        pl.BlockSpec((1, half, LONGITUDES), lambda t: (t, sub, 0)),
+    ]
+    operands = [by_lat, *tables, lat_scale, obs_weight]
+    aliases = {}
+    if into is not None:
+        in_specs.append(pl.BlockSpec(memory_space=pl.ANY))
+        operands.append(into)
+        aliases = {5: 0}
+    return pl.pallas_call(
+        grid_body,
+        grid=(lats,),
+        in_specs=in_specs,
+        out_specs=[
+            pl.BlockSpec((1, 1, half, LONGITUDES), lambda t: (member, t, sub, 0)),
+            lat_rows,
+        ],
+        out_shape=[jax.ShapeDtypeStruct(shape, BF16), jax.ShapeDtypeStruct(by_lat.shape, BF16)],
+        input_output_aliases=aliases,
+        compiler_params=params("arbitrary"),
+        cost_estimate=cost(4 * lats * count * LONGITUDES * width, 6 * lats * count * LONGITUDES),
+        name="grid_stage",
+    )(*operands)
+
+
+def swap(values):
+    return lax.ppermute(values, "lev", [(0, 1), (1, 0)])
+
+
+def exchange(values):
+    return lax.all_to_all(values, "wave", split_axis=0, concat_axis=0, tiled=True)
+
+
+def chunked(control, wave_of_slot, legendre, vertical, points, lat_band, grid_scale, obs_weight):
+    members, slots, rows_dev = control.shape[:3]
+    groups = legendre.shape[2] // points.shape[0]
+    lats, col_dev, _ = obs_weight.shape
+    subs = col_dev // LEVELS
+    info = lax.axis_index("lev").astype(jnp.int32)[None]
+    waves = lax.dynamic_slice_in_dim(wave_of_slot, lax.axis_index("wave") * slots, slots)
+    chooser = (
+        lat_band[:, None] == jnp.arange(grid_scale.shape[0], dtype=jnp.int32)[None, :]
+    ).astype(F32)
+    lat_scale = jnp.dot(chooser, grid_scale, precision=lax.Precision.HIGHEST)[:, :, None]
+    chunks = [(member, sub) for member in range(members) for sub in range(subs)]
+
+    leg_other = swap(legendre)
+    received = []
+    for member, sub in chunks:
+        own, send = vertical_fwd(control, vertical, info, waves, member, sub, subs)
+        received.append((own, swap(send)))
+    tables = fourier_tables(points, wave_of_slot)
+    increment = gradient = None
+    bands = []
+    for (member, sub), (own, recv) in zip(chunks, received):
+        by_lat = exchange(legendre_fwd(legendre, leg_other, own, recv, groups))
+        increment, adjoint = grid_stage(
+            by_lat, tables, lat_scale, obs_weight, member, sub, (members, lats, col_dev, LONGITUDES), increment
+        )
+        bands.append(adjoint)
+    for (member, sub), adjoint in zip(chunks, bands):
+        own, send = legendre_adj(legendre, leg_other, exchange(adjoint))
+        gradient = vertical_adj(
+            own, swap(send), vertical, info, waves, member, sub, subs, control.shape, gradient
+        )
+    return (increment, gradient)
 
 
 def fourier_table(wave_ids, lat_points):
@@ -115,4 +452,13 @@
         P("wave", "lev", None),
     )
     out_specs = (P(None, "wave", "lev", None), P(None, "wave", "lev", None, None))
-    return jax.shard_map(shards, mesh=mesh, in_specs=in_specs, out_specs=out_specs, check_vma=False)
+
+    def body(control, *rest):
+        levs = mesh.shape["lev"]
+        slots, rows_dev = control.shape[1:3]
+        whole_blocks = slots % 16 == 0 and rows_dev % 16 == 0 and rest[3].shape[0] % 16 == 0
+        if levs == 2 and control.shape[4] % (levs * LEVELS) == 0 and whole_blocks:
+            return chunked(control, *rest)
+        return shards(control, *rest)
+
+    return jax.shard_map(body, mesh=mesh, in_specs=in_specs, out_specs=out_specs, check_vma=False)

time: 1030 us -> 657 us (0.64)
  Pallas kernels: 0 us -> 342 us
  local copies, waits for them, and re-layouts: 255 us -> 15.3 us
  matrix products: 162 us -> 0.19 us
  other arithmetic: 128 us -> 0.01 us
  waiting for transfers between devices: 253 us -> 136 us
  blocking collectives: 187 us -> 106 us
  starting transfers between devices: 21.4 us -> 47 us
  between operations: 14.4 us -> 0.71 us
    pallas_call x0 -> x21, Pallas kernels: none -> 342 us  [the longest x4 91.4 us: vertical_adj(): pl.pallas_call(vertical_adj_body, grid_spec=pltpu.PrefetchScalarGridSpec(...]
    all_to_all x3 -> x6, waiting for transfers between devices: 252 us -> 40.3 us  [exchange(): lax.all_to_all(values, 'wave', split_axis=0, concat_axis=0, tiled=True)]
    dot_general x13 -> x1, matrix products: 162 us -> 0.19 us  [chunked(): jnp.dot(chooser, grid_scale, precision=lax.Precision.HIGHEST)[:, :, None]]
    another operation x1 -> x0, other arithmetic: 122 us -> none
    ppermute x0 -> x9, waiting for transfers between devices: none -> 95.8 us  [swap(): return lax.ppermute(values, 'lev', [(0, 1), (1, 0)])]
    all_to_all x7 -> x0, local copies, waits for them, and re-layouts: 94.1 us -> none  [the longest x3 35.2 us: to_bands(): lax.all_to_all(values, 'wave', split_axis=2, concat_axis=1, tiled=True)]
    all_to_all x1 -> x2, blocking collectives: 187 us -> 106 us  [exchange(): lax.all_to_all(values, 'wave', split_axis=0, concat_axis=0, tiled=True)]
    reshape x5 -> x0, local copies, waits for them, and re-layouts: 76.2 us -> none  [the longest x1 21.1 us: shards(): adjoint_coeffs.astype(jnp.bfloat16)]
  transfers between devices with their start and end apart: 4 -> 15, of which waited for: 3 -> 7; matrix products, arithmetic and copies ran while one was open for 18% -> 1% of each run, Pallas kernels for 0% -> 47%
where the time goes in v1:
time: 657 us; the launch traced here: 647 us
  Pallas kernels  342 us (52%)
  waiting for transfers between devices  136 us (21%)
  blocking collectives  106 us (16%)
  starting transfers between devices  47 us (7%)
  local copies, waits for them, and re-layouts  15.3 us (2%)
    all_to_all x2, blocking collectives, exchange(): lax.all_to_all(values, 'wave', split_axis=0, concat_axis=0, tiled=True)  106 us
    ppermute x9, waiting for transfers between devices, swap(): return lax.ppermute(values, 'lev', [(0, 1), (1, 0)])  95.8 us
    pallas_call x4, Pallas kernels, vertical_adj(): pl.pallas_call(vertical_adj_body, grid_spec=pltpu.PrefetchScalarGridSpec(...  91.4 us
    pallas_call x4, Pallas kernels, vertical_fwd(): pl.pallas_call(vertical_fwd_body, grid_spec=pltpu.PrefetchScalarGridSpec(...  72.6 us
    pallas_call x4, Pallas kernels, grid_stage(): pl.pallas_call(grid_body, grid=(lats,), in_specs=in_specs, out_specs=[pl....  62.1 us
    pallas_call x4, Pallas kernels, legendre_adj(): pl.pallas_call(legendre_adj_body, grid=(slots,), in_specs=[row, row, pl.B...  49 us
    pallas_call x4, Pallas kernels, legendre_fwd(): pl.pallas_call(legendre_fwd_body, grid=(slots,), in_specs=[row, row, col,...  48.7 us
    all_to_all x6, waiting for transfers between devices, exchange(): lax.all_to_all(values, 'wave', split_axis=0, concat_axis=0, tiled=True)  40.3 us
  transfers between devices with their start and end apart: 15, of which 7 were waited for; matrix products, arithmetic and copies ran while one was open for 1% of the time, Pallas kernels for 47%

profile of v1, /device:TPU:13, one launch (start us, length us, event | category | flops | bytes accessed | tf_op | source)
XLA Modules:
  0.0 647.1 jit_solution(8629447216405640019)
XLA Ops:
  0.6 0.0 copy-start
  0.6 1.3 collective-permute-start
  1.9 1.3 dynamic_slice.3.waves
  3.2 18.1 %vertical_fwd.7 = (bf16[16,128,256]{2,1,0:T(8,128)(2,1)}, bf16[16,128,256]{2,1,0:T(8,128)(2,1)}) custom-call(s32[1]{0:T(128)} %bitcast.info, s32[16]{0:T(128)} %dynamic_slice.3.waves, bf16[2,16,128,2,512]{4,3,2,1,0:T(2,128)(2,1)} %xs.7, bf16[2,16,128,2,512]{4,3,2,1,0:T(2,128)(2,1)} %xs.7, bf16[4,4,128,128]{3,2,1,0:T(8,128)(2,1)} %v.7, bf16[4,4,128,128]{3,2,1,0:T(8,128)(2,1)} %v.7), custom_call_target="tpu_custom_call" | custom-call | flops 2147483648 | bytes 4194304 | tf_op jit(solution)/shard_map/vertical_fwd/pallas_call | solution.py:65
  21.4 0.3 collective-permute-start.4
  21.6 3.4 collective-permute-done.lx
  25.0 22.5 %collective-permute-done.4.recv = bf16[16,128,256]{2,1,0:T(8,128)(2,1)S(1)} collective-permute-done((bf16[16,128,256]{2,1,0:T(8,128)(2,1)}, bf16[16,128,256]{2,1,0:T(8,128)(2,1)S(1)}, u32[]{:S(2)}, u32[]{:S(2)}) %collective-permute-start.4) | collective-permute-done | bytes 1048608 | tf_op jit(solution)/shard_map/ppermute | solution.py:310
  47.4 1.0 copy-done.11
  48.4 12.2 %legendre_fwd.7 = bf16[16,16,16,256]{3,2,1,0:T(8,128)(2,1)} custom-call(bf16[16,128,256]{2,1,0:T(8,128)(2,1)} %lo.15, bf16[16,128,256]{2,1,0:T(8,128)(2,1)} %copy-done.2, bf16[16,128,256]{2,1,0:T(8,128)(2,1)} %get-tuple-element.36.own, bf16[16,128,256]{2,1,0:T(8,128)(2,1)} %copy-done.11), custom_call_target="tpu_custom_call" | custom-call | flops 536870912 | bytes 4194304 | tf_op jit(solution)/shard_map/legendre_fwd/pallas_call | solution.py:163
  60.6 7.4 %all-to-all-start.3 = ((bf16[16,16,16,256]{3,2,1,0:T(8,128)(2,1)}), bf16[16,16,16,256]{3,2,1,0:T(8,128)(2,1)S(1)}, u32[]{:S(2)}, u32[]{:S(2)}) async-start(bf16[16,16,16,256]{3,2,1,0:T(8,128)(2,1)} %legendre_fwd.7), calls=%async_computation.3 | async-start | bytes 4194304 | tf_op jit(solution)/shard_map/all_to_all | solution.py:314
  68.0 18.2 %vertical_fwd.6 = (bf16[16,128,256]{2,1,0:T(8,128)(2,1)}, bf16[16,128,256]{2,1,0:T(8,128)(2,1)}) custom-call(s32[1]{0:T(128)} %bitcast.info, s32[16]{0:T(128)} %dynamic_slice.3.waves, bf16[2,16,128,2,512]{4,3,2,1,0:T(2,128)(2,1)} %xs.7, bf16[2,16,128,2,512]{4,3,2,1,0:T(2,128)(2,1)} %xs.7, bf16[4,4,128,128]{3,2,1,0:T(8,128)(2,1)} %v.7, bf16[4,4,128,128]{3,2,1,0:T(8,128)(2,1)} %v.7), custom_call_target="tpu_custom_call" | custom-call | flops 2147483648 | bytes 4194304 | tf_op jit(solution)/shard_map/vertical_fwd/pallas_call | solution.py:65
  86.2 1.2 collective-permute-start.3
  87.4 23.3 %collective-permute-done.3.recv = bf16[16,128,256]{2,1,0:T(8,128)(2,1)S(1)} collective-permute-done((bf16[16,128,256]{2,1,0:T(8,128)(2,1)}, bf16[16,128,256]{2,1,0:T(8,128)(2,1)S(1)}, u32[]{:S(2)}, u32[]{:S(2)}) %collective-permute-start.3) | collective-permute-done | bytes 1048608 | tf_op jit(solution)/shard_map/ppermute | solution.py:310
  110.7 1.0 copy-done.12
  111.7 12.2 %legendre_fwd.6 = bf16[16,16,16,256]{3,2,1,0:T(8,128)(2,1)} custom-call(bf16[16,128,256]{2,1,0:T(8,128)(2,1)} %lo.15, bf16[16,128,256]{2,1,0:T(8,128)(2,1)} %copy-done.2, bf16[16,128,256]{2,1,0:T(8,128)(2,1)} %get-tuple-element.34.own, bf16[16,128,256]{2,1,0:T(8,128)(2,1)} %copy-done.12), custom_call_target="tpu_custom_call" | custom-call | flops 536870912 | bytes 4194304 | tf_op jit(solution)/shard_map/legendre_fwd/pallas_call | solution.py:163
  123.9 0.0 all-to-all-done.3.by_lat
  123.9 1.3 copy-done.7
  125.2 6.9 %all-to-all-start.2 = ((bf16[16,16,16,256]{3,2,1,0:T(8,128)(2,1)}), bf16[16,16,16,256]{3,2,1,0:T(8,128)(2,1)S(1)}, u32[]{:S(2)}, u32[]{:S(2)}) async-start(bf16[16,16,16,256]{3,2,1,0:T(8,128)(2,1)} %legendre_fwd.6), calls=%async_computation.2 | async-start | bytes 4194304 | tf_op jit(solution)/shard_map/all_to_all | solution.py:314
  132.1 18.1 %vertical_fwd.5 = (bf16[16,128,256]{2,1,0:T(8,128)(2,1)}, bf16[16,128,256]{2,1,0:T(8,128)(2,1)}) custom-call(s32[1]{0:T(128)} %bitcast.info, s32[16]{0:T(128)} %dynamic_slice.3.waves, bf16[2,16,128,2,512]{4,3,2,1,0:T(2,128)(2,1)} %xs.7, bf16[2,16,128,2,512]{4,3,2,1,0:T(2,128)(2,1)} %xs.7, bf16[4,4,128,128]{3,2,1,0:T(8,128)(2,1)} %v.7, bf16[4,4,128,128]{3,2,1,0:T(8,128)(2,1)} %v.7), custom_call_target="tpu_custom_call" | custom-call | flops 2147483648 | bytes 4194304 | tf_op jit(solution)/shard_map/vertical_fwd/pallas_call | solution.py:65
  150.2 1.2 collective-permute-start.2
  151.5 23.3 %collective-permute-done.2.recv = bf16[16,128,256]{2,1,0:T(8,128)(2,1)S(1)} collective-permute-done((bf16[16,128,256]{2,1,0:T(8,128)(2,1)}, bf16[16,128,256]{2,1,0:T(8,128)(2,1)S(1)}, u32[]{:S(2)}, u32[]{:S(2)}) %collective-permute-start.2) | collective-permute-done | bytes 1048608 | tf_op jit(solution)/shard_map/ppermute | solution.py:310
  174.8 1.0 copy-done.13
  175.8 12.2 %legendre_fwd.5 = bf16[16,16,16,256]{3,2,1,0:T(8,128)(2,1)} custom-call(bf16[16,128,256]{2,1,0:T(8,128)(2,1)} %lo.15, bf16[16,128,256]{2,1,0:T(8,128)(2,1)} %copy-done.2, bf16[16,128,256]{2,1,0:T(8,128)(2,1)} %get-tuple-element.32.own, bf16[16,128,256]{2,1,0:T(8,128)(2,1)} %copy-done.13), custom_call_target="tpu_custom_call" | custom-call | flops 536870912 | bytes 4194304 | tf_op jit(solution)/shard_map/legendre_fwd/pallas_call | solution.py:163
  188.0 1.3 copy-done.3
  189.3 6.9 %all-to-all-start.1 = ((bf16[16,16,16,256]{3,2,1,0:T(8,128)(2,1)}), bf16[16,16,16,256]{3,2,1,0:T(8,128)(2,1)}, u32[]{:S(2)}, u32[]{:S(2)}) async-start(bf16[16,16,16,256]{3,2,1,0:T(8,128)(2,1)} %legendre_fwd.5), calls=%async_computation.1 | async-start | bytes 4194304 | tf_op jit(solution)/shard_map/all_to_all | solution.py:314
  196.1 18.2 %vertical_fwd.4 = (bf16[16,128,256]{2,1,0:T(8,128)(2,1)}, bf16[16,128,256]{2,1,0:T(8,128)(2,1)}) custom-call(s32[1]{0:T(128)} %bitcast.info, s32[16]{0:T(128)} %dynamic_slice.3.waves, bf16[2,16,128,2,512]{4,3,2,1,0:T(2,128)(2,1)} %xs.7, bf16[2,16,128,2,512]{4,3,2,1,0:T(2,128)(2,1)} %xs.7, bf16[4,4,128,128]{3,2,1,0:T(8,128)(2,1)} %v.7, bf16[4,4,128,128]{3,2,1,0:T(8,128)(2,1)} %v.7), custom_call_target="tpu_custom_call" | custom-call | flops 2147483648 | bytes 4194304 | tf_op jit(solution)/shard_map/vertical_fwd/pallas_call | solution.py:65
  214.3 1.2 collective-permute-start.1
  215.5 23.3 %collective-permute-done.1.recv = bf16[16,128,256]{2,1,0:T(8,128)(2,1)S(1)} collective-permute-done((bf16[16,128,256]{2,1,0:T(8,128)(2,1)}, bf16[16,128,256]{2,1,0:T(8,128)(2,1)S(1)}, u32[]{:S(2)}, u32[]{:S(2)}) %collective-permute-start.1) | collective-permute-done | bytes 1048608 | tf_op jit(solution)/shard_map/ppermute | solution.py:310
  238.8 1.0 copy-done.14
  239.8 12.2 %legendre_fwd.4 = bf16[16,16,16,256]{3,2,1,0:T(8,128)(2,1)} custom-call(bf16[16,128,256]{2,1,0:T(8,128)(2,1)} %lo.15, bf16[16,128,256]{2,1,0:T(8,128)(2,1)} %copy-done.2, bf16[16,128,256]{2,1,0:T(8,128)(2,1)} %get-tuple-element.28.own, bf16[16,128,256]{2,1,0:T(8,128)(2,1)} %copy-done.14), custom_call_target="tpu_custom_call" | custom-call | flops 536870912 | bytes 4194304 | tf_op jit(solution)/shard_map/legendre_fwd/pallas_call | solution.py:163
  252.0 0.0 all-to-all-done.1.by_lat
  252.0 7.0 %all-to-all-start = ((bf16[16,16,16,256]{3,2,1,0:T(8,128)(2,1)}), bf16[16,16,16,256]{3,2,1,0:T(8,128)(2,1)S(1)}, u32[]{:S(2)}, u32[]{:S(2)}) async-start(bf16[16,16,16,256]{3,2,1,0:T(8,128)(2,1)} %legendre_fwd.4), calls=%async_computation | async-start | bytes 4194304 | tf_op jit(solution)/shard_map/all_to_all | solution.py:314
  259.0 0.8 copy.16.waves
  259.8 0.2 convolution_bitcast_fusion
  260.0 2.0 copy.20.scale
  262.0 18.1 %fourier_tables.1 = (bf16[16,256,512]{2,1,0:T(8,128)(2,1)}, bf16[16,256,512]{2,1,0:T(8,128)(2,1)}) custom-call(s32[16]{0:T(128)} %points.1, f32[256,1]{1,0:T(8,128)} %copy.16.waves), custom_call_target="tpu_custom_call" | custom-call | flops 83886080 | bytes 8388608 | tf_op jit(solution)/shard_map/fourier_tables/pallas_call | solution.py:243
  280.1 15.5 %grid_stage.4 = (bf16[2,16,256,512]{3,2,1,0:T(8,128)(2,1)}, bf16[16,16,16,256]{3,2,1,0:T(8,128)(2,1)}) custom-call(bf16[16,16,16,256]{3,2,1,0:T(8,128)(2,1)} %copy-done.7, bf16[16,256,512]{2,1,0:T(8,128)(2,1)} %get-tuple-element.30.cosine, bf16[16,256,512]{2,1,0:T(8,128)(2,1)} %get-tuple-element.31.sine, f32[16,256,1]{2,1,0:T(8,128)} %copy.20.scale, ...), custom_call_target="tpu_custom_call" | custom-call | flops 2147483648 | bytes 12582912 | tf_op jit(solution)/shard_map/grid_stage/pallas_call | solution.py:293
  295.6 15.5 %grid_stage.5 = (bf16[2,16,256,512]{3,2,1,0:T(8,128)(2,1)}, bf16[16,16,16,256]{3,2,1,0:T(8,128)(2,1)}) custom-call(bf16[16,16,16,256]{3,2,1,0:T(8,128)(2,1)} %copy-done.3, bf16[16,256,512]{2,1,0:T(8,128)(2,1)} %get-tuple-element.30.cosine, bf16[16,256,512]{2,1,0:T(8,128)(2,1)} %get-tuple-element.31.sine, ...), custom_call_target="tpu_custom_call", output_to_operand_aliasing={{0}: (5, {})} | custom-call | flops 2147483648 | bytes 12582912 | tf_op jit(solution)/shard_map/grid_stage/pallas_call | solution.py:293
  311.2 15.5 %grid_stage.6 = (bf16[2,16,256,512]{3,2,1,0:T(8,128)(2,1)}, bf16[16,16,16,256]{3,2,1,0:T(8,128)(2,1)}) custom-call(bf16[16,16,16,256]{3,2,1,0:T(8,128)(2,1)} %all-to-all-done.1.by_lat, bf16[16,256,512]{2,1,0:T(8,128)(2,1)} %get-tuple-element.30.cosine, bf16[16,256,512]{2,1,0:T(8,128)(2,1)} %get-tuple-element.31.sine, ...), custom_call_target="tpu_custom_call", output_to_operand_aliasing={{0}: (5, {})} | custom-call | flops 2147483648 | bytes 12582912 | tf_op jit(solution)/shard_map/grid_stage/pallas_call | solution.py:293
  326.7 53.7 %all_to_all.40.band = bf16[16,16,16,256]{3,2,1,0:T(8,128)(2,1)} all-to-all(bf16[16,16,16,256]{3,2,1,0:T(8,128)(2,1)} %get-tuple-element.45), channel_id=1, replica_groups=mesh['wave'=16,'lev'=2] {'wave'}, dimensions={0} | all-to-all | bytes 4194304 | tf_op jit(solution)/shard_map/all_to_all | solution.py:314
  380.4 52.2 %all_to_all.41.band = bf16[16,16,16,256]{3,2,1,0:T(8,128)(2,1)} all-to-all(bf16[16,16,16,256]{3,2,1,0:T(8,128)(2,1)S(1)} %copy-done.8), channel_id=1, replica_groups=mesh['wave'=16,'lev'=2] {'wave'}, dimensions={0} | all-to-all | bytes 4194304 | tf_op jit(solution)/shard_map/all_to_all | solution.py:314
  432.6 5.0 all-to-all-start.7
  437.6 15.5 %grid_stage.7 = (bf16[2,16,256,512]{3,2,1,0:T(8,128)(2,1)}, bf16[16,16,16,256]{3,2,1,0:T(8,128)(2,1)}) custom-call(bf16[16,16,16,256]{3,2,1,0:T(8,128)(2,1)} %copy-done.4, bf16[16,256,512]{2,1,0:T(8,128)(2,1)} %get-tuple-element.30.cosine, bf16[16,256,512]{2,1,0:T(8,128)(2,1)} %get-tuple-element.31.sine, ...), custom_call_target="tpu_custom_call", output_to_operand_aliasing={{0}: (5, {})} | custom-call | flops 2147483648 | bytes 12582912 | tf_op jit(solution)/shard_map/grid_stage/pallas_call | solution.py:293
  453.1 31.9 %all-to-all-done.7.band = bf16[16,16,16,256]{3,2,1,0:T(8,128)(2,1)S(1)} async-done(((bf16[16,16,16,256]{3,2,1,0:T(8,128)(2,1)}), bf16[16,16,16,256]{3,2,1,0:T(8,128)(2,1)S(1)}, u32[]{:S(2)}, u32[]{:S(2)}) %all-to-all-start.7) | async-done | bytes 2097184 | tf_op jit(solution)/shard_map/all_to_all | solution.py:314
  485.0 1.3 copy-done.6
  486.3 4.8 all-to-all-start.4
  491.1 12.3 %legendre_adj.7 = (bf16[16,128,256]{2,1,0:T(8,128)(2,1)}, bf16[16,128,256]{2,1,0:T(8,128)(2,1)}) custom-call(bf16[16,128,256]{2,1,0:T(8,128)(2,1)} %lo.15, bf16[16,128,256]{2,1,0:T(8,128)(2,1)} %copy-done.2, bf16[16,16,16,256]{3,2,1,0:T(8,128)(2,1)} %copy-done.6), custom_call_target="tpu_custom_call" | custom-call | flops 536870912 | bytes 4194304 | tf_op jit(solution)/shard_map/legendre_adj/pallas_call | solution.py:200
  503.4 1.2 collective-permute-start.8
  504.6 12.2 %legendre_adj.6 = (bf16[16,128,256]{2,1,0:T(8,128)(2,1)}, bf16[16,128,256]{2,1,0:T(8,128)(2,1)}) custom-call(bf16[16,128,256]{2,1,0:T(8,128)(2,1)} %lo.15, bf16[16,128,256]{2,1,0:T(8,128)(2,1)} %copy-done.2, bf16[16,16,16,256]{3,2,1,0:T(8,128)(2,1)} %all_to_all.41.band), custom_call_target="tpu_custom_call" | custom-call | flops 536870912 | bytes 4194304 | tf_op jit(solution)/shard_map/legendre_adj/pallas_call | solution.py:200
  516.8 0.3 collective-permute-start.7
  517.1 12.2 %legendre_adj.5 = (bf16[16,128,256]{2,1,0:T(8,128)(2,1)}, bf16[16,128,256]{2,1,0:T(8,128)(2,1)}) custom-call(bf16[16,128,256]{2,1,0:T(8,128)(2,1)} %lo.15, bf16[16,128,256]{2,1,0:T(8,128)(2,1)} %copy-done.2, bf16[16,16,16,256]{3,2,1,0:T(8,128)(2,1)} %all_to_all.40.band), custom_call_target="tpu_custom_call" | custom-call | flops 536870912 | bytes 4194304 | tf_op jit(solution)/shard_map/legendre_adj/pallas_call | solution.py:200
  529.3 1.2 collective-permute-start.6
  530.5 8.4 %all-to-all-done.4.band = bf16[16,16,16,256]{3,2,1,0:T(8,128)(2,1)S(1)} async-done(((bf16[16,16,16,256]{3,2,1,0:T(8,128)(2,1)}), bf16[16,16,16,256]{3,2,1,0:T(8,128)(2,1)S(1)}, u32[]{:S(2)}, u32[]{:S(2)}) %all-to-all-start.4) | async-done | bytes 2097184 | tf_op jit(solution)/shard_map/all_to_all | solution.py:314
  538.9 1.3 copy-done.5
  540.3 12.2 %legendre_adj.4 = (bf16[16,128,256]{2,1,0:T(8,128)(2,1)}, bf16[16,128,256]{2,1,0:T(8,128)(2,1)}) custom-call(bf16[16,128,256]{2,1,0:T(8,128)(2,1)} %lo.15, bf16[16,128,256]{2,1,0:T(8,128)(2,1)} %copy-done.2, bf16[16,16,16,256]{3,2,1,0:T(8,128)(2,1)} %copy-done.5), custom_call_target="tpu_custom_call" | custom-call | flops 536870912 | bytes 4194304 | tf_op jit(solution)/shard_map/legendre_adj/pallas_call | solution.py:200
  552.5 1.2 collective-permute-start.5
  553.7 0.0 collective-permute-done.8.other
  553.7 22.8 %vertical_adj.4.rest_0_ = bf16[2,16,128,2,512]{4,3,2,1,0:T(2,128)(2,1)} custom-call(s32[1]{0:T(128)} %bitcast.info, s32[16]{0:T(128)} %dynamic_slice.3.waves, bf16[16,128,256]{2,1,0:T(8,128)(2,1)} %get-tuple-element.52.own, bf16[16,128,256]{2,1,0:T(8,128)(2,1)} %collective-permute-done.8.other, bf16[4,4,128,128]{3,2,1,0:T(8,128)(2,1)} %v.7), custom_call_target="tpu_custom_call" | custom-call | flops 2147483648 | bytes 4194304 | tf_op jit(solution)/shard_map/vertical_adj/pallas_call | solution.py:124
  576.5 0.0 collective-permute-done.7.other
  576.5 22.8 %vertical_adj.5.rest_0_ = bf16[2,16,128,2,512]{4,3,2,1,0:T(2,128)(2,1)} custom-call(s32[1]{0:T(128)} %bitcast.info, s32[16]{0:T(128)} %dynamic_slice.3.waves, bf16[16,128,256]{2,1,0:T(8,128)(2,1)} %get-tuple-element.49.own, bf16[16,128,256]{2,1,0:T(8,128)(2,1)} %collective-permute-done.7.other, ...), custom_call_target="tpu_custom_call", output_to_operand_aliasing={{}: (5, {})} | custom-call | flops 2147483648 | bytes 4194304 | tf_op jit(solution)/shard_map/vertical_adj/pallas_call | solution.py:124
  599.4 1.0 copy-done.9
  600.3 22.8 %vertical_adj.6.rest_0_ = bf16[2,16,128,2,512]{4,3,2,1,0:T(2,128)(2,1)} custom-call(s32[1]{0:T(128)} %bitcast.info, s32[16]{0:T(128)} %dynamic_slice.3.waves, bf16[16,128,256]{2,1,0:T(8,128)(2,1)} %get-tuple-element.46.own, bf16[16,128,256]{2,1,0:T(8,128)(2,1)} %copy-done.9, bf16[4,4,128,128]{3,2,1,0:T(8,128)(2,1)} %v.7, ...), custom_call_target="tpu_custom_call", output_to_operand_aliasing={{}: (5, {})} | custom-call | flops 2147483648 | bytes 4194304 | tf_op jit(solution)/shard_map/vertical_adj/pallas_call | solution.py:124
  623.2 1.0 copy-done.10
  624.2 23.0 %vertical_adj.7 = bf16[2,16,128,2,512]{4,3,2,1,0:T(2,128)(2,1)} custom-call(s32[1]{0:T(128)} %bitcast.info, s32[16]{0:T(128)} %dynamic_slice.3.waves, bf16[16,128,256]{2,1,0:T(8,128)(2,1)} %get-tuple-element.43.own, bf16[16,128,256]{2,1,0:T(8,128)(2,1)} %copy-done.10, bf16[4,4,128,128]{3,2,1,0:T(8,128)(2,1)} %v.7, ...), custom_call_target="tpu_custom_call", output_to_operand_aliasing={{}: (5, {})} | custom-call | flops 2147483648 | bytes 4194304 | tf_op jit(solution)/shard_map/vertical_adj/pallas_call | solution.py:124
  (28 shorter events, 0.1 us)
Async XLA Ops:
  0.6 259.2 %copy-start = (f32[8,256]{1,0:T(8,128)S(1)}, f32[8,256]{1,0:T(8,128)}, u32[]{:S(2)}) copy-start(f32[8,256]{1,0:T(8,128)} %param.14) | copy-start | bytes 24580
  0.6 24.3 %collective-permute-start = (bf16[16,128,256]{2,1,0:T(8,128)(2,1)}, bf16[16,128,256]{2,1,0:T(8,128)(2,1)S(1)}, u32[]{:S(2)}, u32[]{:S(2)}) collective-permute-start(bf16[16,128,256]{2,1,0:T(8,128)(2,1)} %lo.15), channel_id=1, source_target_pairs={{0,1},{1,0},{2,3},{3,2},{4,5},{5,4},{6,7},{7,6},{8,9},{9,8},{10,11... | collective-permute-start | bytes 3145736 | tf_op jit(solution)/shard_map/ppermute | solution.py:310
  21.4 26.1 %collective-permute-start.4 = (bf16[16,128,256]{2,1,0:T(8,128)(2,1)}, bf16[16,128,256]{2,1,0:T(8,128)(2,1)S(1)}, u32[]{:S(2)}, u32[]{:S(2)}) collective-permute-start(bf16[16,128,256]{2,1,0:T(8,128)(2,1)} %get-tuple-element.37), channel_id=1, source_target_pairs={{0,1},{1,0},{2,3},{3,2},{4,5},{5,4},{6,7},{7,6},{8,9},{9,8},{10,11... | collective-permute-start | bytes 3145736 | tf_op jit(solution)/shard_map/ppermute | solution.py:310
  25.0 22.5 %copy-start.2 = (bf16[16,128,256]{2,1,0:T(8,128)(2,1)}, bf16[16,128,256]{2,1,0:T(8,128)(2,1)S(1)}, u32[]{:S(2)}) copy-start(bf16[16,128,256]{2,1,0:T(8,128)(2,1)S(1)} %collective-permute-done.lx) | copy-start | bytes 3145732
  47.4 1.0 copy-start.11
  60.6 63.3 %all-to-all-start.3 = ((bf16[16,16,16,256]{3,2,1,0:T(8,128)(2,1)}), bf16[16,16,16,256]{3,2,1,0:T(8,128)(2,1)S(1)}, u32[]{:S(2)}, u32[]{:S(2)}) async-start(bf16[16,16,16,256]{3,2,1,0:T(8,128)(2,1)} %legendre_fwd.7), calls=%async_computation.3 | async-start | bytes 4194304 | tf_op jit(solution)/shard_map/all_to_all | solution.py:314
  86.2 24.5 %collective-permute-start.3 = (bf16[16,128,256]{2,1,0:T(8,128)(2,1)}, bf16[16,128,256]{2,1,0:T(8,128)(2,1)S(1)}, u32[]{:S(2)}, u32[]{:S(2)}) collective-permute-start(bf16[16,128,256]{2,1,0:T(8,128)(2,1)} %get-tuple-element.35), channel_id=1, source_target_pairs={{0,1},{1,0},{2,3},{3,2},{4,5},{5,4},{6,7},{7,6},{8,9},{9,8},{10,11... | collective-permute-start | bytes 3145736 | tf_op jit(solution)/shard_map/ppermute | solution.py:310
  110.7 1.0 copy-start.12
  123.9 1.4 copy-start.7
  125.2 62.7 %all-to-all-start.2 = ((bf16[16,16,16,256]{3,2,1,0:T(8,128)(2,1)}), bf16[16,16,16,256]{3,2,1,0:T(8,128)(2,1)S(1)}, u32[]{:S(2)}, u32[]{:S(2)}) async-start(bf16[16,16,16,256]{3,2,1,0:T(8,128)(2,1)} %legendre_fwd.6), calls=%async_computation.2 | async-start | bytes 4194304 | tf_op jit(solution)/shard_map/all_to_all | solution.py:314
  150.2 24.5 %collective-permute-start.2 = (bf16[16,128,256]{2,1,0:T(8,128)(2,1)}, bf16[16,128,256]{2,1,0:T(8,128)(2,1)S(1)}, u32[]{:S(2)}, u32[]{:S(2)}) collective-permute-start(bf16[16,128,256]{2,1,0:T(8,128)(2,1)} %get-tuple-element.33), channel_id=1, source_target_pairs={{0,1},{1,0},{2,3},{3,2},{4,5},{5,4},{6,7},{7,6},{8,9},{9,8},{10,11... | collective-permute-start | bytes 3145736 | tf_op jit(solution)/shard_map/ppermute | solution.py:310
  174.8 1.0 copy-start.13
  188.0 1.3 copy-start.3
  189.3 62.7 %all-to-all-start.1 = ((bf16[16,16,16,256]{3,2,1,0:T(8,128)(2,1)}), bf16[16,16,16,256]{3,2,1,0:T(8,128)(2,1)}, u32[]{:S(2)}, u32[]{:S(2)}) async-start(bf16[16,16,16,256]{3,2,1,0:T(8,128)(2,1)} %legendre_fwd.5), calls=%async_computation.1 | async-start | bytes 4194304 | tf_op jit(solution)/shard_map/all_to_all | solution.py:314
  214.3 24.5 %collective-permute-start.1 = (bf16[16,128,256]{2,1,0:T(8,128)(2,1)}, bf16[16,128,256]{2,1,0:T(8,128)(2,1)S(1)}, u32[]{:S(2)}, u32[]{:S(2)}) collective-permute-start(bf16[16,128,256]{2,1,0:T(8,128)(2,1)} %get-tuple-element.29), channel_id=1, source_target_pairs={{0,1},{1,0},{2,3},{3,2},{4,5},{5,4},{6,7},{7,6},{8,9},{9,8},{10,11... | collective-permute-start | bytes 3145736 | tf_op jit(solution)/shard_map/ppermute | solution.py:310
  238.8 1.0 copy-start.14
  252.0 7.0 %copy-start.15 = (s32[256]{0:T(256)S(1)}, s32[256]{0:T(256)}, u32[]{:S(2)}) copy-start(s32[256]{0:T(256)} %param.9) | copy-start | bytes 3076
  252.0 7.8 %copy-start.16 = (s32[16]{0:T(128)S(1)}, s32[16]{0:T(128)}, u32[]{:S(2)}) copy-start(s32[16]{0:T(128)} %param.13) | copy-start | bytes 196
  252.0 74.7 %all-to-all-start = ((bf16[16,16,16,256]{3,2,1,0:T(8,128)(2,1)}), bf16[16,16,16,256]{3,2,1,0:T(8,128)(2,1)S(1)}, u32[]{:S(2)}, u32[]{:S(2)}) async-start(bf16[16,16,16,256]{3,2,1,0:T(8,128)(2,1)} %legendre_fwd.4), calls=%async_computation | async-start | bytes 4194304 | tf_op jit(solution)/shard_map/all_to_all | solution.py:314
  326.7 53.7 %copy-start.4 = (bf16[16,16,16,256]{3,2,1,0:T(8,128)(2,1)}, bf16[16,16,16,256]{3,2,1,0:T(8,128)(2,1)S(1)}, u32[]{:S(2)}) copy-start(bf16[16,16,16,256]{3,2,1,0:T(8,128)(2,1)S(1)} %all-to-all-done.by_lat) | copy-start | bytes 6291460
  326.7 53.7 %copy-start.8 = (bf16[16,16,16,256]{3,2,1,0:T(8,128)(2,1)S(1)}, bf16[16,16,16,256]{3,2,1,0:T(8,128)(2,1)}, u32[]{:S(2)}) copy-start(bf16[16,16,16,256]{3,2,1,0:T(8,128)(2,1)} %get-tuple-element.48) | copy-start | bytes 6291460
  432.6 52.4 %all-to-all-start.7 = ((bf16[16,16,16,256]{3,2,1,0:T(8,128)(2,1)}), bf16[16,16,16,256]{3,2,1,0:T(8,128)(2,1)S(1)}, u32[]{:S(2)}, u32[]{:S(2)}) async-start(bf16[16,16,16,256]{3,2,1,0:T(8,128)(2,1)} %get-tuple-element.51), calls=%async_computation.7 | async-start | bytes 4194304 | tf_op jit(solution)/shard_map/all_to_all | solution.py:314
  485.0 1.3 copy-start.6
  486.3 52.6 %all-to-all-start.4 = ((bf16[16,16,16,256]{3,2,1,0:T(8,128)(2,1)}), bf16[16,16,16,256]{3,2,1,0:T(8,128)(2,1)S(1)}, u32[]{:S(2)}, u32[]{:S(2)}) async-start(bf16[16,16,16,256]{3,2,1,0:T(8,128)(2,1)} %get-tuple-element.42), calls=%async_computation.4 | async-start | bytes 4194304 | tf_op jit(solution)/shard_map/all_to_all | solution.py:314
  503.4 50.3 %collective-permute-start.8 = (bf16[16,128,256]{2,1,0:T(8,128)(2,1)}, bf16[16,128,256]{2,1,0:T(8,128)(2,1)}, u32[]{:S(2)}, u32[]{:S(2)}) collective-permute-start(bf16[16,128,256]{2,1,0:T(8,128)(2,1)} %get-tuple-element.53), channel_id=1, source_target_pairs={{0,1},{1,0},{2,3},{3,2},{4,5},{5,4},{6,7},{7,6},{8,9},{9,8},{10,11... | collective-permute-start | bytes 3145736 | tf_op jit(solution)/shard_map/ppermute | solution.py:310
  516.8 59.7 %collective-permute-start.7 = (bf16[16,128,256]{2,1,0:T(8,128)(2,1)}, bf16[16,128,256]{2,1,0:T(8,128)(2,1)}, u32[]{:S(2)}, u32[]{:S(2)}) collective-permute-start(bf16[16,128,256]{2,1,0:T(8,128)(2,1)} %get-tuple-element.50), channel_id=1, source_target_pairs={{0,1},{1,0},{2,3},{3,2},{4,5},{5,4},{6,7},{7,6},{8,9},{9,8},{10,11... | collective-permute-start | bytes 3145736 | tf_op jit(solution)/shard_map/ppermute | solution.py:310
  529.3 70.1 %collective-permute-start.6 = (bf16[16,128,256]{2,1,0:T(8,128)(2,1)}, bf16[16,128,256]{2,1,0:T(8,128)(2,1)S(1)}, u32[]{:S(2)}, u32[]{:S(2)}) collective-permute-start(bf16[16,128,256]{2,1,0:T(8,128)(2,1)} %get-tuple-element.47), channel_id=1, source_target_pairs={{0,1},{1,0},{2,3},{3,2},{4,5},{5,4},{6,7},{7,6},{8,9},{9,8},{10,11... | collective-permute-start | bytes 3145736 | tf_op jit(solution)/shard_map/ppermute | solution.py:310
  538.9 1.3 copy-start.5
  552.5 70.7 %collective-permute-start.5 = (bf16[16,128,256]{2,1,0:T(8,128)(2,1)}, bf16[16,128,256]{2,1,0:T(8,128)(2,1)S(1)}, u32[]{:S(2)}, u32[]{:S(2)}) collective-permute-start(bf16[16,128,256]{2,1,0:T(8,128)(2,1)} %get-tuple-element.44), channel_id=1, source_target_pairs={{0,1},{1,0},{2,3},{3,2},{4,5},{5,4},{6,7},{7,6},{8,9},{9,8},{10,11... | collective-permute-start | bytes 3145736 | tf_op jit(solution)/shard_map/ppermute | solution.py:310
  599.4 1.0 copy-start.9
  623.2 1.0 copy-start.10
  624.2 23.0 %copy-start.1 = (f32[8,256]{1,0:T(8,128)S(1)}, f32[8,256]{1,0:T(8,128)}, u32[]{:S(2)}) copy-start(f32[8,256]{1,0:T(8,128)} %param.14) | copy-start | bytes 24580

commit v2 on v1

--- a/solution.py
+++ b/solution.py
@@ -8,12 +8,14 @@
 from jax.experimental.pallas import tpu as pltpu
 from jax.sharding import PartitionSpec as P
 
+
 WAVES = 256
 LONGITUDES = 512
 LEVELS = 128
 VARIABLES = 4
 COV_BANDS = 4
 LANES = 128
+STEP = 4
 
 BF16 = jnp.bfloat16
 F32 = jnp.float32
@@ -31,181 +33,203 @@
     return lax.dot_general(a, b, (contract, ((), ())), preferred_element_type=F32)
 
 
-def band_masked(rows, first_total):
-    row_total = first_total + lax.broadcasted_iota(jnp.int32, rows.shape, 0) // 2
+def band_masks(count, first_total):
+    row_total = first_total + (lax.broadcasted_iota(jnp.int32, (count, LEVELS), 0) >> 1)
     width = WAVES // COV_BANDS
-    parts = []
+    masks = []
     for band in range(COV_BANDS):
         inside = (row_total >= band * width) & (row_total < (band + 1) * width)
-        parts.append(jnp.where(inside, rows, jnp.zeros_like(rows)))
-    return jnp.concatenate(parts, axis=1)
-
-
-def vertical_fwd_body(info, waves, xo, xs, vo, vs, own, send, scratch):
-    rows_dev = own.shape[1]
-    first_total = waves[pl.program_id(0)] + info[0] * rows_dev
-    for x, v, out in ((xo, vo, own), (xs, vs, send)):
-        rows = x[0, 0].reshape(2 * rows_dev, LEVELS)
-        matrix = jnp.concatenate([v[band, 0] for band in range(COV_BANDS)], axis=1)
-        scratch[...] = dot(band_masked(rows, first_total), matrix, ((1,), (1,)))
+        masks.append(jnp.where(inside, 1.0, 0.0).astype(BF16))
+    return masks
+
+
+def band_rows_of(rows, first_total):
+    return jnp.concatenate([rows * mask for mask in band_masks(rows.shape[0], first_total)], axis=1)
+
+
+def vertical_fwd_body(first_slot, info, waves, x, v, out, scratch):
+    step, rows_dev = out.shape[:2]
+    matrix = jnp.concatenate([v[band, 0] for band in range(COV_BANDS)], axis=1)
+
+    @pl.loop(0, step)
+    def _(i):
+        slot = first_slot + pl.program_id(0) * step + i
+        first_total = waves[slot] + info[0] * rows_dev
+        rows = x[0, i].reshape(2 * rows_dev, LEVELS)
+        scratch[...] = dot(band_rows_of(rows, first_total), matrix, ((1,), (1,)))
         for part in range(2):
-            out[0, :, part * LEVELS : (part + 1) * LEVELS] = scratch[
+            out[i, :, part * LEVELS : (part + 1) * LEVELS] = scratch[
                 pl.ds(part, rows_dev, stride=2), :
             ].astype(BF16)
 
 
-def vertical_fwd(control, vertical, info, waves, member, sub, subs):
-    _, slots, rows_dev, _, _ = control.shape
-    block = (1, 1, rows_dev, 2, LEVELS)
-    vblock = (COV_BANDS, 1, LEVELS, LEVELS)
-    oblock = (1, rows_dev, 2 * LEVELS)
-    mine = lambda info: info[0] * subs + sub
-    other = lambda info: (1 - info[0]) * subs + sub
-    shape = jax.ShapeDtypeStruct((slots, rows_dev, 2 * LEVELS), BF16)
+def column_of(info, sub, subs, other):
+    lev = (1 - info[0]) if other else info[0]
+    return lev * subs + sub
+
+
+def vertical_fwd(control, vertical, info, waves, where, first_slot, slots):
+    member, sub, subs, other = where
+    rows_dev = control.shape[2]
+    step = STEP if slots % STEP == 0 else 1
+    first = first_slot // step
+    column = lambda info: column_of(info, sub, subs, other)
     return pl.pallas_call(
-        vertical_fwd_body,
+        functools.partial(vertical_fwd_body, first_slot),
         grid_spec=pltpu.PrefetchScalarGridSpec(
             num_scalar_prefetch=2,
-            grid=(slots,),
+            grid=(slots // step,),
             in_specs=[
-                pl.BlockSpec(block, lambda s, info, w: (member, s, 0, 0, mine(info))),
-                pl.BlockSpec(block, lambda s, info, w: (member, s, 0, 0, other(info))),
-                pl.BlockSpec(vblock, lambda s, info, w: (0, mine(info), 0, 0)),
-                pl.BlockSpec(vblock, lambda s, info, w: (0, other(info), 0, 0)),
+                pl.BlockSpec(
+                    (1, step, rows_dev, 2, LEVELS), lambda s, info, w: (member, first + s, 0, 0, column(info))
+                ),
+                pl.BlockSpec((COV_BANDS, 1, LEVELS, LEVELS), lambda s, info, w: (0, column(info), 0, 0)),
             ],
-            out_specs=[
-                pl.BlockSpec(oblock, lambda s, info, w: (s, 0, 0)),
-                pl.BlockSpec(oblock, lambda s, info, w: (s, 0, 0)),
-            ],
+            out_specs=pl.BlockSpec((step, rows_dev, 2 * LEVELS), lambda s, info, w: (s, 0, 0)),
             scratch_shapes=[pltpu.VMEM((2 * rows_dev, LEVELS), F32)],
         ),
-        out_shape=[shape, shape],
+        out_shape=jax.ShapeDtypeStruct((slots, rows_dev, 2 * LEVELS), BF16),
         compiler_params=params("arbitrary"),
-        cost_estimate=cost(16 * slots * rows_dev * COV_BANDS * LEVELS * LEVELS, 8 * slots * rows_dev * 256),
+        cost_estimate=cost(64 * slots * rows_dev * COV_BANDS * LEVELS * LEVELS, 8 * slots * rows_dev * 256),
         name="vertical_fwd",
-    )(info, waves, control, control, vertical, vertical)
-
-
-def vertical_adj_body(info, waves, own, other, v, *rest):
+    )(info, waves, control, vertical)
+
+
+def vertical_adj_body(first_slot, info, waves, block, v, *rest):
     out, scratch = rest[-2:]
-    rows_dev = own.shape[1]
-    first_total = waves[pl.program_id(0)] + info[0] * rows_dev
-
-    def run(block):
+    step, rows_dev = block.shape[:2]
+    matrix = v[:, 0].reshape(COV_BANDS * LEVELS, LEVELS)
+
+    @pl.loop(0, step)
+    def _(i):
+        slot = first_slot + pl.program_id(0) * step + i
+        first_total = waves[slot] + info[0] * rows_dev
         for part in range(2):
             scratch[pl.ds(part, rows_dev, stride=2), :] = block[
-                0, :, part * LEVELS : (part + 1) * LEVELS
+                i, :, part * LEVELS : (part + 1) * LEVELS
             ].astype(F32)
         rows = scratch[...].astype(BF16)
-        matrix = v[:, 0].reshape(COV_BANDS * LEVELS, LEVELS)
-        total = dot(band_masked(rows, first_total), matrix, ((1,), (0,)))
-        out[0, 0] = total.astype(BF16).reshape(rows_dev, 2, LEVELS)
-
-    pl.when(pl.program_id(1) == 0)(lambda: run(own))
-    pl.when(pl.program_id(1) == 1)(lambda: run(other))
-
-
-def vertical_adj(own, other, vertical, info, waves, member, sub, subs, shape, into):
-    _, slots, rows_dev, _, _ = shape
-    block = (1, 1, rows_dev, 2, LEVELS)
-    iblock = (1, rows_dev, 2 * LEVELS)
-    column = lambda r, info: (info[0] + r - 2 * info[0] * r) * subs + sub
+        total = dot(band_rows_of(rows, first_total), matrix, ((1,), (0,)))
+        out[0, i] = total.astype(BF16).reshape(rows_dev, 2, LEVELS)
+
+
+def vertical_adj(block, vertical, info, waves, where, first_slot, shape, into):
+    member, sub, subs, other = where
+    slots, rows_dev, width = block.shape
+    step = STEP if slots % STEP == 0 else 1
+    first = first_slot // step
+    column = lambda info: column_of(info, sub, subs, other)
     in_specs = [
-        pl.BlockSpec(iblock, lambda s, r, info, w: (s, 0, 0)),
-        pl.BlockSpec(iblock, lambda s, r, info, w: (s, 0, 0)),
-        pl.BlockSpec((COV_BANDS, 1, LEVELS, LEVELS), lambda s, r, info, w: (0, column(r, info), 0, 0)),
+        pl.BlockSpec((step, rows_dev, width), lambda s, info, w: (s, 0, 0)),
+        pl.BlockSpec((COV_BANDS, 1, LEVELS, LEVELS), lambda s, info, w: (0, column(info), 0, 0)),
     ]
-    operands = [info, waves, own, other, vertical]
+    operands = [info, waves, block, vertical]
     aliases = {}
     if into is not None:
         in_specs.append(pl.BlockSpec(memory_space=pl.ANY))
         operands.append(into)
-        aliases = {5: 0}
+        aliases = {4: 0}
     return pl.pallas_call(
-        vertical_adj_body,
+        functools.partial(vertical_adj_body, first_slot),
         grid_spec=pltpu.PrefetchScalarGridSpec(
             num_scalar_prefetch=2,
-            grid=(slots, 2),
+            grid=(slots // step,),
             in_specs=in_specs,
-            out_specs=pl.BlockSpec(block, lambda s, r, info, w: (member, s, 0, 0, column(r, info))),
+            out_specs=pl.BlockSpec(
+                (1, step, rows_dev, 2, LEVELS), lambda s, info, w: (member, first + s, 0, 0, column(info))
+            ),
             scratch_shapes=[pltpu.VMEM((2 * rows_dev, LEVELS), F32)],
         ),
         out_shape=jax.ShapeDtypeStruct(shape, BF16),
         input_output_aliases=aliases,
-        compiler_params=params("arbitrary", "arbitrary"),
-        cost_estimate=cost(16 * slots * rows_dev * COV_BANDS * LEVELS * LEVELS, 8 * slots * rows_dev * 256),
+        compiler_params=params("arbitrary"),
+        cost_estimate=cost(64 * slots * rows_dev * COV_BANDS * LEVELS * LEVELS, 8 * slots * rows_dev * 256),
         name="vertical_adj",
     )(*operands)
 
 
 def legendre_fwd_body(lo, lx, own, recv, out, scratch):
-    slot = pl.program_id(0)
     groups, lats, slots, width = out.shape
-    total = dot(lo[0], own[0], ((0,), (0,))) + dot(lx[0], recv[0], ((0,), (0,)))
-    for tile in range(width // LANES):
-        scratch[tile, pl.ds(slot, groups * lats, stride=slots), :] = total[:, tile * LANES : (tile + 1) * LANES]
-
-    @pl.when(slot == slots - 1)
+    step = own.shape[0]
+    for i in range(step):
+        slot = pl.program_id(0) * step + i
+        total = dot(lo[i], own[i], ((0,), (0,))) + dot(lx[i], recv[i], ((0,), (0,)))
+        for tile in range(width // LANES):
+            scratch[tile, pl.ds(slot, groups * lats, stride=slots), :] = total[:, tile * LANES : (tile + 1) * LANES]
+
+    @pl.when(pl.program_id(0) == slots // step - 1)
     def _():
-        for group in range(groups):
+        @pl.loop(0, groups)
+        def _(group):
+            start = pl.multiple_of(group * lats * slots, lats * slots)
             for tile in range(width // LANES):
-                rows = scratch[tile, group * lats * slots : (group + 1) * lats * slots, :]
+                rows = scratch[tile, pl.ds(start, lats * slots), :]
                 out[group, :, :, tile * LANES : (tile + 1) * LANES] = rows.astype(BF16).reshape(lats, slots, LANES)
 
 
-def legendre_fwd(leg_own, leg_other, own, recv, groups):
-    slots, rows_dev, latitudes = leg_own.shape
-    width = own.shape[2]
+def legendre_fwd(leg_own, leg_other, own, recv, groups, first_slot):
+    slots, rows_dev, width = own.shape
+    latitudes = leg_own.shape[2]
+    step = STEP if slots % STEP == 0 else 1
+    first = first_slot // step
     lats = latitudes // groups
-    row = pl.BlockSpec((1, rows_dev, latitudes), lambda s: (s, 0, 0))
-    col = pl.BlockSpec((1, rows_dev, width), lambda s: (s, 0, 0))
+    row = pl.BlockSpec((step, rows_dev, latitudes), lambda s: (first + s, 0, 0))
+    other_row = pl.BlockSpec((step, rows_dev, latitudes), lambda s: (s, 0, 0))
+    col = pl.BlockSpec((step, rows_dev, width), lambda s: (s, 0, 0))
     shape = (groups, lats, slots, width)
     return pl.pallas_call(
         legendre_fwd_body,
-        grid=(slots,),
-        in_specs=[row, row, col, col],
+        grid=(slots // step,),
+        in_specs=[row, other_row, col, col],
         out_specs=pl.BlockSpec(shape, lambda s: (0, 0, 0, 0)),
         out_shape=jax.ShapeDtypeStruct(shape, BF16),
         scratch_shapes=[pltpu.VMEM((width // LANES, latitudes * slots, LANES), F32)],
         compiler_params=params("arbitrary"),
-        cost_estimate=cost(4 * slots * rows_dev * latitudes * width, 8 * slots * rows_dev * width),
+        cost_estimate=cost(16 * slots * rows_dev * latitudes * width, 8 * slots * rows_dev * width),
         name="legendre_fwd",
     )(leg_own, leg_other, own, recv)
 
 
 def legendre_adj_body(lo, lx, band, own, send, scratch):
-    slot = pl.program_id(0)
     groups, lats, slots, width = band.shape
-
-    @pl.when(slot == 0)
+    step = own.shape[0]
+
+    @pl.when(pl.program_id(0) == 0)
     def _():
-        for group in range(groups):
+        @pl.loop(0, groups)
+        def _(group):
+            start = pl.multiple_of(group * lats * slots, lats * slots)
             for tile in range(width // LANES):
                 rows = band[group, :, :, tile * LANES : (tile + 1) * LANES].reshape(lats * slots, LANES)
-                scratch[tile, group * lats * slots : (group + 1) * lats * slots, :] = rows.astype(F32)
-
-    rows = jnp.concatenate(
-        [scratch[tile, pl.ds(slot, groups * lats, stride=slots), :] for tile in range(width // LANES)], axis=1
-    ).astype(BF16)
-    own[0] = dot(lo[0], rows, ((1,), (0,))).astype(BF16)
-    send[0] = dot(lx[0], rows, ((1,), (0,))).astype(BF16)
-
-
-def legendre_adj(leg_own, leg_other, band_rows):
-    slots, rows_dev, latitudes = leg_own.shape
-    width = band_rows.shape[3]
-    row = pl.BlockSpec((1, rows_dev, latitudes), lambda s: (s, 0, 0))
-    col = pl.BlockSpec((1, rows_dev, width), lambda s: (s, 0, 0))
+                scratch[tile, pl.ds(start, lats * slots), :] = rows.astype(F32)
+
+    for i in range(step):
+        slot = pl.program_id(0) * step + i
+        rows = jnp.concatenate(
+            [scratch[tile, pl.ds(slot, groups * lats, stride=slots), :] for tile in range(width // LANES)], axis=1
+        ).astype(BF16)
+        own[i] = dot(lo[i], rows, ((1,), (0,))).astype(BF16)
+        send[i] = dot(lx[i], rows, ((1,), (0,))).astype(BF16)
+
+
+def legendre_adj(leg_own, leg_other, band_rows, first_slot):
+    _, rows_dev, latitudes = leg_own.shape
+    slots, width = band_rows.shape[2:]
+    step = STEP if slots % STEP == 0 else 1
+    first = first_slot // step
+    row = pl.BlockSpec((step, rows_dev, latitudes), lambda s: (first + s, 0, 0))
+    other_row = pl.BlockSpec((step, rows_dev, latitudes), lambda s: (s, 0, 0))
+    col = pl.BlockSpec((step, rows_dev, width), lambda s: (s, 0, 0))
     shape = jax.ShapeDtypeStruct((slots, rows_dev, width), BF16)
     return pl.pallas_call(
         legendre_adj_body,
-        grid=(slots,),
-        in_specs=[row, row, pl.BlockSpec(band_rows.shape, lambda s: (0, 0, 0, 0))],
+        grid=(slots // step,),
+        in_specs=[row, other_row, pl.BlockSpec(band_rows.shape, lambda s: (0, 0, 0, 0))],
         out_specs=[col, col],
         out_shape=[shape, shape],
         scratch_shapes=[pltpu.VMEM((width // LANES, latitudes * slots, LANES), F32)],
         compiler_params=params("arbitrary"),
-        cost_estimate=cost(4 * slots * rows_dev * latitudes * width, 8 * slots * rows_dev * width),
+        cost_estimate=cost(16 * slots * rows_dev * latitudes * width, 8 * slots * rows_dev * width),
         name="legendre_adj",
     )(leg_own, leg_other, band_rows)
 
@@ -315,10 +339,12 @@
 
 
 def chunked(control, wave_of_slot, legendre, vertical, points, lat_band, grid_scale, obs_weight):
-    members, slots, rows_dev = control.shape[:3]
+    members, slots, _ = control.shape[:3]
     groups = legendre.shape[2] // points.shape[0]
     lats, col_dev, _ = obs_weight.shape
     subs = col_dev // LEVELS
+    half = slots // 2
+    grid_shape = (members, lats, col_dev, LONGITUDES)
     info = lax.axis_index("lev").astype(jnp.int32)[None]
     waves = lax.dynamic_slice_in_dim(wave_of_slot, lax.axis_index("wave") * slots, slots)
     chooser = (
@@ -326,26 +352,47 @@
     ).astype(F32)
     lat_scale = jnp.dot(chooser, grid_scale, precision=lax.Precision.HIGHEST)[:, :, None]
     chunks = [(member, sub) for member in range(members) for sub in range(subs)]
-
-    leg_other = swap(legendre)
-    received = []
-    for member, sub in chunks:
-        own, send = vertical_fwd(control, vertical, info, waves, member, sub, subs)
-        received.append((own, swap(send)))
+    last = len(chunks) - 1
+    whole = [(q, 0, slots) for q in range(len(chunks))]
+    units_out = [(0, 0, half), (0, half, half)] + whole[1:]
+    units_back = whole[:-1] + [(last, 0, half), (last, half, half)]
+
+    leg_parts = []
+    for first in (0, half):
+        leg_parts.append(swap(legendre[first : first + half]))
+    fields = []
+    for q, first, count in units_out:
+        member, sub = chunks[q]
+        sent = vertical_fwd(control, vertical, info, waves, (member, sub, subs, True), first, count)
+        recv = swap(sent)
+        own = vertical_fwd(control, vertical, info, waves, (member, sub, subs, False), first, count)
+        fields.append((own, recv))
     tables = fourier_tables(points, wave_of_slot)
+    leg_other = jnp.concatenate(leg_parts, axis=0)
+
+    arrived = [[] for _ in chunks]
+    for (q, first, count), (own, recv) in zip(units_out, fields):
+        partner = leg_other if count == slots else leg_parts[first // half]
+        coeffs = legendre_fwd(legendre, partner, own, recv, groups, first)
+        arrived[q].append(exchange(coeffs))
     increment = gradient = None
-    bands = []
-    for (member, sub), (own, recv) in zip(chunks, received):
-        by_lat = exchange(legendre_fwd(legendre, leg_other, own, recv, groups))
+    adjoints = []
+    for q, (member, sub) in enumerate(chunks):
+        by_lat = arrived[q][0] if len(arrived[q]) == 1 else jnp.concatenate(arrived[q], axis=2)
         increment, adjoint = grid_stage(
-            by_lat, tables, lat_scale, obs_weight, member, sub, (members, lats, col_dev, LONGITUDES), increment
+            by_lat, tables, lat_scale, obs_weight, member, sub, grid_shape, increment
         )
-        bands.append(adjoint)
-    for (member, sub), adjoint in zip(chunks, bands):
-        own, send = legendre_adj(legendre, leg_other, exchange(adjoint))
-        gradient = vertical_adj(
-            own, swap(send), vertical, info, waves, member, sub, subs, control.shape, gradient
-        )
+        adjoints.append(adjoint)
+    for q, first, count in units_back:
+        member, sub = chunks[q]
+        partner = leg_other if count == slots else leg_parts[first // half]
+        band_rows = exchange(adjoints[q] if count == slots else adjoints[q][:, :, first : first + count])
+        own, sent = legendre_adj(legendre, partner, band_rows, first)
+        recv = swap(sent)
+        for block, other in ((own, False), (recv, True)):
+            gradient = vertical_adj(
+                block, vertical, info, waves, (member, sub, subs, other), first, control.shape, gradient
+            )
     return (increment, gradient)
 
 

time: 657 us -> 590 us (0.90)
  Pallas kernels: 342 us -> 275 us
  waiting for transfers between devices: 136 us -> 125 us
  blocking collectives: 106 us -> 113 us
    pallas_call x16 -> x30, Pallas kernels: 262 us -> 195 us  [the longest x10 85.2 us: vertical_fwd(): pl.pallas_call(functools.partial(vertical_fwd_body, first_slot), grid_spe...]
    all_to_all x6 -> x7, waiting for transfers between devices: 40.3 us -> 28.6 us  [exchange(): lax.all_to_all(values, 'wave', split_axis=0, concat_axis=0, tiled=True)]
    all_to_all x2 -> x3, blocking collectives: 106 us -> 113 us  [exchange(): lax.all_to_all(values, 'wave', split_axis=0, concat_axis=0, tiled=True)]
    all_to_all x6 -> x7, starting transfers between devices: 37.9 us -> 40.5 us  [exchange(): lax.all_to_all(values, 'wave', split_axis=0, concat_axis=0, tiled=True)]
    ppermute x9 -> x12, waiting for transfers between devices: 95.8 us -> 96.5 us  [swap(): return lax.ppermute(values, 'lev', [(0, 1), (1, 0)])]
  transfers between devices with their start and end apart: 15 -> 19, of which waited for: 7 -> 14; matrix products, arithmetic and copies ran while one was open for 1% -> 1% of each run, Pallas kernels for 47% -> 45%
where the time goes in v2:
time: 590 us; the launch traced here: 584 us
  Pallas kernels  275 us (47%)
  waiting for transfers between devices  125 us (21%)
  blocking collectives  113 us (19%)
  starting transfers between devices  51.3 us (9%)
  local copies, waits for them, and re-layouts  16.6 us (3%)
    all_to_all x3, blocking collectives, exchange(): lax.all_to_all(values, 'wave', split_axis=0, concat_axis=0, tiled=True)  113 us
    ppermute x12, waiting for transfers between devices, swap(): return lax.ppermute(values, 'lev', [(0, 1), (1, 0)])  96.5 us
    pallas_call x10, Pallas kernels, vertical_fwd(): pl.pallas_call(functools.partial(vertical_fwd_body, first_slot), grid_spe...  85.2 us
    pallas_call x4, Pallas kernels, grid_stage(): pl.pallas_call(grid_body, grid=(lats,), in_specs=in_specs, out_specs=[pl....  62.2 us
    pallas_call x10, Pallas kernels, vertical_adj(): pl.pallas_call(functools.partial(vertical_adj_body, first_slot), grid_spe...  59 us
    all_to_all x7, starting transfers between devices, exchange(): lax.all_to_all(values, 'wave', split_axis=0, concat_axis=0, tiled=True)  40.5 us
    all_to_all x7, waiting for transfers between devices, exchange(): lax.all_to_all(values, 'wave', split_axis=0, concat_axis=0, tiled=True)  28.6 us
    pallas_call x5, Pallas kernels, legendre_adj(): pl.pallas_call(legendre_adj_body, grid=(slots // step,), in_specs=[row, o...  25.6 us
  transfers between devices with their start and end apart: 19, of which 14 were waited for; matrix products, arithmetic and copies ran while one was open for 1% of the time, Pallas kernels for 45%

profile of v2, /device:TPU:13, one launch (start us, length us, event | category | flops | bytes accessed | tf_op | source)
XLA Modules:
  0.0 584.2 jit_solution(7153102642034402997)
XLA Ops:
  0.7 1.3 dynamic_slice.3.waves
  2.0 6.3 %vertical_fwd.19 = bf16[8,128,256]{2,1,0:T(8,128)(2,1)} custom-call(s32[1]{0:T(128)} %bitcast.info, s32[16]{0:T(128)} %dynamic_slice.3.waves, bf16[2,16,128,2,512]{4,3,2,1,0:T(2,128)(2,1)} %x.19, bf16[4,4,128,128]{3,2,1,0:T(8,128)(2,1)} %v.39), custom_call_target="tpu_custom_call" | custom-call | flops 4294967296 | bytes 2097152 | tf_op jit(solution)/shard_map/vertical_fwd/pallas_call | solution.py:77
  9.9 6.2 %vertical_fwd.18.own = bf16[8,128,256]{2,1,0:T(8,128)(2,1)} custom-call(s32[1]{0:T(128)} %bitcast.info, s32[16]{0:T(128)} %dynamic_slice.3.waves, bf16[2,16,128,2,512]{4,3,2,1,0:T(2,128)(2,1)} %x.19, bf16[4,4,128,128]{3,2,1,0:T(8,128)(2,1)} %v.39), custom_call_target="tpu_custom_call" | custom-call | flops 4294967296 | bytes 2097152 | tf_op jit(solution)/shard_map/vertical_fwd/pallas_call | solution.py:77
  16.1 5.2 collective-permute-done.6.recv
  21.3 11.2 %collective-permute-done.1.lx = bf16[8,128,256]{2,1,0:T(8,128)(2,1)S(1)} collective-permute-done((bf16[8,128,256]{2,1,0:T(8,128)(2,1)S(1)}, bf16[8,128,256]{2,1,0:T(8,128)(2,1)S(1)}, u32[]{:S(2)}, u32[]{:S(2)}) %collective-permute-start.1) | collective-permute-done | bytes 524320 | tf_op jit(solution)/shard_map/ppermute | solution.py:334
  33.4 3.4 legendre_fwd.9
  36.7 7.4 %all-to-all-start.4 = ((bf16[16,16,8,256]{3,2,1,0:T(8,128)(2,1)}), bf16[16,16,8,256]{3,2,1,0:T(8,128)(2,1)S(1)}, u32[]{:S(2)}, u32[]{:S(2)}) async-start(bf16[16,16,8,256]{3,2,1,0:T(8,128)(2,1)} %legendre_fwd.9), calls=%async_computation.4 | async-start | bytes 2097152 | tf_op jit(solution)/shard_map/all_to_all | solution.py:338
  44.1 6.2 %vertical_fwd.17 = bf16[8,128,256]{2,1,0:T(8,128)(2,1)} custom-call(s32[1]{0:T(128)} %bitcast.info, s32[16]{0:T(128)} %dynamic_slice.3.waves, bf16[2,16,128,2,512]{4,3,2,1,0:T(2,128)(2,1)} %x.19, bf16[4,4,128,128]{3,2,1,0:T(8,128)(2,1)} %v.39), custom_call_target="tpu_custom_call" | custom-call | flops 4294967296 | bytes 2097152 | tf_op jit(solution)/shard_map/vertical_fwd/pallas_call | solution.py:77
  51.8 6.2 %vertical_fwd.16.own = bf16[8,128,256]{2,1,0:T(8,128)(2,1)} custom-call(s32[1]{0:T(128)} %bitcast.info, s32[16]{0:T(128)} %dynamic_slice.3.waves, bf16[2,16,128,2,512]{4,3,2,1,0:T(2,128)(2,1)} %x.19, bf16[4,4,128,128]{3,2,1,0:T(8,128)(2,1)} %v.39), custom_call_target="tpu_custom_call" | custom-call | flops 4294967296 | bytes 2097152 | tf_op jit(solution)/shard_map/vertical_fwd/pallas_call | solution.py:77
  58.0 5.6 collective-permute-done.5.recv
  63.6 11.2 %collective-permute-done.lx = bf16[8,128,256]{2,1,0:T(8,128)(2,1)S(1)} collective-permute-done((bf16[8,128,256]{2,1,0:T(8,128)(2,1)S(1)}, bf16[8,128,256]{2,1,0:T(8,128)(2,1)S(1)}, u32[]{:S(2)}, u32[]{:S(2)}) %collective-permute-start) | collective-permute-done | bytes 524320 | tf_op jit(solution)/shard_map/ppermute | solution.py:334
  75.6 3.4 legendre_fwd.8
  79.1 6.9 %all-to-all-start.3 = ((bf16[16,16,8,256]{3,2,1,0:T(8,128)(2,1)}), bf16[16,16,8,256]{3,2,1,0:T(8,128)(2,1)S(1)}, u32[]{:S(2)}, u32[]{:S(2)}) async-start(bf16[16,16,8,256]{3,2,1,0:T(8,128)(2,1)} %legendre_fwd.8), calls=%async_computation.3 | async-start | bytes 2097152 | tf_op jit(solution)/shard_map/all_to_all | solution.py:338
  85.9 10.0 %vertical_fwd.11 = bf16[16,128,256]{2,1,0:T(8,128)(2,1)} custom-call(s32[1]{0:T(128)} %bitcast.info, s32[16]{0:T(128)} %dynamic_slice.3.waves, bf16[2,16,128,2,512]{4,3,2,1,0:T(2,128)(2,1)} %x.19, bf16[4,4,128,128]{3,2,1,0:T(8,128)(2,1)} %v.39), custom_call_target="tpu_custom_call" | custom-call | flops 8589934592 | bytes 4194304 | tf_op jit(solution)/shard_map/vertical_fwd/pallas_call | solution.py:77
  97.2 10.0 %vertical_fwd.10.own = bf16[16,128,256]{2,1,0:T(8,128)(2,1)} custom-call(s32[1]{0:T(128)} %bitcast.info, s32[16]{0:T(128)} %dynamic_slice.3.waves, bf16[2,16,128,2,512]{4,3,2,1,0:T(2,128)(2,1)} %x.19, bf16[4,4,128,128]{3,2,1,0:T(8,128)(2,1)} %v.39), custom_call_target="tpu_custom_call" | custom-call | flops 8589934592 | bytes 4194304 | tf_op jit(solution)/shard_map/vertical_fwd/pallas_call | solution.py:77
  107.3 13.2 %collective-permute-done.2.recv = bf16[16,128,256]{2,1,0:T(8,128)(2,1)S(1)} collective-permute-done((bf16[16,128,256]{2,1,0:T(8,128)(2,1)}, bf16[16,128,256]{2,1,0:T(8,128)(2,1)S(1)}, u32[]{:S(2)}, u32[]{:S(2)}) %collective-permute-start.2) | collective-permute-done | bytes 1048608 | tf_op jit(solution)/shard_map/ppermute | solution.py:334
  121.5 6.0 %legendre_fwd.5 = bf16[16,16,16,256]{3,2,1,0:T(8,128)(2,1)} custom-call(bf16[16,128,256]{2,1,0:T(8,128)(2,1)} %lo.19, bf16[16,128,256]{2,1,0:T(8,128)(2,1)} %copy-done.14, bf16[16,128,256]{2,1,0:T(8,128)(2,1)} %vertical_fwd.10.own, bf16[16,128,256]{2,1,0:T(8,128)(2,1)} %copy-done.18), custom_call_target="tpu_custom_call" | custom-call | flops 2147483648 | bytes 4194304 | tf_op jit(solution)/shard_map/legendre_fwd/pallas_call | solution.py:180
  128.6 6.9 %all-to-all-start = ((bf16[16,16,16,256]{3,2,1,0:T(8,128)(2,1)}), bf16[16,16,16,256]{3,2,1,0:T(8,128)(2,1)S(1)}, u32[]{:S(2)}, u32[]{:S(2)}) async-start(bf16[16,16,16,256]{3,2,1,0:T(8,128)(2,1)} %legendre_fwd.5), calls=%async_computation | async-start | bytes 4194304 | tf_op jit(solution)/shard_map/all_to_all | solution.py:338
  135.4 10.0 %vertical_fwd.13 = bf16[16,128,256]{2,1,0:T(8,128)(2,1)} custom-call(s32[1]{0:T(128)} %bitcast.info, s32[16]{0:T(128)} %dynamic_slice.3.waves, bf16[2,16,128,2,512]{4,3,2,1,0:T(2,128)(2,1)} %x.19, bf16[4,4,128,128]{3,2,1,0:T(8,128)(2,1)} %v.39), custom_call_target="tpu_custom_call" | custom-call | flops 8589934592 | bytes 4194304 | tf_op jit(solution)/shard_map/vertical_fwd/pallas_call | solution.py:77
  146.7 10.0 %vertical_fwd.12.own = bf16[16,128,256]{2,1,0:T(8,128)(2,1)} custom-call(s32[1]{0:T(128)} %bitcast.info, s32[16]{0:T(128)} %dynamic_slice.3.waves, bf16[2,16,128,2,512]{4,3,2,1,0:T(2,128)(2,1)} %x.19, bf16[4,4,128,128]{3,2,1,0:T(8,128)(2,1)} %v.39), custom_call_target="tpu_custom_call" | custom-call | flops 8589934592 | bytes 4194304 | tf_op jit(solution)/shard_map/vertical_fwd/pallas_call | solution.py:77
  156.7 13.3 %collective-permute-done.3.recv = bf16[16,128,256]{2,1,0:T(8,128)(2,1)S(1)} collective-permute-done((bf16[16,128,256]{2,1,0:T(8,128)(2,1)}, bf16[16,128,256]{2,1,0:T(8,128)(2,1)S(1)}, u32[]{:S(2)}, u32[]{:S(2)}) %collective-permute-start.3) | collective-permute-done | bytes 1048608 | tf_op jit(solution)/shard_map/ppermute | solution.py:334
  171.0 6.0 %legendre_fwd.6 = bf16[16,16,16,256]{3,2,1,0:T(8,128)(2,1)} custom-call(bf16[16,128,256]{2,1,0:T(8,128)(2,1)} %lo.19, bf16[16,128,256]{2,1,0:T(8,128)(2,1)} %copy-done.14, bf16[16,128,256]{2,1,0:T(8,128)(2,1)} %vertical_fwd.12.own, bf16[16,128,256]{2,1,0:T(8,128)(2,1)} %copy-done.19), custom_call_target="tpu_custom_call" | custom-call | flops 2147483648 | bytes 4194304 | tf_op jit(solution)/shard_map/legendre_fwd/pallas_call | solution.py:180
  177.1 5.8 all-to-all-done.by_lat
  182.9 4.8 all-to-all-start.1
  187.6 10.0 %vertical_fwd.15 = bf16[16,128,256]{2,1,0:T(8,128)(2,1)} custom-call(s32[1]{0:T(128)} %bitcast.info, s32[16]{0:T(128)} %dynamic_slice.3.waves, bf16[2,16,128,2,512]{4,3,2,1,0:T(2,128)(2,1)} %x.19, bf16[4,4,128,128]{3,2,1,0:T(8,128)(2,1)} %v.39), custom_call_target="tpu_custom_call" | custom-call | flops 8589934592 | bytes 4194304 | tf_op jit(solution)/shard_map/vertical_fwd/pallas_call | solution.py:77
  198.9 10.0 %vertical_fwd.14.own = bf16[16,128,256]{2,1,0:T(8,128)(2,1)} custom-call(s32[1]{0:T(128)} %bitcast.info, s32[16]{0:T(128)} %dynamic_slice.3.waves, bf16[2,16,128,2,512]{4,3,2,1,0:T(2,128)(2,1)} %x.19, bf16[4,4,128,128]{3,2,1,0:T(8,128)(2,1)} %v.39), custom_call_target="tpu_custom_call" | custom-call | flops 8589934592 | bytes 4194304 | tf_op jit(solution)/shard_map/vertical_fwd/pallas_call | solution.py:77
  208.9 13.4 %collective-permute-done.4.recv = bf16[16,128,256]{2,1,0:T(8,128)(2,1)S(1)} collective-permute-done((bf16[16,128,256]{2,1,0:T(8,128)(2,1)}, bf16[16,128,256]{2,1,0:T(8,128)(2,1)S(1)}, u32[]{:S(2)}, u32[]{:S(2)}) %collective-permute-start.4) | collective-permute-done | bytes 1048608 | tf_op jit(solution)/shard_map/ppermute | solution.py:334
  223.3 6.1 %legendre_fwd.7 = bf16[16,16,16,256]{3,2,1,0:T(8,128)(2,1)} custom-call(bf16[16,128,256]{2,1,0:T(8,128)(2,1)} %lo.19, bf16[16,128,256]{2,1,0:T(8,128)(2,1)} %copy-done.14, bf16[16,128,256]{2,1,0:T(8,128)(2,1)} %vertical_fwd.14.own, bf16[16,128,256]{2,1,0:T(8,128)(2,1)} %copy-done.20), custom_call_target="tpu_custom_call" | custom-call | flops 2147483648 | bytes 4194304 | tf_op jit(solution)/shard_map/legendre_fwd/pallas_call | solution.py:180
  229.4 5.8 all-to-all-done.1.by_lat
  235.2 4.8 all-to-all-start.2
  241.0 1.9 copy.26.scale
  242.9 18.1 %fourier_tables.1 = (bf16[16,256,512]{2,1,0:T(8,128)(2,1)}, bf16[16,256,512]{2,1,0:T(8,128)(2,1)}) custom-call(s32[16]{0:T(128)} %points.1, f32[256,1]{1,0:T(8,128)} %copy.22.waves), custom_call_target="tpu_custom_call" | custom-call | flops 83886080 | bytes 8388608 | tf_op jit(solution)/shard_map/fourier_tables/pallas_call | solution.py:267
  261.0 2.8 pad_maximum_fusion.by_lat
  263.8 15.5 %grid_stage.4 = (bf16[2,16,256,512]{3,2,1,0:T(8,128)(2,1)}, bf16[16,16,16,256]{3,2,1,0:T(8,128)(2,1)}) custom-call(bf16[16,16,16,256]{3,2,1,0:T(8,128)(2,1)} %pad_maximum_fusion.by_lat, bf16[16,256,512]{2,1,0:T(8,128)(2,1)} %get-tuple-element.22.cosine, bf16[16,256,512]{2,1,0:T(8,128)(2,1)} %get-tuple-element.23.sine, f32[16,256,1]{2,1,0:T(8,128)} %copy.26.scale, ...), custom_call_target="tpu_custom_call" | custom-call | flops 2147483648 | bytes 12582912 | tf_op jit(solution)/shard_map/grid_stage/pallas_call | solution.py:317
  279.4 8.0 %all-to-all-done.2.by_lat = bf16[16,16,16,256]{3,2,1,0:T(8,128)(2,1)S(1)} async-done(((bf16[16,16,16,256]{3,2,1,0:T(8,128)(2,1)}), bf16[16,16,16,256]{3,2,1,0:T(8,128)(2,1)S(1)}, u32[]{:S(2)}, u32[]{:S(2)}) %all-to-all-start.2) | async-done | bytes 2097184 | tf_op jit(solution)/shard_map/all_to_all | solution.py:338
  287.4 4.8 all-to-all-start.9
  292.1 15.6 %grid_stage.5 = (bf16[2,16,256,512]{3,2,1,0:T(8,128)(2,1)}, bf16[16,16,16,256]{3,2,1,0:T(8,128)(2,1)}) custom-call(bf16[16,16,16,256]{3,2,1,0:T(8,128)(2,1)} %copy-done.3, bf16[16,256,512]{2,1,0:T(8,128)(2,1)} %get-tuple-element.22.cosine, bf16[16,256,512]{2,1,0:T(8,128)(2,1)} %get-tuple-element.23.sine, ...), custom_call_target="tpu_custom_call", output_to_operand_aliasing={{0}: (5, {})} | custom-call | flops 2147483648 | bytes 12582912 | tf_op jit(solution)/shard_map/grid_stage/pallas_call | solution.py:317
  307.7 15.5 %grid_stage.6 = (bf16[2,16,256,512]{3,2,1,0:T(8,128)(2,1)}, bf16[16,16,16,256]{3,2,1,0:T(8,128)(2,1)}) custom-call(bf16[16,16,16,256]{3,2,1,0:T(8,128)(2,1)} %all-to-all-done.1.by_lat, bf16[16,256,512]{2,1,0:T(8,128)(2,1)} %get-tuple-element.22.cosine, bf16[16,256,512]{2,1,0:T(8,128)(2,1)} %get-tuple-element.23.sine, ...), custom_call_target="tpu_custom_call", output_to_operand_aliasing={{0}: (5, {})} | custom-call | flops 2147483648 | bytes 12582912 | tf_op jit(solution)/shard_map/grid_stage/pallas_call | solution.py:317
  323.2 15.5 %grid_stage.7 = (bf16[2,16,256,512]{3,2,1,0:T(8,128)(2,1)}, bf16[16,16,16,256]{3,2,1,0:T(8,128)(2,1)}) custom-call(bf16[16,16,16,256]{3,2,1,0:T(8,128)(2,1)} %copy-done.2, bf16[16,256,512]{2,1,0:T(8,128)(2,1)} %get-tuple-element.22.cosine, bf16[16,256,512]{2,1,0:T(8,128)(2,1)} %get-tuple-element.23.sine, ...), custom_call_target="tpu_custom_call", output_to_operand_aliasing={{0}: (5, {})} | custom-call | flops 2147483648 | bytes 12582912 | tf_op jit(solution)/shard_map/grid_stage/pallas_call | solution.py:317
  338.8 1.7 fusion.1
  340.5 30.9 %all_to_all.50.band = bf16[16,16,8,256]{3,2,1,0:T(8,128)(2,1)} all-to-all(bf16[16,16,8,256]{3,2,1,0:T(8,128)(2,1)S(1)} %get-tuple-element.42), channel_id=1, replica_groups=mesh['wave'=16,'lev'=2] {'wave'}, dimensions={0} | all-to-all | bytes 2097152 | tf_op jit(solution)/shard_map/all_to_all | solution.py:338
  371.3 29.6 %all_to_all.51.band = bf16[16,16,8,256]{3,2,1,0:T(8,128)(2,1)} all-to-all(bf16[16,16,8,256]{3,2,1,0:T(8,128)(2,1)S(1)} %get-tuple-element.43), channel_id=1, replica_groups=mesh['wave'=16,'lev'=2] {'wave'}, dimensions={0} | all-to-all | bytes 2097152 | tf_op jit(solution)/shard_map/all_to_all | solution.py:338
  400.9 52.1 %all_to_all.52.band = bf16[16,16,16,256]{3,2,1,0:T(8,128)(2,1)} all-to-all(bf16[16,16,16,256]{3,2,1,0:T(8,128)(2,1)S(1)} %copy-done.6), channel_id=1, replica_groups=mesh['wave'=16,'lev'=2] {'wave'}, dimensions={0} | all-to-all | bytes 4194304 | tf_op jit(solution)/shard_map/all_to_all | solution.py:338
  453.0 5.0 all-to-all-start.7
  458.0 6.4 %legendre_adj.9 = (bf16[16,128,256]{2,1,0:T(8,128)(2,1)}, bf16[16,128,256]{2,1,0:T(8,128)(2,1)}) custom-call(bf16[16,128,256]{2,1,0:T(8,128)(2,1)} %lo.19, bf16[16,128,256]{2,1,0:T(8,128)(2,1)} %copy-done.14, bf16[16,16,16,256]{3,2,1,0:T(8,128)(2,1)} %all-to-all-done.9.band), custom_call_target="tpu_custom_call" | custom-call | flops 2147483648 | bytes 4194304 | tf_op jit(solution)/shard_map/legendre_adj/pallas_call | solution.py:224
  465.6 6.8 %vertical_adj.10.rest_0_ = bf16[2,16,128,2,512]{4,3,2,1,0:T(2,128)(2,1)} custom-call(s32[1]{0:T(128)} %bitcast.info, s32[16]{0:T(128)} %dynamic_slice.3.waves, bf16[16,128,256]{2,1,0:T(8,128)(2,1)} %get-tuple-element.41.block, bf16[4,4,128,128]{3,2,1,0:T(8,128)(2,1)} %v.39), custom_call_target="tpu_custom_call" | custom-call | flops 8589934592 | bytes 4194304 | tf_op jit(solution)/shard_map/vertical_adj/pallas_call | solution.py:132
  472.4 3.3 legendre_adj.5
  475.9 3.3 legendre_adj.6
  480.4 6.3 %legendre_adj.8 = (bf16[16,128,256]{2,1,0:T(8,128)(2,1)}, bf16[16,128,256]{2,1,0:T(8,128)(2,1)}) custom-call(bf16[16,128,256]{2,1,0:T(8,128)(2,1)} %lo.19, bf16[16,128,256]{2,1,0:T(8,128)(2,1)} %copy-done.14, bf16[16,16,16,256]{3,2,1,0:T(8,128)(2,1)} %all_to_all.52.band), custom_call_target="tpu_custom_call" | custom-call | flops 2147483648 | bytes 4194304 | tf_op jit(solution)/shard_map/legendre_adj/pallas_call | solution.py:224
  487.0 1.9 collective-permute-done.11.block
  489.9 6.8 %vertical_adj.11.rest_0_ = bf16[2,16,128,2,512]{4,3,2,1,0:T(2,128)(2,1)} custom-call(s32[1]{0:T(128)} %bitcast.info, s32[16]{0:T(128)} %dynamic_slice.3.waves, bf16[16,128,256]{2,1,0:T(8,128)(2,1)} %copy-done.16, bf16[4,4,128,128]{3,2,1,0:T(8,128)(2,1)} %v.39, bf16[2,16,128,2,512]{4,3,2,1,0:T(2,128)(2,1)} %vertical_adj.10.rest_0_), custom_call_target="tpu_custom_call", output_to_operand_aliasing={{}: (4, {})} | custom-call | flops 8589934592 | bytes 4194304 | tf_op jit(solution)/shard_map/vertical_adj/pallas_call | solution.py:132
  496.7 9.1 %all-to-all-done.7.band = bf16[16,16,16,256]{3,2,1,0:T(8,128)(2,1)S(1)} async-done(((bf16[16,16,16,256]{3,2,1,0:T(8,128)(2,1)}), bf16[16,16,16,256]{3,2,1,0:T(8,128)(2,1)S(1)}, u32[]{:S(2)}, u32[]{:S(2)}) %all-to-all-start.7) | async-done | bytes 2097184 | tf_op jit(solution)/shard_map/all_to_all | solution.py:338
  505.7 1.4 copy-done.5
  507.1 6.3 %legendre_adj.7 = (bf16[16,128,256]{2,1,0:T(8,128)(2,1)}, bf16[16,128,256]{2,1,0:T(8,128)(2,1)}) custom-call(bf16[16,128,256]{2,1,0:T(8,128)(2,1)} %lo.19, bf16[16,128,256]{2,1,0:T(8,128)(2,1)} %copy-done.14, bf16[16,16,16,256]{3,2,1,0:T(8,128)(2,1)} %copy-done.5), custom_call_target="tpu_custom_call" | custom-call | flops 2147483648 | bytes 4194304 | tf_op jit(solution)/shard_map/legendre_adj/pallas_call | solution.py:224
  514.6 6.8 %vertical_adj.12.rest_0_ = bf16[2,16,128,2,512]{4,3,2,1,0:T(2,128)(2,1)} custom-call(s32[1]{0:T(128)} %bitcast.info, s32[16]{0:T(128)} %dynamic_slice.3.waves, bf16[16,128,256]{2,1,0:T(8,128)(2,1)} %get-tuple-element.38.block, bf16[4,4,128,128]{3,2,1,0:T(8,128)(2,1)} %v.39, ...), custom_call_target="tpu_custom_call", output_to_operand_aliasing={{}: (4, {})} | custom-call | flops 8589934592 | bytes 4194304 | tf_op jit(solution)/shard_map/vertical_adj/pallas_call | solution.py:132
  521.4 12.6 %collective-permute-done.10.block = bf16[16,128,256]{2,1,0:T(8,128)(2,1)} collective-permute-done((bf16[16,128,256]{2,1,0:T(8,128)(2,1)}, bf16[16,128,256]{2,1,0:T(8,128)(2,1)}, u32[]{:S(2)}, u32[]{:S(2)}) %collective-permute-start.10) | collective-permute-done | bytes 1048608 | tf_op jit(solution)/shard_map/ppermute | solution.py:334
  534.0 6.8 %vertical_adj.13.rest_0_ = bf16[2,16,128,2,512]{4,3,2,1,0:T(2,128)(2,1)} custom-call(s32[1]{0:T(128)} %bitcast.info, s32[16]{0:T(128)} %dynamic_slice.3.waves, bf16[16,128,256]{2,1,0:T(8,128)(2,1)} %collective-permute-done.10.block, bf16[4,4,128,128]{3,2,1,0:T(8,128)(2,1)} %v.39, ...), custom_call_target="tpu_custom_call", output_to_operand_aliasing={{}: (4, {})} | custom-call | flops 8589934592 | bytes 4194304 | tf_op jit(solution)/shard_map/vertical_adj/pallas_call | solution.py:132
  540.8 6.8 %vertical_adj.14.rest_0_ = bf16[2,16,128,2,512]{4,3,2,1,0:T(2,128)(2,1)} custom-call(s32[1]{0:T(128)} %bitcast.info, s32[16]{0:T(128)} %dynamic_slice.3.waves, bf16[16,128,256]{2,1,0:T(8,128)(2,1)} %get-tuple-element.35.block, bf16[4,4,128,128]{3,2,1,0:T(8,128)(2,1)} %v.39, ...), custom_call_target="tpu_custom_call", output_to_operand_aliasing={{}: (4, {})} | custom-call | flops 8589934592 | bytes 4194304 | tf_op jit(solution)/shard_map/vertical_adj/pallas_call | solution.py:132
  547.6 8.8 %collective-permute-done.9.block = bf16[16,128,256]{2,1,0:T(8,128)(2,1)S(1)} collective-permute-done((bf16[16,128,256]{2,1,0:T(8,128)(2,1)}, bf16[16,128,256]{2,1,0:T(8,128)(2,1)S(1)}, u32[]{:S(2)}, u32[]{:S(2)}) %collective-permute-start.9) | collective-permute-done | bytes 1048608 | tf_op jit(solution)/shard_map/ppermute | solution.py:334
  557.4 6.8 %vertical_adj.15.rest_0_ = bf16[2,16,128,2,512]{4,3,2,1,0:T(2,128)(2,1)} custom-call(s32[1]{0:T(128)} %bitcast.info, s32[16]{0:T(128)} %dynamic_slice.3.waves, bf16[16,128,256]{2,1,0:T(8,128)(2,1)} %copy-done.17, bf16[4,4,128,128]{3,2,1,0:T(8,128)(2,1)} %v.39, bf16[2,16,128,2,512]{4,3,2,1,0:T(2,128)(2,1)} %vertical_adj.14.rest_0_), custom_call_target="tpu_custom_call", output_to_operand_aliasing={{}: (4, {})} | custom-call | flops 8589934592 | bytes 4194304 | tf_op jit(solution)/shard_map/vertical_adj/pallas_call | solution.py:132
  564.2 4.6 vertical_adj.16.rest_0_
  569.5 4.6 vertical_adj.17.rest_0_
  574.1 4.6 vertical_adj.18.rest_0_
  579.5 4.7 vertical_adj.19
  (70 shorter events, 21.2 us)
Async XLA Ops:
  0.6 240.1 %copy-start = (f32[8,256]{1,0:T(8,128)S(1)}, f32[8,256]{1,0:T(8,128)}, u32[]{:S(2)}) copy-start(f32[8,256]{1,0:T(8,128)} %param.14) | copy-start | bytes 24580
  2.0 7.6 %copy-start.7 = (bf16[16,128,256]{2,1,0:T(8,128)(2,1)S(1)}, bf16[16,128,256]{2,1,0:T(8,128)(2,1)}, u32[]{:S(2)}) copy-start(bf16[16,128,256]{2,1,0:T(8,128)(2,1)} %lo.19) | copy-start | bytes 3145732
  8.3 13.0 %collective-permute-start.6 = (bf16[8,128,256]{2,1,0:T(8,128)(2,1)}, bf16[8,128,256]{2,1,0:T(8,128)(2,1)S(1)}, u32[]{:S(2)}, u32[]{:S(2)}) collective-permute-start(bf16[8,128,256]{2,1,0:T(8,128)(2,1)} %vertical_fwd.19), channel_id=1, source_target_pairs={{0,1},{1,0},{2,3},{3,2},{4,5},{5,4},{6,7},{7,6},{8,9},{9,8},{10,11... | collective-permute-start | bytes 1572872 | tf_op jit(solution)/shard_map/ppermute | solution.py:334
  9.6 22.9 %collective-permute-start.1 = (bf16[8,128,256]{2,1,0:T(8,128)(2,1)S(1)}, bf16[8,128,256]{2,1,0:T(8,128)(2,1)S(1)}, u32[]{:S(2)}, u32[]{:S(2)}) collective-permute-start(bf16[8,128,256]{2,1,0:T(8,128)(2,1)S(1)} %get-tuple-element.44), channel_id=1, source_target_pairs={{0,1},{1,0},{2,3},{3,2},{4,5},{5,4},{6,7},{7,6},{8,9},{9,8},{10,11... | collective-permute-start | bytes 1572872 | tf_op jit(solution)/shard_map/ppermute | solution.py:334
  21.3 11.2 %copy-start.21 = (bf16[8,128,256]{2,1,0:T(8,128)(2,1)}, bf16[8,128,256]{2,1,0:T(8,128)(2,1)S(1)}, u32[]{:S(2)}) copy-start(bf16[8,128,256]{2,1,0:T(8,128)(2,1)S(1)} %collective-permute-done.6.recv) | copy-start | bytes 1572868
  32.6 0.8 copy-start.10
  36.7 42.3 %all-to-all-start.4 = ((bf16[16,16,8,256]{3,2,1,0:T(8,128)(2,1)}), bf16[16,16,8,256]{3,2,1,0:T(8,128)(2,1)S(1)}, u32[]{:S(2)}, u32[]{:S(2)}) async-start(bf16[16,16,8,256]{3,2,1,0:T(8,128)(2,1)} %legendre_fwd.9), calls=%async_computation.4 | async-start | bytes 2097152 | tf_op jit(solution)/shard_map/all_to_all | solution.py:338
  50.3 13.3 %collective-permute-start.5 = (bf16[8,128,256]{2,1,0:T(8,128)(2,1)}, bf16[8,128,256]{2,1,0:T(8,128)(2,1)S(1)}, u32[]{:S(2)}, u32[]{:S(2)}) collective-permute-start(bf16[8,128,256]{2,1,0:T(8,128)(2,1)} %vertical_fwd.17), channel_id=1, source_target_pairs={{0,1},{1,0},{2,3},{3,2},{4,5},{5,4},{6,7},{7,6},{8,9},{9,8},{10,11... | collective-permute-start | bytes 1572872 | tf_op jit(solution)/shard_map/ppermute | solution.py:334
  51.5 23.3 %collective-permute-start = (bf16[8,128,256]{2,1,0:T(8,128)(2,1)S(1)}, bf16[8,128,256]{2,1,0:T(8,128)(2,1)S(1)}, u32[]{:S(2)}, u32[]{:S(2)}) collective-permute-start(bf16[8,128,256]{2,1,0:T(8,128)(2,1)S(1)} %get-tuple-element.45), channel_id=1, source_target_pairs={{0,1},{1,0},{2,3},{3,2},{4,5},{5,4},{6,7},{7,6},{8,9},{9,8},{10,11... | collective-permute-start | bytes 1572872 | tf_op jit(solution)/shard_map/ppermute | solution.py:334
  63.6 11.2 %copy-start.22 = (bf16[8,128,256]{2,1,0:T(8,128)(2,1)}, bf16[8,128,256]{2,1,0:T(8,128)(2,1)S(1)}, u32[]{:S(2)}) copy-start(bf16[8,128,256]{2,1,0:T(8,128)(2,1)S(1)} %collective-permute-done.5.recv) | copy-start | bytes 1572868
  74.8 0.8 copy-start.12
  79.1 48.5 %all-to-all-start.3 = ((bf16[16,16,8,256]{3,2,1,0:T(8,128)(2,1)}), bf16[16,16,8,256]{3,2,1,0:T(8,128)(2,1)S(1)}, u32[]{:S(2)}, u32[]{:S(2)}) async-start(bf16[16,16,8,256]{3,2,1,0:T(8,128)(2,1)} %legendre_fwd.8), calls=%async_computation.3 | async-start | bytes 2097152 | tf_op jit(solution)/shard_map/all_to_all | solution.py:338
  96.0 11.3 %copy-start.13 = (bf16[8,128,256]{2,1,0:T(8,128)(2,1)S(1)}, bf16[8,128,256]{2,1,0:T(8,128)(2,1)}, u32[]{:S(2)}) copy-start(bf16[8,128,256]{2,1,0:T(8,128)(2,1)} %copy-done.12) | copy-start | bytes 1572868
  96.0 11.3 %copy-start.11 = (bf16[8,128,256]{2,1,0:T(8,128)(2,1)S(1)}, bf16[8,128,256]{2,1,0:T(8,128)(2,1)}, u32[]{:S(2)}) copy-start(bf16[8,128,256]{2,1,0:T(8,128)(2,1)} %copy-done.10) | copy-start | bytes 1572868
  96.0 24.5 %collective-permute-start.2 = (bf16[16,128,256]{2,1,0:T(8,128)(2,1)}, bf16[16,128,256]{2,1,0:T(8,128)(2,1)S(1)}, u32[]{:S(2)}, u32[]{:S(2)}) collective-permute-start(bf16[16,128,256]{2,1,0:T(8,128)(2,1)} %vertical_fwd.11), channel_id=1, source_target_pairs={{0,1},{1,0},{2,3},{3,2},{4,5},{5,4},{6,7},{7,6},{8,9},{9,8},{10,11... | collective-permute-start | bytes 3145736 | tf_op jit(solution)/shard_map/ppermute | solution.py:334
  107.3 13.2 %copy-start.14 = (bf16[16,128,256]{2,1,0:T(8,128)(2,1)}, bf16[16,128,256]{2,1,0:T(8,128)(2,1)S(1)}, u32[]{:S(2)}) copy-start(bf16[16,128,256]{2,1,0:T(8,128)(2,1)S(1)} %constant_dynamic-update-slice_fusion.lx) | copy-start | bytes 3145732
  120.5 1.0 copy-start.18
  127.6 1.0 copy-start.4
  128.6 54.3 %all-to-all-start = ((bf16[16,16,16,256]{3,2,1,0:T(8,128)(2,1)}), bf16[16,16,16,256]{3,2,1,0:T(8,128)(2,1)S(1)}, u32[]{:S(2)}, u32[]{:S(2)}) async-start(bf16[16,16,16,256]{3,2,1,0:T(8,128)(2,1)} %legendre_fwd.5), calls=%async_computation | async-start | bytes 4194304 | tf_op jit(solution)/shard_map/all_to_all | solution.py:338
  145.5 24.5 %collective-permute-start.3 = (bf16[16,128,256]{2,1,0:T(8,128)(2,1)}, bf16[16,128,256]{2,1,0:T(8,128)(2,1)S(1)}, u32[]{:S(2)}, u32[]{:S(2)}) collective-permute-start(bf16[16,128,256]{2,1,0:T(8,128)(2,1)} %vertical_fwd.13), channel_id=1, source_target_pairs={{0,1},{1,0},{2,3},{3,2},{4,5},{5,4},{6,7},{7,6},{8,9},{9,8},{10,11... | collective-permute-start | bytes 3145736 | tf_op jit(solution)/shard_map/ppermute | solution.py:334
  170.0 1.0 copy-start.19
  182.9 14.8 %copy-start.2 = (bf16[16,16,16,256]{3,2,1,0:T(8,128)(2,1)}, bf16[16,16,16,256]{3,2,1,0:T(8,128)(2,1)S(1)}, u32[]{:S(2)}) copy-start(bf16[16,16,16,256]{3,2,1,0:T(8,128)(2,1)S(1)} %all-to-all-done.by_lat) | copy-start | bytes 6291460
  182.9 52.3 %all-to-all-start.1 = ((bf16[16,16,16,256]{3,2,1,0:T(8,128)(2,1)}), bf16[16,16,16,256]{3,2,1,0:T(8,128)(2,1)}, u32[]{:S(2)}, u32[]{:S(2)}) async-start(bf16[16,16,16,256]{3,2,1,0:T(8,128)(2,1)} %legendre_fwd.6), calls=%async_computation.1 | async-start | bytes 4194304 | tf_op jit(solution)/shard_map/all_to_all | solution.py:338
  197.7 24.6 %collective-permute-start.4 = (bf16[16,128,256]{2,1,0:T(8,128)(2,1)}, bf16[16,128,256]{2,1,0:T(8,128)(2,1)S(1)}, u32[]{:S(2)}, u32[]{:S(2)}) collective-permute-start(bf16[16,128,256]{2,1,0:T(8,128)(2,1)} %vertical_fwd.15), channel_id=1, source_target_pairs={{0,1},{1,0},{2,3},{3,2},{4,5},{5,4},{6,7},{7,6},{8,9},{9,8},{10,11... | collective-permute-start | bytes 3145736 | tf_op jit(solution)/shard_map/ppermute | solution.py:334
  208.9 31.0 %copy-start.15 = (s32[256]{0:T(256)S(1)}, s32[256]{0:T(256)}, u32[]{:S(2)}) copy-start(s32[256]{0:T(256)} %param.9) | copy-start | bytes 3076
  208.9 31.8 %copy-start.23 = (s32[16]{0:T(128)S(1)}, s32[16]{0:T(128)}, u32[]{:S(2)}) copy-start(s32[16]{0:T(128)} %param.13) | copy-start | bytes 196
  222.3 1.0 copy-start.20
  235.2 52.2 %all-to-all-start.2 = ((bf16[16,16,16,256]{3,2,1,0:T(8,128)(2,1)}), bf16[16,16,16,256]{3,2,1,0:T(8,128)(2,1)S(1)}, u32[]{:S(2)}, u32[]{:S(2)}) async-start(bf16[16,16,16,256]{3,2,1,0:T(8,128)(2,1)} %legendre_fwd.7), calls=%async_computation.2 | async-start | bytes 4194304 | tf_op jit(solution)/shard_map/all_to_all | solution.py:338
  287.4 4.8 copy-start.3
  287.4 53.1 %all-to-all-start.9 = ((bf16[16,16,16,256]{3,2,1,0:T(8,128)(2,1)}), bf16[16,16,16,256]{3,2,1,0:T(8,128)(2,1)}, u32[]{:S(2)}, u32[]{:S(2)}) async-start(bf16[16,16,16,256]{3,2,1,0:T(8,128)(2,1)} %get-tuple-element.39), calls=%async_computation.9 | async-start | bytes 4194304 | tf_op jit(solution)/shard_map/all_to_all | solution.py:338
  340.5 60.5 %copy-start.6 = (bf16[16,16,16,256]{3,2,1,0:T(8,128)(2,1)S(1)}, bf16[16,16,16,256]{3,2,1,0:T(8,128)(2,1)}, u32[]{:S(2)}) copy-start(bf16[16,16,16,256]{3,2,1,0:T(8,128)(2,1)} %get-tuple-element.36) | copy-start | bytes 6291460
  453.0 52.7 %all-to-all-start.7 = ((bf16[16,16,16,256]{3,2,1,0:T(8,128)(2,1)}), bf16[16,16,16,256]{3,2,1,0:T(8,128)(2,1)S(1)}, u32[]{:S(2)}, u32[]{:S(2)}) async-start(bf16[16,16,16,256]{3,2,1,0:T(8,128)(2,1)} %get-tuple-element.33), calls=%async_computation.7 | async-start | bytes 4194304 | tf_op jit(solution)/shard_map/all_to_all | solution.py:338
  464.4 24.5 %collective-permute-start.11 = (bf16[16,128,256]{2,1,0:T(8,128)(2,1)}, bf16[16,128,256]{2,1,0:T(8,128)(2,1)S(1)}, u32[]{:S(2)}, u32[]{:S(2)}) collective-permute-start(bf16[16,128,256]{2,1,0:T(8,128)(2,1)} %get-tuple-element.40), channel_id=1, source_target_pairs={{0,1},{1,0},{2,3},{3,2},{4,5},{5,4},{6,7},{7,6},{8,9},{9,8},{10,11... | collective-permute-start | bytes 3145736 | tf_op jit(solution)/shard_map/ppermute | solution.py:334
  475.7 103.0 %collective-permute-start.7 = (bf16[8,128,256]{2,1,0:T(8,128)(2,1)}, bf16[8,128,256]{2,1,0:T(8,128)(2,1)S(1)}, u32[]{:S(2)}, u32[]{:S(2)}) collective-permute-start(bf16[8,128,256]{2,1,0:T(8,128)(2,1)} %get-tuple-element.29), channel_id=1, source_target_pairs={{0,1},{1,0},{2,3},{3,2},{4,5},{5,4},{6,7},{7,6},{8,9},{9,8},{10,11... | collective-permute-start | bytes 1572872 | tf_op jit(solution)/shard_map/ppermute | solution.py:334
  479.2 89.5 %collective-permute-start.8 = (bf16[8,128,256]{2,1,0:T(8,128)(2,1)}, bf16[8,128,256]{2,1,0:T(8,128)(2,1)S(1)}, u32[]{:S(2)}, u32[]{:S(2)}) collective-permute-start(bf16[8,128,256]{2,1,0:T(8,128)(2,1)} %get-tuple-element.31), channel_id=1, source_target_pairs={{0,1},{1,0},{2,3},{3,2},{4,5},{5,4},{6,7},{7,6},{8,9},{9,8},{10,11... | collective-permute-start | bytes 1572872 | tf_op jit(solution)/shard_map/ppermute | solution.py:334
  486.7 47.2 %collective-permute-start.10 = (bf16[16,128,256]{2,1,0:T(8,128)(2,1)}, bf16[16,128,256]{2,1,0:T(8,128)(2,1)}, u32[]{:S(2)}, u32[]{:S(2)}) collective-permute-start(bf16[16,128,256]{2,1,0:T(8,128)(2,1)} %get-tuple-element.37), channel_id=1, source_target_pairs={{0,1},{1,0},{2,3},{3,2},{4,5},{5,4},{6,7},{7,6},{8,9},{9,8},{10,11... | collective-permute-start | bytes 3145736 | tf_op jit(solution)/shard_map/ppermute | solution.py:334
  488.9 1.0 copy-start.16
  505.7 1.4 copy-start.5
  513.4 42.9 %collective-permute-start.9 = (bf16[16,128,256]{2,1,0:T(8,128)(2,1)}, bf16[16,128,256]{2,1,0:T(8,128)(2,1)S(1)}, u32[]{:S(2)}, u32[]{:S(2)}) collective-permute-start(bf16[16,128,256]{2,1,0:T(8,128)(2,1)} %get-tuple-element.34), channel_id=1, source_target_pairs={{0,1},{1,0},{2,3},{3,2},{4,5},{5,4},{6,7},{7,6},{8,9},{9,8},{10,11... | collective-permute-start | bytes 3145736 | tf_op jit(solution)/shard_map/ppermute | solution.py:334
  556.4 1.0 copy-start.17
  568.7 0.8 copy-start.9
  578.7 0.8 copy-start.8
  579.5 4.7 copy-start.1

commit v3 on v2

--- a/solution.py
+++ b/solution.py
@@ -16,6 +16,8 @@
 COV_BANDS = 4
 LANES = 128
 STEP = 4
+NEAR = 4
+
 
 BF16 = jnp.bfloat16
 F32 = jnp.float32
@@ -148,90 +150,118 @@
     )(*operands)
 
 
-def legendre_fwd_body(lo, lx, own, recv, out, scratch):
-    groups, lats, slots, width = out.shape
+def legendre_fwd_body(info, lo, lx, own, recv, *rest):
+    outs, scratch = rest[:-1], rest[-1]
+    inner, lats, slots, width = outs[0].shape
+    far = len(outs)
     step = own.shape[0]
     for i in range(step):
         slot = pl.program_id(0) * step + i
         total = dot(lo[i], own[i], ((0,), (0,))) + dot(lx[i], recv[i], ((0,), (0,)))
         for tile in range(width // LANES):
-            scratch[tile, pl.ds(slot, groups * lats, stride=slots), :] = total[:, tile * LANES : (tile + 1) * LANES]
+            scratch[tile, pl.ds(slot, far * inner * lats, stride=slots), :] = total[
+                :, tile * LANES : (tile + 1) * LANES
+            ]
 
     @pl.when(pl.program_id(0) == slots // step - 1)
     def _():
-        @pl.loop(0, groups)
-        def _(group):
-            start = pl.multiple_of(group * lats * slots, lats * slots)
-            for tile in range(width // LANES):
-                rows = scratch[tile, pl.ds(start, lats * slots), :]
-                out[group, :, :, tile * LANES : (tile + 1) * LANES] = rows.astype(BF16).reshape(lats, slots, LANES)
-
-
-def legendre_fwd(leg_own, leg_other, own, recv, groups, first_slot):
+        for shift, out in enumerate(outs):
+            base = (info[1] + shift) % far * inner
+
+            @pl.loop(0, inner)
+            def _(near):
+                start = pl.multiple_of((base + near) * lats * slots, lats * slots)
+                for tile in range(width // LANES):
+                    rows = scratch[tile, pl.ds(start, lats * slots), :]
+                    out[near, :, :, tile * LANES : (tile + 1) * LANES] = rows.astype(BF16).reshape(
+                        lats, slots, LANES
+                    )
+
+
+def legendre_fwd(leg_own, leg_other, own, recv, info, far, inner, first_slot):
     slots, rows_dev, width = own.shape
     latitudes = leg_own.shape[2]
     step = STEP if slots % STEP == 0 else 1
     first = first_slot // step
-    lats = latitudes // groups
-    row = pl.BlockSpec((step, rows_dev, latitudes), lambda s: (first + s, 0, 0))
-    other_row = pl.BlockSpec((step, rows_dev, latitudes), lambda s: (s, 0, 0))
-    col = pl.BlockSpec((step, rows_dev, width), lambda s: (s, 0, 0))
-    shape = (groups, lats, slots, width)
+    lats = latitudes // (far * inner)
+    shape = (inner, lats, slots, width)
     return pl.pallas_call(
         legendre_fwd_body,
-        grid=(slots // step,),
-        in_specs=[row, other_row, col, col],
-        out_specs=pl.BlockSpec(shape, lambda s: (0, 0, 0, 0)),
-        out_shape=jax.ShapeDtypeStruct(shape, BF16),
-        scratch_shapes=[pltpu.VMEM((width // LANES, latitudes * slots, LANES), F32)],
+        grid_spec=pltpu.PrefetchScalarGridSpec(
+            num_scalar_prefetch=1,
+            grid=(slots // step,),
+            in_specs=[
+                pl.BlockSpec((step, rows_dev, latitudes), lambda s, info: (first + s, 0, 0)),
+                pl.BlockSpec((step, rows_dev, latitudes), lambda s, info: (s, 0, 0)),
+                pl.BlockSpec((step, rows_dev, width), lambda s, info: (s, 0, 0)),
+                pl.BlockSpec((step, rows_dev, width), lambda s, info: (s, 0, 0)),
+            ],
+            out_specs=[pl.BlockSpec(shape, lambda s, info: (0, 0, 0, 0)) for _ in range(far)],
+            scratch_shapes=[pltpu.VMEM((width // LANES, latitudes * slots, LANES), F32)],
+        ),
+        out_shape=[jax.ShapeDtypeStruct(shape, BF16) for _ in range(far)],
         compiler_params=params("arbitrary"),
         cost_estimate=cost(16 * slots * rows_dev * latitudes * width, 8 * slots * rows_dev * width),
         name="legendre_fwd",
-    )(leg_own, leg_other, own, recv)
-
-
-def legendre_adj_body(lo, lx, band, own, send, scratch):
-    groups, lats, slots, width = band.shape
+    )(info, leg_own, leg_other, own, recv)
+
+
+def legendre_adj_body(info, lo, lx, *rest):
+    bands, (own, send, scratch) = rest[:-3], rest[-3:]
+    inner, lats, slots, width = bands[0].shape
+    far = len(bands)
     step = own.shape[0]
 
     @pl.when(pl.program_id(0) == 0)
     def _():
-        @pl.loop(0, groups)
-        def _(group):
-            start = pl.multiple_of(group * lats * slots, lats * slots)
-            for tile in range(width // LANES):
-                rows = band[group, :, :, tile * LANES : (tile + 1) * LANES].reshape(lats * slots, LANES)
-                scratch[tile, pl.ds(start, lats * slots), :] = rows.astype(F32)
+        for shift, band in enumerate(bands):
+            base = (info[1] + shift) % far * inner
+
+            @pl.loop(0, inner)
+            def _(near):
+                start = pl.multiple_of((base + near) * lats * slots, lats * slots)
+                for tile in range(width // LANES):
+                    rows = band[near, :, :, tile * LANES : (tile + 1) * LANES].reshape(lats * slots, LANES)
+                    scratch[tile, pl.ds(start, lats * slots), :] = rows.astype(F32)
 
     for i in range(step):
         slot = pl.program_id(0) * step + i
         rows = jnp.concatenate(
-            [scratch[tile, pl.ds(slot, groups * lats, stride=slots), :] for tile in range(width // LANES)], axis=1
+            [
+                scratch[tile, pl.ds(slot, far * inner * lats, stride=slots), :]
+                for tile in range(width // LANES)
+            ],
+            axis=1,
         ).astype(BF16)
         own[i] = dot(lo[i], rows, ((1,), (0,))).astype(BF16)
         send[i] = dot(lx[i], rows, ((1,), (0,))).astype(BF16)
 
 
-def legendre_adj(leg_own, leg_other, band_rows, first_slot):
+def legendre_adj(leg_own, leg_other, bands, info, first_slot):
     _, rows_dev, latitudes = leg_own.shape
-    slots, width = band_rows.shape[2:]
+    slots, width = bands[0].shape[2:]
     step = STEP if slots % STEP == 0 else 1
     first = first_slot // step
-    row = pl.BlockSpec((step, rows_dev, latitudes), lambda s: (first + s, 0, 0))
-    other_row = pl.BlockSpec((step, rows_dev, latitudes), lambda s: (s, 0, 0))
-    col = pl.BlockSpec((step, rows_dev, width), lambda s: (s, 0, 0))
+    col = pl.BlockSpec((step, rows_dev, width), lambda s, info: (s, 0, 0))
     shape = jax.ShapeDtypeStruct((slots, rows_dev, width), BF16)
     return pl.pallas_call(
         legendre_adj_body,
-        grid=(slots // step,),
-        in_specs=[row, other_row, pl.BlockSpec(band_rows.shape, lambda s: (0, 0, 0, 0))],
-        out_specs=[col, col],
+        grid_spec=pltpu.PrefetchScalarGridSpec(
+            num_scalar_prefetch=1,
+            grid=(slots // step,),
+            in_specs=[
+                pl.BlockSpec((step, rows_dev, latitudes), lambda s, info: (first + s, 0, 0)),
+                pl.BlockSpec((step, rows_dev, latitudes), lambda s, info: (s, 0, 0)),
+            ]
+            + [pl.BlockSpec(band.shape, lambda s, info: (0, 0, 0, 0)) for band in bands],
+            out_specs=[col, col],
+            scratch_shapes=[pltpu.VMEM((width // LANES, latitudes * slots, LANES), F32)],
+        ),
         out_shape=[shape, shape],
-        scratch_shapes=[pltpu.VMEM((width // LANES, latitudes * slots, LANES), F32)],
         compiler_params=params("arbitrary"),
         cost_estimate=cost(16 * slots * rows_dev * latitudes * width, 8 * slots * rows_dev * width),
         name="legendre_adj",
-    )(leg_own, leg_other, band_rows)
+    )(info, leg_own, leg_other, *bands)
 
 
 def table_body(points, waves, cosine, sine):
@@ -334,19 +364,32 @@
     return lax.ppermute(values, "lev", [(0, 1), (1, 0)])
 
 
-def exchange(values):
-    return lax.all_to_all(values, "wave", split_axis=0, concat_axis=0, tiled=True)
+def near_exchange(values, far, inner):
+    runs = [[i * inner + j for j in range(inner)] for i in range(far)]
+    return lax.all_to_all(values, "wave", split_axis=0, concat_axis=0, axis_index_groups=runs, tiled=True)
+
+
+def far_shift(values, shift, far, inner):
+    count = far * inner
+    return lax.ppermute(values, "wave", [(i, (i + shift * inner) % count) for i in range(count)])
 
 
 def chunked(control, wave_of_slot, legendre, vertical, points, lat_band, grid_scale, obs_weight):
     members, slots, _ = control.shape[:3]
     groups = legendre.shape[2] // points.shape[0]
+    inner = NEAR if groups % NEAR == 0 else 1
+    far = groups // inner
     lats, col_dev, _ = obs_weight.shape
     subs = col_dev // LEVELS
     half = slots // 2
     grid_shape = (members, lats, col_dev, LONGITUDES)
-    info = lax.axis_index("lev").astype(jnp.int32)[None]
-    waves = lax.dynamic_slice_in_dim(wave_of_slot, lax.axis_index("wave") * slots, slots)
+    place = lax.axis_index("wave").astype(jnp.int32)
+    run = place // inner
+    info = jnp.stack([lax.axis_index("lev").astype(jnp.int32), run])
+    waves = lax.dynamic_slice_in_dim(wave_of_slot, place * slots, slots)
+    sources = (run - jnp.arange(far, dtype=jnp.int32)) % far
+    by_run = wave_of_slot.reshape(far, inner, slots)[sources]
+    arrival_waves = jnp.swapaxes(by_run, 0, 1).reshape(-1)
     chooser = (
         lat_band[:, None] == jnp.arange(grid_scale.shape[0], dtype=jnp.int32)[None, :]
     ).astype(F32)
@@ -367,18 +410,20 @@
         recv = swap(sent)
         own = vertical_fwd(control, vertical, info, waves, (member, sub, subs, False), first, count)
         fields.append((own, recv))
-    tables = fourier_tables(points, wave_of_slot)
+    tables = fourier_tables(points, arrival_waves)
     leg_other = jnp.concatenate(leg_parts, axis=0)
 
     arrived = [[] for _ in chunks]
     for (q, first, count), (own, recv) in zip(units_out, fields):
         partner = leg_other if count == slots else leg_parts[first // half]
-        coeffs = legendre_fwd(legendre, partner, own, recv, groups, first)
-        arrived[q].append(exchange(coeffs))
+        pieces = list(legendre_fwd(legendre, partner, own, recv, info, far, inner, first))
+        pieces = pieces[:1] + [far_shift(pieces[r], r, far, inner) for r in range(1, far)]
+        arrived[q].append(near_exchange(jnp.stack(pieces, axis=1), far, inner))
     increment = gradient = None
     adjoints = []
     for q, (member, sub) in enumerate(chunks):
-        by_lat = arrived[q][0] if len(arrived[q]) == 1 else jnp.concatenate(arrived[q], axis=2)
+        by_lat = arrived[q][0] if len(arrived[q]) == 1 else jnp.concatenate(arrived[q], axis=3)
+        by_lat = by_lat.reshape(groups, lats, slots, by_lat.shape[-1])
         increment, adjoint = grid_stage(
             by_lat, tables, lat_scale, obs_weight, member, sub, grid_shape, increment
         )
@@ -386,8 +431,10 @@
     for q, first, count in units_back:
         member, sub = chunks[q]
         partner = leg_other if count == slots else leg_parts[first // half]
-        band_rows = exchange(adjoints[q] if count == slots else adjoints[q][:, :, first : first + count])
-        own, sent = legendre_adj(legendre, partner, band_rows, first)
+        near = adjoints[q] if count == slots else adjoints[q][:, :, first : first + count]
+        near = near_exchange(near.reshape(inner, far, *near.shape[1:]), far, inner)
+        bands = [near[:, 0]] + [far_shift(near[:, r], -r, far, inner) for r in range(1, far)]
+        own, sent = legendre_adj(legendre, partner, bands, info, first)
         recv = swap(sent)
         for block, other in ((own, False), (recv, True)):
             gradient = vertical_adj(

time: 590 us -> 724 us (1.23)
  waiting for transfers between devices: 125 us -> 261 us
  blocking collectives: 113 us -> 33.2 us
  starting transfers between devices: 51.3 us -> 101 us
  local copies, waits for them, and re-layouts: 16.6 us -> 33.4 us
    ppermute x0 -> x30, waiting for transfers between devices: none -> 239 us  [far_shift(): lax.ppermute(values, 'wave', [(i, (i + shift * inner) % count) for i in r...]
    all_to_all x3 -> x2, blocking collectives: 113 us -> 33.2 us  [near_exchange(): lax.all_to_all(values, 'wave', split_axis=0, concat_axis=0, axis_index_gr...]
    ppermute x12, waiting for transfers between devices: 96.5 us -> 22.3 us  [swap(): return lax.ppermute(values, 'lev', [(0, 1), (1, 0)])]
    ppermute x0 -> x30, starting transfers between devices: none -> 52.3 us  [far_shift(): lax.ppermute(values, 'wave', [(i, (i + shift * inner) % count) for i in r...]
    all_to_all x7 -> x8, waiting for transfers between devices: 28.6 us -> 0.02 us  [near_exchange(): lax.all_to_all(values, 'wave', split_axis=0, concat_axis=0, axis_index_gr...]
    squeeze x0 -> x5, local copies, waits for them, and re-layouts: none -> 7.59 us  [chunked(): near[:, r]]
    all_to_all x7 -> x8, starting transfers between devices: 40.5 us -> 36.7 us  [near_exchange(): lax.all_to_all(values, 'wave', split_axis=0, concat_axis=0, axis_index_gr...]
  transfers between devices with their start and end apart: 19 -> 50, of which waited for: 14 -> 22; matrix products, arithmetic and copies ran while one was open for 1% -> 4% of each run, Pallas kernels for 45% -> 38%
where the time goes in v3:
time: 724 us; the launch traced here: 719 us
  Pallas kernels  282 us (39%)
  waiting for transfers between devices  261 us (36%)
  starting transfers between devices  101 us (14%)
  local copies, waits for them, and re-layouts  33.4 us (5%)
  blocking collectives  33.2 us (5%)
    ppermute x30, waiting for transfers between devices, far_shift(): lax.ppermute(values, 'wave', [(i, (i + shift * inner) % count) for i in r...  239 us
    pallas_call x10, Pallas kernels, vertical_fwd(): pl.pallas_call(functools.partial(vertical_fwd_body, first_slot), grid_spe...  85.4 us
    pallas_call x4, Pallas kernels, grid_stage(): pl.pallas_call(grid_body, grid=(lats,), in_specs=in_specs, out_specs=[pl....  62.2 us
    pallas_call x10, Pallas kernels, vertical_adj(): pl.pallas_call(functools.partial(vertical_adj_body, first_slot), grid_spe...  59.1 us
    ppermute x30, starting transfers between devices, far_shift(): lax.ppermute(values, 'wave', [(i, (i + shift * inner) % count) for i in r...  52.3 us
    all_to_all x8, starting transfers between devices, near_exchange(): lax.all_to_all(values, 'wave', split_axis=0, concat_axis=0, axis_index_gr...  36.7 us
    all_to_all x2, blocking collectives, near_exchange(): lax.all_to_all(values, 'wave', split_axis=0, concat_axis=0, axis_index_gr...  33.2 us
    pallas_call x5, Pallas kernels, legendre_adj(): pl.pallas_call(legendre_adj_body, grid_spec=pltpu.PrefetchScalarGridSpec(...  28.7 us
  transfers between devices with their start and end apart: 50, of which 22 were waited for; matrix products, arithmetic and copies ran while one was open for 4% of the time, Pallas kernels for 38%

profile of v3, /device:TPU:13, one launch (start us, length us, event | category | flops | bytes accessed | tf_op | source)
XLA Modules:
  0.0 719.0 jit_solution(16388368878207197547)
XLA Ops:
  2.6 6.2 vertical_fwd.17
  10.0 6.2 vertical_fwd.19
  18.2 10.1 %vertical_fwd.11 = bf16[16,128,256]{2,1,0:T(8,128)(2,1)} custom-call(s32[2]{0:T(128)} %pad_add_fusion.info, s32[16]{0:T(128)} %dynamic_slice.3.waves, bf16[2,16,128,2,512]{4,3,2,1,0:T(2,128)(2,1)} %x.19, bf16[4,4,128,128]{3,2,1,0:T(8,128)(2,1)} %v.39), custom_call_target="tpu_custom_call" | custom-call | flops 8589934592 | bytes 4194304 | tf_op jit(solution)/shard_map/vertical_fwd/pallas_call | solution.py:79
  28.3 6.2 vertical_fwd.18.own
  34.5 9.8 %collective-permute-done.1.lx = bf16[8,128,256]{2,1,0:T(8,128)(2,1)S(1)} collective-permute-done((bf16[8,128,256]{2,1,0:T(8,128)(2,1)S(1)}, bf16[8,128,256]{2,1,0:T(8,128)(2,1)S(1)}, u32[]{:S(2)}, u32[]{:S(2)}) %collective-permute-start.1) | collective-permute-done | bytes 524320 | tf_op jit(solution)/shard_map/ppermute | solution.py:364
  45.1 4.1 legendre_fwd.9
  53.0 6.2 vertical_fwd.16.own
  61.3 4.0 legendre_fwd.8
  71.1 15.5 %collective-permute-done.21 = bf16[4,16,8,256]{3,2,1,0:T(8,128)(2,1)S(1)} collective-permute-done((bf16[4,16,8,256]{3,2,1,0:T(8,128)(2,1)}, bf16[4,16,8,256]{3,2,1,0:T(8,128)(2,1)S(1)}, u32[]{:S(2)}, u32[]{:S(2)}) %collective-permute-start.21) | collective-permute-done | bytes 262176 | tf_op jit(solution)/shard_map/ppermute | solution.py:374
  87.7 4.2 all-to-all-start.4
  91.9 10.2 %vertical_fwd.10.own = bf16[16,128,256]{2,1,0:T(8,128)(2,1)} custom-call(s32[2]{0:T(128)} %pad_add_fusion.info, s32[16]{0:T(128)} %dynamic_slice.3.waves, bf16[2,16,128,2,512]{4,3,2,1,0:T(2,128)(2,1)} %x.19, bf16[4,4,128,128]{3,2,1,0:T(8,128)(2,1)} %v.39), custom_call_target="tpu_custom_call" | custom-call | flops 8589934592 | bytes 4194304 | tf_op jit(solution)/shard_map/vertical_fwd/pallas_call | solution.py:79
  104.2 6.7 legendre_fwd.5
  111.0 4.8 collective-permute-start.4
  115.8 4.1 all-to-all-start.3
  119.9 10.2 %vertical_fwd.13 = bf16[16,128,256]{2,1,0:T(8,128)(2,1)} custom-call(s32[2]{0:T(128)} %pad_add_fusion.info, s32[16]{0:T(128)} %dynamic_slice.3.waves, bf16[2,16,128,2,512]{4,3,2,1,0:T(2,128)(2,1)} %x.19, bf16[4,4,128,128]{3,2,1,0:T(8,128)(2,1)} %v.39), custom_call_target="tpu_custom_call" | custom-call | flops 8589934592 | bytes 4194304 | tf_op jit(solution)/shard_map/vertical_fwd/pallas_call | solution.py:79
  131.3 24.7 %collective-permute-done.4 = bf16[4,16,16,256]{3,2,1,0:T(8,128)(2,1)} collective-permute-done((bf16[4,16,16,256]{3,2,1,0:T(8,128)(2,1)}, bf16[4,16,16,256]{3,2,1,0:T(8,128)(2,1)}, u32[]{:S(2)}, u32[]{:S(2)}) %collective-permute-start.4) | collective-permute-done | bytes 524320 | tf_op jit(solution)/shard_map/ppermute | solution.py:374
  156.0 4.7 collective-permute-done.5
  164.6 4.8 all-to-all-start
  169.4 10.0 %vertical_fwd.12.own = bf16[16,128,256]{2,1,0:T(8,128)(2,1)} custom-call(s32[2]{0:T(128)} %pad_add_fusion.info, s32[16]{0:T(128)} %dynamic_slice.3.waves, bf16[2,16,128,2,512]{4,3,2,1,0:T(2,128)(2,1)} %x.19, bf16[4,4,128,128]{3,2,1,0:T(8,128)(2,1)} %v.39), custom_call_target="tpu_custom_call" | custom-call | flops 8589934592 | bytes 4194304 | tf_op jit(solution)/shard_map/vertical_fwd/pallas_call | solution.py:79
  179.5 6.8 legendre_fwd.6
  187.7 10.1 %vertical_fwd.15 = bf16[16,128,256]{2,1,0:T(8,128)(2,1)} custom-call(s32[2]{0:T(128)} %pad_add_fusion.info, s32[16]{0:T(128)} %dynamic_slice.3.waves, bf16[2,16,128,2,512]{4,3,2,1,0:T(2,128)(2,1)} %x.19, bf16[4,4,128,128]{3,2,1,0:T(8,128)(2,1)} %v.39), custom_call_target="tpu_custom_call" | custom-call | flops 8589934592 | bytes 4194304 | tf_op jit(solution)/shard_map/vertical_fwd/pallas_call | solution.py:79
  199.5 31.9 %collective-permute-done.8 = bf16[4,16,16,256]{3,2,1,0:T(8,128)(2,1)S(1)} collective-permute-done((bf16[4,16,16,256]{3,2,1,0:T(8,128)(2,1)}, bf16[4,16,16,256]{3,2,1,0:T(8,128)(2,1)S(1)}, u32[]{:S(2)}, u32[]{:S(2)}) %collective-permute-start.8) | collective-permute-done | bytes 524320 | tf_op jit(solution)/shard_map/ppermute | solution.py:374
  234.6 5.4 all-to-all-start.1
  240.0 10.0 %vertical_fwd.14.own = bf16[16,128,256]{2,1,0:T(8,128)(2,1)} custom-call(s32[2]{0:T(128)} %pad_add_fusion.info, s32[16]{0:T(128)} %dynamic_slice.3.waves, bf16[2,16,128,2,512]{4,3,2,1,0:T(2,128)(2,1)} %x.19, bf16[4,4,128,128]{3,2,1,0:T(8,128)(2,1)} %v.39), custom_call_target="tpu_custom_call" | custom-call | flops 8589934592 | bytes 4194304 | tf_op jit(solution)/shard_map/vertical_fwd/pallas_call | solution.py:79
  250.1 6.7 legendre_fwd.7
  261.3 8.8 %collective-permute-done.11 = bf16[4,16,16,256]{3,2,1,0:T(8,128)(2,1)S(1)} collective-permute-done((bf16[4,16,16,256]{3,2,1,0:T(8,128)(2,1)}, bf16[4,16,16,256]{3,2,1,0:T(8,128)(2,1)S(1)}, u32[]{:S(2)}, u32[]{:S(2)}) %collective-permute-start.11) | collective-permute-done | bytes 524320 | tf_op jit(solution)/shard_map/ppermute | solution.py:374
  270.1 31.9 %collective-permute-done.12 = bf16[4,16,16,256]{3,2,1,0:T(8,128)(2,1)S(1)} collective-permute-done((bf16[4,16,16,256]{3,2,1,0:T(8,128)(2,1)}, bf16[4,16,16,256]{3,2,1,0:T(8,128)(2,1)S(1)}, u32[]{:S(2)}, u32[]{:S(2)}) %collective-permute-start.12) | collective-permute-done | bytes 524320 | tf_op jit(solution)/shard_map/ppermute | solution.py:374
  302.0 4.2 collective-permute-done.13
  309.0 4.2 all-to-all-start.2
  316.8 18.1 %fourier_tables.1 = (bf16[16,256,512]{2,1,0:T(8,128)(2,1)}, bf16[16,256,512]{2,1,0:T(8,128)(2,1)}) custom-call(s32[16]{0:T(128)} %points.1, f32[256,1]{1,0:T(8,128)} %convert_element_type.20.waves), custom_call_target="tpu_custom_call" | custom-call | flops 83886080 | bytes 8388608 | tf_op jit(solution)/shard_map/fourier_tables/pallas_call | solution.py:297
  337.7 15.5 %grid_stage.4 = (bf16[2,16,256,512]{3,2,1,0:T(8,128)(2,1)}, bf16[16,16,16,256]{3,2,1,0:T(8,128)(2,1)}) custom-call(bf16[16,16,16,256]{3,2,1,0:T(8,128)(2,1)} %bitcast.120, bf16[16,256,512]{2,1,0:T(8,128)(2,1)} %get-tuple-element.46.cosine, bf16[16,256,512]{2,1,0:T(8,128)(2,1)} %get-tuple-element.47.sine, f32[16,256,1]{2,1,0:T(8,128)} %copy.51.scale, ...), custom_call_target="tpu_custom_call" | custom-call | flops 2147483648 | bytes 12582912 | tf_op jit(solution)/shard_map/grid_stage/pallas_call | solution.py:347
  354.6 4.5 all-to-all-start.9
  359.1 15.6 %grid_stage.5 = (bf16[2,16,256,512]{3,2,1,0:T(8,128)(2,1)}, bf16[16,16,16,256]{3,2,1,0:T(8,128)(2,1)}) custom-call(bf16[16,16,16,256]{3,2,1,0:T(8,128)(2,1)} %bitcast.119, bf16[16,256,512]{2,1,0:T(8,128)(2,1)} %get-tuple-element.46.cosine, bf16[16,256,512]{2,1,0:T(8,128)(2,1)} %get-tuple-element.47.sine, ...), custom_call_target="tpu_custom_call", output_to_operand_aliasing={{0}: (5, {})} | custom-call | flops 2147483648 | bytes 12582912 | tf_op jit(solution)/shard_map/grid_stage/pallas_call | solution.py:347
  374.6 15.5 %grid_stage.6 = (bf16[2,16,256,512]{3,2,1,0:T(8,128)(2,1)}, bf16[16,16,16,256]{3,2,1,0:T(8,128)(2,1)}) custom-call(bf16[16,16,16,256]{3,2,1,0:T(8,128)(2,1)} %bitcast.14.by_lat, bf16[16,256,512]{2,1,0:T(8,128)(2,1)} %get-tuple-element.46.cosine, bf16[16,256,512]{2,1,0:T(8,128)(2,1)} %get-tuple-element.47.sine, ...), custom_call_target="tpu_custom_call", output_to_operand_aliasing={{0}: (5, {})} | custom-call | flops 2147483648 | bytes 12582912 | tf_op jit(solution)/shard_map/grid_stage/pallas_call | solution.py:347
  390.2 15.5 %grid_stage.7 = (bf16[2,16,256,512]{3,2,1,0:T(8,128)(2,1)}, bf16[16,16,16,256]{3,2,1,0:T(8,128)(2,1)}) custom-call(bf16[16,16,16,256]{3,2,1,0:T(8,128)(2,1)} %bitcast.118, bf16[16,256,512]{2,1,0:T(8,128)(2,1)} %get-tuple-element.46.cosine, bf16[16,256,512]{2,1,0:T(8,128)(2,1)} %get-tuple-element.47.sine, ...), custom_call_target="tpu_custom_call", output_to_operand_aliasing={{0}: (5, {})} | custom-call | flops 2147483648 | bytes 12582912 | tf_op jit(solution)/shard_map/grid_stage/pallas_call | solution.py:347
  407.4 15.7 %all_to_all.50 = bf16[4,4,16,8,256]{4,3,2,1,0:T(8,128)(2,1)S(1)} all-to-all(bf16[4,4,16,8,256]{4,3,2,1,0:T(8,128)(2,1)S(1)} %bitcast.122), channel_id=1, replica_groups={{0,2,4,6},{8,10,12,14},{16,18,20,22},{24,26,28,30},{1,3,5,7},{9,11,13,1..., dimensions={0} | all-to-all | bytes 2097152 | tf_op jit(solution)/shard_map/all_to_all | solution.py:369
  423.1 17.5 %all_to_all.51 = bf16[4,4,16,8,256]{4,3,2,1,0:T(8,128)(2,1)} all-to-all(bf16[4,4,16,8,256]{4,3,2,1,0:T(8,128)(2,1)S(1)} %bitcast.121), channel_id=1, replica_groups={{0,2,4,6},{8,10,12,14},{16,18,20,22},{24,26,28,30},{1,3,5,7},{9,11,13,1..., dimensions={0} | all-to-all | bytes 2097152 | tf_op jit(solution)/shard_map/all_to_all | solution.py:369
  440.6 5.4 all-to-all-start.8
  450.0 11.6 %collective-permute-done.40.rest_3_ = bf16[4,16,16,256]{3,2,1,0:T(8,128)(2,1)S(1)} collective-permute-done((bf16[4,16,16,256]{3,2,1,0:T(8,128)(2,1)S(1)}, bf16[4,16,16,256]{3,2,1,0:T(8,128)(2,1)S(1)}, u32[]{:S(2)}, u32[]{:S(2)}) %collective-permute-start.40) | collective-permute-done | bytes 524320 | tf_op jit(solution)/shard_map/ppermute | solution.py:374
  461.6 31.8 %collective-permute-done.39.rest_2_ = bf16[4,16,16,256]{3,2,1,0:T(8,128)(2,1)S(1)} collective-permute-done((bf16[4,16,16,256]{3,2,1,0:T(8,128)(2,1)S(1)}, bf16[4,16,16,256]{3,2,1,0:T(8,128)(2,1)S(1)}, u32[]{:S(2)}, u32[]{:S(2)}) %collective-permute-start.39) | collective-permute-done | bytes 524320 | tf_op jit(solution)/shard_map/ppermute | solution.py:374
  494.8 6.9 legendre_adj.9
  503.0 4.1 all-to-all-start.7
  519.2 7.0 collective-permute-done.27.rest_2_
  526.1 16.7 %collective-permute-start.26 = (bf16[4,16,8,256]{3,2,1,0:T(8,128)(2,1)S(1)}, bf16[4,16,8,256]{3,2,1,0:T(8,128)(2,1)S(1)}, u32[]{:S(2)}, u32[]{:S(2)}) collective-permute-start(bf16[4,16,8,256]{3,2,1,0:T(8,128)(2,1)S(1)} %get-tuple-element.98), channel_id=1, source_target_pairs={{0,24},{2,26},{4,28},{6,30},{8,0},{10,2},{12,4},{14,6},{16,8},{18,... | collective-permute-start | bytes 786440 | tf_op jit(solution)/shard_map/ppermute | solution.py:374
  545.2 9.1 %collective-permute-done.23.rest_2_ = bf16[4,16,8,256]{3,2,1,0:T(8,128)(2,1)S(1)} collective-permute-done((bf16[4,16,8,256]{3,2,1,0:T(8,128)(2,1)S(1)}, bf16[4,16,8,256]{3,2,1,0:T(8,128)(2,1)S(1)}, u32[]{:S(2)}, u32[]{:S(2)}) %collective-permute-start.23) | collective-permute-done | bytes 262176 | tf_op jit(solution)/shard_map/ppermute | solution.py:374
  557.4 18.0 %collective-permute-done.22.rest_1_ = bf16[4,16,8,256]{3,2,1,0:T(8,128)(2,1)S(1)} collective-permute-done((bf16[4,16,8,256]{3,2,1,0:T(8,128)(2,1)S(1)}, bf16[4,16,8,256]{3,2,1,0:T(8,128)(2,1)S(1)}, u32[]{:S(2)}, u32[]{:S(2)}) %collective-permute-start.22) | collective-permute-done | bytes 262176 | tf_op jit(solution)/shard_map/ppermute | solution.py:374
  575.4 6.8 vertical_adj.10.rest_0_
  582.2 4.0 legendre_adj.5
  587.5 3.9 legendre_adj.6
  593.9 5.5 collective-permute-done.35.rest_2_
  602.5 23.7 %collective-permute-done.34.rest_1_ = bf16[4,16,16,256]{3,2,1,0:T(8,128)(2,1)} collective-permute-done((bf16[4,16,16,256]{3,2,1,0:T(8,128)(2,1)S(1)}, bf16[4,16,16,256]{3,2,1,0:T(8,128)(2,1)}, u32[]{:S(2)}, u32[]{:S(2)}) %collective-permute-start.34) | collective-permute-done | bytes 524320 | tf_op jit(solution)/shard_map/ppermute | solution.py:374
  626.1 7.0 legendre_adj.8
  634.4 6.8 vertical_adj.11.rest_0_
  644.2 4.3 collective-permute-done.30.rest_1_
  649.3 6.9 legendre_adj.7
  657.5 6.8 vertical_adj.12.rest_0_
  665.2 6.8 vertical_adj.13.rest_0_
  672.0 6.8 vertical_adj.14.rest_0_
  678.8 12.4 %collective-permute-done.33.block = bf16[16,128,256]{2,1,0:T(8,128)(2,1)S(1)} collective-permute-done((bf16[16,128,256]{2,1,0:T(8,128)(2,1)}, bf16[16,128,256]{2,1,0:T(8,128)(2,1)S(1)}, u32[]{:S(2)}, u32[]{:S(2)}) %collective-permute-start.33) | collective-permute-done | bytes 1048608 | tf_op jit(solution)/shard_map/ppermute | solution.py:364
  692.2 6.8 vertical_adj.15.rest_0_
  699.0 4.6 vertical_adj.16.rest_0_
  704.4 4.6 vertical_adj.17.rest_0_
  709.0 4.6 vertical_adj.18.rest_0_
  714.3 4.7 vertical_adj.19
  (182 shorter events, 90.0 us)
Async XLA Ops:
  0.6 314.1 %copy-start = (f32[8,256]{1,0:T(8,128)S(1)}, f32[8,256]{1,0:T(8,128)}, u32[]{:S(2)}) copy-start(f32[8,256]{1,0:T(8,128)} %param.14) | copy-start | bytes 24580
  8.8 50.4 %collective-permute-start.14 = (bf16[8,128,256]{2,1,0:T(8,128)(2,1)}, bf16[8,128,256]{2,1,0:T(8,128)(2,1)S(1)}, u32[]{:S(2)}, u32[]{:S(2)}) collective-permute-start(bf16[8,128,256]{2,1,0:T(8,128)(2,1)} %vertical_fwd.17), channel_id=1, source_target_pairs={{0,1},{1,0},{2,3},{3,2},{4,5},{5,4},{6,7},{7,6},{8,9},{9,8},{10,11... | collective-permute-start | bytes 1572872 | tf_op jit(solution)/shard_map/ppermute | solution.py:364
  16.2 18.3 %collective-permute-start.18 = (bf16[8,128,256]{2,1,0:T(8,128)(2,1)}, bf16[8,128,256]{2,1,0:T(8,128)(2,1)S(1)}, u32[]{:S(2)}, u32[]{:S(2)}) collective-permute-start(bf16[8,128,256]{2,1,0:T(8,128)(2,1)} %vertical_fwd.19), channel_id=1, source_target_pairs={{0,1},{1,0},{2,3},{3,2},{4,5},{5,4},{6,7},{7,6},{8,9},{9,8},{10,11... | collective-permute-start | bytes 1572872 | tf_op jit(solution)/shard_map/ppermute | solution.py:364
  16.7 27.6 %collective-permute-start.1 = (bf16[8,128,256]{2,1,0:T(8,128)(2,1)S(1)}, bf16[8,128,256]{2,1,0:T(8,128)(2,1)S(1)}, u32[]{:S(2)}, u32[]{:S(2)}) collective-permute-start(bf16[8,128,256]{2,1,0:T(8,128)(2,1)S(1)} %get-tuple-element.104), channel_id=1, source_target_pairs={{0,1},{1,0},{2,3},{3,2},{4,5},{5,4},{6,7},{7,6},{8,9},{9,8},{10,11... | collective-permute-start | bytes 1572872 | tf_op jit(solution)/shard_map/ppermute | solution.py:364
  17.9 42.6 %collective-permute-start = (bf16[8,128,256]{2,1,0:T(8,128)(2,1)S(1)}, bf16[8,128,256]{2,1,0:T(8,128)(2,1)S(1)}, u32[]{:S(2)}, u32[]{:S(2)}) collective-permute-start(bf16[8,128,256]{2,1,0:T(8,128)(2,1)S(1)} %get-tuple-element.105), channel_id=1, source_target_pairs={{0,1},{1,0},{2,3},{3,2},{4,5},{5,4},{6,7},{7,6},{8,9},{9,8},{10,11... | collective-permute-start | bytes 1572872 | tf_op jit(solution)/shard_map/ppermute | solution.py:364
  34.5 9.8 %copy-start.28 = (bf16[8,128,256]{2,1,0:T(8,128)(2,1)}, bf16[8,128,256]{2,1,0:T(8,128)(2,1)S(1)}, u32[]{:S(2)}) copy-start(bf16[8,128,256]{2,1,0:T(8,128)(2,1)S(1)} %collective-permute-done.18.recv) | copy-start | bytes 1572868
  49.2 16.2 %collective-permute-start.19 = (bf16[4,16,8,256]{3,2,1,0:T(8,128)(2,1)}, bf16[4,16,8,256]{3,2,1,0:T(8,128)(2,1)S(1)}, u32[]{:S(2)}, u32[]{:S(2)}) collective-permute-start(bf16[4,16,8,256]{3,2,1,0:T(8,128)(2,1)} %get-tuple-element.61), channel_id=1, source_target_pairs={{0,8},{2,10},{4,12},{6,14},{8,16},{10,18},{12,20},{14,22},{16,24},... | collective-permute-start | bytes 786440 | tf_op jit(solution)/shard_map/ppermute | solution.py:374
  50.5 20.6 %collective-permute-start.20 = (bf16[4,16,8,256]{3,2,1,0:T(8,128)(2,1)}, bf16[4,16,8,256]{3,2,1,0:T(8,128)(2,1)S(1)}, u32[]{:S(2)}, u32[]{:S(2)}) collective-permute-start(bf16[4,16,8,256]{3,2,1,0:T(8,128)(2,1)} %get-tuple-element.62), channel_id=1, source_target_pairs={{0,16},{2,18},{4,20},{6,22},{8,24},{10,26},{12,28},{14,30},{16,0},... | collective-permute-start | bytes 786440 | tf_op jit(solution)/shard_map/ppermute | solution.py:374
  51.5 35.0 %collective-permute-start.21 = (bf16[4,16,8,256]{3,2,1,0:T(8,128)(2,1)}, bf16[4,16,8,256]{3,2,1,0:T(8,128)(2,1)S(1)}, u32[]{:S(2)}, u32[]{:S(2)}) collective-permute-start(bf16[4,16,8,256]{3,2,1,0:T(8,128)(2,1)} %get-tuple-element.63), channel_id=1, source_target_pairs={{0,24},{2,26},{4,28},{6,30},{8,0},{10,2},{12,4},{14,6},{16,8},{18,... | collective-permute-start | bytes 786440 | tf_op jit(solution)/shard_map/ppermute | solution.py:374
  59.2 27.4 %copy-start.17 = (bf16[4,16,8,256]{3,2,1,0:T(8,128)(2,1)S(1)}, bf16[4,16,8,256]{3,2,1,0:T(8,128)(2,1)}, u32[]{:S(2)}) copy-start(bf16[4,16,8,256]{3,2,1,0:T(8,128)(2,1)} %get-tuple-element.60) | copy-start | bytes 786436
  59.2 45.1 %collective-permute-start.2 = (bf16[16,128,256]{2,1,0:T(8,128)(2,1)S(1)}, bf16[16,128,256]{2,1,0:T(8,128)(2,1)}, u32[]{:S(2)}, u32[]{:S(2)}) collective-permute-start(bf16[16,128,256]{2,1,0:T(8,128)(2,1)S(1)} %copy-done.20), channel_id=1, source_target_pairs={{0,1},{1,0},{2,3},{3,2},{4,5},{5,4},{6,7},{7,6},{8,9},{9,8},{10,11... | collective-permute-start | bytes 3145736 | tf_op jit(solution)/shard_map/ppermute | solution.py:364
  65.3 36.9 %collective-permute-start.15 = (bf16[4,16,8,256]{3,2,1,0:T(8,128)(2,1)}, bf16[4,16,8,256]{3,2,1,0:T(8,128)(2,1)S(1)}, u32[]{:S(2)}, u32[]{:S(2)}) collective-permute-start(bf16[4,16,8,256]{3,2,1,0:T(8,128)(2,1)} %get-tuple-element.57), channel_id=1, source_target_pairs={{0,8},{2,10},{4,12},{6,14},{8,16},{10,18},{12,20},{14,22},{16,24},... | collective-permute-start | bytes 786440 | tf_op jit(solution)/shard_map/ppermute | solution.py:374
  65.4 36.9 %collective-permute-start.16 = (bf16[4,16,8,256]{3,2,1,0:T(8,128)(2,1)}, bf16[4,16,8,256]{3,2,1,0:T(8,128)(2,1)S(1)}, u32[]{:S(2)}, u32[]{:S(2)}) collective-permute-start(bf16[4,16,8,256]{3,2,1,0:T(8,128)(2,1)} %get-tuple-element.58), channel_id=1, source_target_pairs={{0,16},{2,18},{4,20},{6,22},{8,24},{10,26},{12,28},{14,30},{16,0},... | collective-permute-start | bytes 786440 | tf_op jit(solution)/shard_map/ppermute | solution.py:374
  71.1 31.2 %collective-permute-start.17 = (bf16[4,16,8,256]{3,2,1,0:T(8,128)(2,1)}, bf16[4,16,8,256]{3,2,1,0:T(8,128)(2,1)S(1)}, u32[]{:S(2)}, u32[]{:S(2)}) collective-permute-start(bf16[4,16,8,256]{3,2,1,0:T(8,128)(2,1)} %get-tuple-element.59), channel_id=1, source_target_pairs={{0,24},{2,26},{4,28},{6,30},{8,0},{10,2},{12,4},{14,6},{16,8},{18,... | collective-permute-start | bytes 786440 | tf_op jit(solution)/shard_map/ppermute | solution.py:374
  87.7 28.1 %all-to-all-start.4 = ((bf16[4,4,16,8,256]{4,3,2,1,0:T(8,128)(2,1)}), bf16[4,4,16,8,256]{4,3,2,1,0:T(8,128)(2,1)S(1)}, u32[]{:S(2)}, u32[]{:S(2)}) async-start(bf16[4,4,16,8,256]{4,3,2,1,0:T(8,128)(2,1)} %copy.47), calls=%async_computation.4 | async-start | bytes 2097152 | tf_op jit(solution)/shard_map/all_to_all | solution.py:369
  91.9 10.2 %copy-start.11 = (bf16[8,128,256]{2,1,0:T(8,128)(2,1)S(1)}, bf16[8,128,256]{2,1,0:T(8,128)(2,1)}, u32[]{:S(2)}) copy-start(bf16[8,128,256]{2,1,0:T(8,128)(2,1)} %copy-done.10) | copy-start | bytes 1572868
  91.9 10.2 %copy-start.13 = (bf16[8,128,256]{2,1,0:T(8,128)(2,1)S(1)}, bf16[8,128,256]{2,1,0:T(8,128)(2,1)}, u32[]{:S(2)}) copy-start(bf16[8,128,256]{2,1,0:T(8,128)(2,1)} %copy-done.12) | copy-start | bytes 1572868
  111.0 20.3 %collective-permute-start.3 = (bf16[4,16,16,256]{3,2,1,0:T(8,128)(2,1)}, bf16[4,16,16,256]{3,2,1,0:T(8,128)(2,1)S(1)}, u32[]{:S(2)}, u32[]{:S(2)}) collective-permute-start(bf16[4,16,16,256]{3,2,1,0:T(8,128)(2,1)} %get-tuple-element.43), channel_id=1, source_target_pairs={{0,8},{2,10},{4,12},{6,14},{8,16},{10,18},{12,20},{14,22},{16,24},... | collective-permute-start | bytes 1572872 | tf_op jit(solution)/shard_map/ppermute | solution.py:374
  111.0 45.0 %collective-permute-start.4 = (bf16[4,16,16,256]{3,2,1,0:T(8,128)(2,1)}, bf16[4,16,16,256]{3,2,1,0:T(8,128)(2,1)}, u32[]{:S(2)}, u32[]{:S(2)}) collective-permute-start(bf16[4,16,16,256]{3,2,1,0:T(8,128)(2,1)} %get-tuple-element.44), channel_id=1, source_target_pairs={{0,16},{2,18},{4,20},{6,22},{8,24},{10,26},{12,28},{14,30},{16,0},... | collective-permute-start | bytes 1572872 | tf_op jit(solution)/shard_map/ppermute | solution.py:374
  115.8 44.8 %collective-permute-start.5 = (bf16[4,16,16,256]{3,2,1,0:T(8,128)(2,1)}, bf16[4,16,16,256]{3,2,1,0:T(8,128)(2,1)}, u32[]{:S(2)}, u32[]{:S(2)}) collective-permute-start(bf16[4,16,16,256]{3,2,1,0:T(8,128)(2,1)} %get-tuple-element.45), channel_id=1, source_target_pairs={{0,24},{2,26},{4,28},{6,30},{8,0},{10,2},{12,4},{14,6},{16,8},{18,... | collective-permute-start | bytes 1572872 | tf_op jit(solution)/shard_map/ppermute | solution.py:374
  115.8 47.8 %all-to-all-start.3 = ((bf16[4,4,16,8,256]{4,3,2,1,0:T(8,128)(2,1)}), bf16[4,4,16,8,256]{4,3,2,1,0:T(8,128)(2,1)S(1)}, u32[]{:S(2)}, u32[]{:S(2)}) async-start(bf16[4,4,16,8,256]{4,3,2,1,0:T(8,128)(2,1)} %copy.46), calls=%async_computation.3 | async-start | bytes 2097152 | tf_op jit(solution)/shard_map/all_to_all | solution.py:369
  119.9 40.7 %copy-start.14 = (bf16[4,16,16,256]{3,2,1,0:T(8,128)(2,1)S(1)}, bf16[4,16,16,256]{3,2,1,0:T(8,128)(2,1)}, u32[]{:S(2)}) copy-start(bf16[4,16,16,256]{3,2,1,0:T(8,128)(2,1)} %get-tuple-element.42) | copy-start | bytes 1572868
  130.1 49.4 %collective-permute-start.6 = (bf16[16,128,256]{2,1,0:T(8,128)(2,1)}, bf16[16,128,256]{2,1,0:T(8,128)(2,1)}, u32[]{:S(2)}, u32[]{:S(2)}) collective-permute-start(bf16[16,128,256]{2,1,0:T(8,128)(2,1)} %vertical_fwd.13), channel_id=1, source_target_pairs={{0,1},{1,0},{2,3},{3,2},{4,5},{5,4},{6,7},{7,6},{8,9},{9,8},{10,11... | collective-permute-start | bytes 3145736 | tf_op jit(solution)/shard_map/ppermute | solution.py:364
  164.6 68.6 %all-to-all-start = ((bf16[4,4,16,16,256]{4,3,2,1,0:T(8,128)(2,1)}), bf16[4,4,16,16,256]{4,3,2,1,0:T(8,128)(2,1)S(1)}, u32[]{:S(2)}, u32[]{:S(2)}) async-start(bf16[4,4,16,16,256]{4,3,2,1,0:T(8,128)(2,1)} %copy.41), calls=%async_computation | async-start | bytes 4194304 | tf_op jit(solution)/shard_map/all_to_all | solution.py:369
  186.2 13.3 %collective-permute-start.7 = (bf16[4,16,16,256]{3,2,1,0:T(8,128)(2,1)}, bf16[4,16,16,256]{3,2,1,0:T(8,128)(2,1)S(1)}, u32[]{:S(2)}, u32[]{:S(2)}) collective-permute-start(bf16[4,16,16,256]{3,2,1,0:T(8,128)(2,1)} %get-tuple-element.49), channel_id=1, source_target_pairs={{0,8},{2,10},{4,12},{6,14},{8,16},{10,18},{12,20},{14,22},{16,24},... | collective-permute-start | bytes 1572872 | tf_op jit(solution)/shard_map/ppermute | solution.py:374
  186.2 45.2 %collective-permute-start.8 = (bf16[4,16,16,256]{3,2,1,0:T(8,128)(2,1)}, bf16[4,16,16,256]{3,2,1,0:T(8,128)(2,1)S(1)}, u32[]{:S(2)}, u32[]{:S(2)}) collective-permute-start(bf16[4,16,16,256]{3,2,1,0:T(8,128)(2,1)} %get-tuple-element.50), channel_id=1, source_target_pairs={{0,16},{2,18},{4,20},{6,22},{8,24},{10,26},{12,28},{14,30},{16,0},... | collective-permute-start | bytes 1572872 | tf_op jit(solution)/shard_map/ppermute | solution.py:374
  186.3 45.2 %copy-start.15 = (bf16[4,16,16,256]{3,2,1,0:T(8,128)(2,1)S(1)}, bf16[4,16,16,256]{3,2,1,0:T(8,128)(2,1)}, u32[]{:S(2)}) copy-start(bf16[4,16,16,256]{3,2,1,0:T(8,128)(2,1)} %get-tuple-element.48) | copy-start | bytes 1572868
  186.3 45.1 %collective-permute-start.9 = (bf16[4,16,16,256]{3,2,1,0:T(8,128)(2,1)}, bf16[4,16,16,256]{3,2,1,0:T(8,128)(2,1)S(1)}, u32[]{:S(2)}, u32[]{:S(2)}) collective-permute-start(bf16[4,16,16,256]{3,2,1,0:T(8,128)(2,1)} %get-tuple-element.51), channel_id=1, source_target_pairs={{0,24},{2,26},{4,28},{6,30},{8,0},{10,2},{12,4},{14,6},{16,8},{18,... | collective-permute-start | bytes 1572872 | tf_op jit(solution)/shard_map/ppermute | solution.py:374
  197.8 52.3 %collective-permute-start.10 = (bf16[16,128,256]{2,1,0:T(8,128)(2,1)}, bf16[16,128,256]{2,1,0:T(8,128)(2,1)}, u32[]{:S(2)}, u32[]{:S(2)}) collective-permute-start(bf16[16,128,256]{2,1,0:T(8,128)(2,1)} %vertical_fwd.15), channel_id=1, source_target_pairs={{0,1},{1,0},{2,3},{3,2},{4,5},{5,4},{6,7},{7,6},{8,9},{9,8},{10,11... | collective-permute-start | bytes 3145736 | tf_op jit(solution)/shard_map/ppermute | solution.py:364
  234.6 74.4 %all-to-all-start.1 = ((bf16[4,4,16,16,256]{4,3,2,1,0:T(8,128)(2,1)}), bf16[4,4,16,16,256]{4,3,2,1,0:T(8,128)(2,1)}, u32[]{:S(2)}, u32[]{:S(2)}) async-start(bf16[4,4,16,16,256]{4,3,2,1,0:T(8,128)(2,1)} %copy.44), calls=%async_computation.1 | async-start | bytes 4194304 | tf_op jit(solution)/shard_map/all_to_all | solution.py:369
  256.8 13.3 %collective-permute-start.11 = (bf16[4,16,16,256]{3,2,1,0:T(8,128)(2,1)}, bf16[4,16,16,256]{3,2,1,0:T(8,128)(2,1)S(1)}, u32[]{:S(2)}, u32[]{:S(2)}) collective-permute-start(bf16[4,16,16,256]{3,2,1,0:T(8,128)(2,1)} %get-tuple-element.53), channel_id=1, source_target_pairs={{0,8},{2,10},{4,12},{6,14},{8,16},{10,18},{12,20},{14,22},{16,24},... | collective-permute-start | bytes 1572872 | tf_op jit(solution)/shard_map/ppermute | solution.py:374
  256.8 45.2 %collective-permute-start.12 = (bf16[4,16,16,256]{3,2,1,0:T(8,128)(2,1)}, bf16[4,16,16,256]{3,2,1,0:T(8,128)(2,1)S(1)}, u32[]{:S(2)}, u32[]{:S(2)}) collective-permute-start(bf16[4,16,16,256]{3,2,1,0:T(8,128)(2,1)} %get-tuple-element.54), channel_id=1, source_target_pairs={{0,16},{2,18},{4,20},{6,22},{8,24},{10,26},{12,28},{14,30},{16,0},... | collective-permute-start | bytes 1572872 | tf_op jit(solution)/shard_map/ppermute | solution.py:374
  259.8 46.3 %collective-permute-start.13 = (bf16[4,16,16,256]{3,2,1,0:T(8,128)(2,1)}, bf16[4,16,16,256]{3,2,1,0:T(8,128)(2,1)S(1)}, u32[]{:S(2)}, u32[]{:S(2)}) collective-permute-start(bf16[4,16,16,256]{3,2,1,0:T(8,128)(2,1)} %get-tuple-element.55), channel_id=1, source_target_pairs={{0,24},{2,26},{4,28},{6,30},{8,0},{10,2},{12,4},{14,6},{16,8},{18,... | collective-permute-start | bytes 1572872 | tf_op jit(solution)/shard_map/ppermute | solution.py:374
  309.0 44.2 %all-to-all-start.2 = ((bf16[4,4,16,16,256]{4,3,2,1,0:T(8,128)(2,1)}), bf16[4,4,16,16,256]{4,3,2,1,0:T(8,128)(2,1)S(1)}, u32[]{:S(2)}, u32[]{:S(2)}) async-start(bf16[4,4,16,16,256]{4,3,2,1,0:T(8,128)(2,1)} %copy.45), calls=%async_computation.2 | async-start | bytes 4194304 | tf_op jit(solution)/shard_map/all_to_all | solution.py:369
  354.6 52.8 %all-to-all-start.9 = ((bf16[4,4,16,16,256]{4,3,2,1,0:T(8,128)(2,1)}), bf16[4,4,16,16,256]{4,3,2,1,0:T(8,128)(2,1)}, u32[]{:S(2)}, u32[]{:S(2)}) async-start(bf16[4,4,16,16,256]{4,3,2,1,0:T(8,128)(2,1)} %bitcast.125), calls=%async_computation.9 | async-start | bytes 4194304 | tf_op jit(solution)/shard_map/all_to_all | solution.py:369
  440.6 61.1 %all-to-all-start.8 = ((bf16[4,4,16,16,256]{4,3,2,1,0:T(8,128)(2,1)}), bf16[4,4,16,16,256]{4,3,2,1,0:T(8,128)(2,1)S(1)}, u32[]{:S(2)}, u32[]{:S(2)}) async-start(bf16[4,4,16,16,256]{4,3,2,1,0:T(8,128)(2,1)} %bitcast.124), calls=%async_computation.8 | async-start | bytes 4194304 | tf_op jit(solution)/shard_map/all_to_all | solution.py:369
  448.5 13.1 %collective-permute-start.40 = (bf16[4,16,16,256]{3,2,1,0:T(8,128)(2,1)S(1)}, bf16[4,16,16,256]{3,2,1,0:T(8,128)(2,1)S(1)}, u32[]{:S(2)}, u32[]{:S(2)}) collective-permute-start(bf16[4,16,16,256]{3,2,1,0:T(8,128)(2,1)S(1)} %get-tuple-element.82), channel_id=1, source_target_pairs={{0,8},{2,10},{4,12},{6,14},{8,16},{10,18},{12,20},{14,22},{16,24},... | collective-permute-start | bytes 1572872 | tf_op jit(solution)/shard_map/ppermute | solution.py:374
  448.5 44.9 %collective-permute-start.39 = (bf16[4,16,16,256]{3,2,1,0:T(8,128)(2,1)S(1)}, bf16[4,16,16,256]{3,2,1,0:T(8,128)(2,1)S(1)}, u32[]{:S(2)}, u32[]{:S(2)}) collective-permute-start(bf16[4,16,16,256]{3,2,1,0:T(8,128)(2,1)S(1)} %get-tuple-element.83), channel_id=1, source_target_pairs={{0,16},{2,18},{4,20},{6,22},{8,24},{10,26},{12,28},{14,30},{16,0},... | collective-permute-start | bytes 1572872 | tf_op jit(solution)/shard_map/ppermute | solution.py:374
  448.5 45.5 %collective-permute-start.38 = (bf16[4,16,16,256]{3,2,1,0:T(8,128)(2,1)S(1)}, bf16[4,16,16,256]{3,2,1,0:T(8,128)(2,1)S(1)}, u32[]{:S(2)}, u32[]{:S(2)}) collective-permute-start(bf16[4,16,16,256]{3,2,1,0:T(8,128)(2,1)S(1)} %get-tuple-element.84), channel_id=1, source_target_pairs={{0,24},{2,26},{4,28},{6,30},{8,0},{10,2},{12,4},{14,6},{16,8},{18,... | collective-permute-start | bytes 1572872 | tf_op jit(solution)/shard_map/ppermute | solution.py:374
  461.6 32.4 %copy-start.29 = (bf16[4,16,16,256]{3,2,1,0:T(8,128)(2,1)}, bf16[4,16,16,256]{3,2,1,0:T(8,128)(2,1)S(1)}, u32[]{:S(2)}) copy-start(bf16[4,16,16,256]{3,2,1,0:T(8,128)(2,1)S(1)} %collective-permute-done.40.rest_3_) | copy-start | bytes 1572868
  503.0 88.4 %all-to-all-start.7 = ((bf16[4,4,16,16,256]{4,3,2,1,0:T(8,128)(2,1)}), bf16[4,4,16,16,256]{4,3,2,1,0:T(8,128)(2,1)S(1)}, u32[]{:S(2)}, u32[]{:S(2)}) async-start(bf16[4,4,16,16,256]{4,3,2,1,0:T(8,128)(2,1)} %bitcast.123), calls=%async_computation.7 | async-start | bytes 4194304 | tf_op jit(solution)/shard_map/all_to_all | solution.py:369
  507.2 9.6 %copy-start.5 = (bf16[4,4,16,16,256]{4,3,2,1,0:T(8,128)(2,1)S(1)}, bf16[4,4,16,16,256]{4,3,2,1,0:T(8,128)(2,1)}, u32[]{:S(2)}) copy-start(bf16[4,4,16,16,256]{4,3,2,1,0:T(8,128)(2,1)} %copy-done.4) | copy-start | bytes 6291460
  509.3 8.7 %collective-permute-start.28 = (bf16[4,16,8,256]{3,2,1,0:T(8,128)(2,1)S(1)}, bf16[4,16,8,256]{3,2,1,0:T(8,128)(2,1)S(1)}, u32[]{:S(2)}, u32[]{:S(2)}) collective-permute-start(bf16[4,16,8,256]{3,2,1,0:T(8,128)(2,1)S(1)} %get-tuple-element.96), channel_id=1, source_target_pairs={{0,8},{2,10},{4,12},{6,14},{8,16},{10,18},{12,20},{14,22},{16,24},... | collective-permute-start | bytes 786440 | tf_op jit(solution)/shard_map/ppermute | solution.py:374
  509.3 16.8 %collective-permute-start.27 = (bf16[4,16,8,256]{3,2,1,0:T(8,128)(2,1)S(1)}, bf16[4,16,8,256]{3,2,1,0:T(8,128)(2,1)S(1)}, u32[]{:S(2)}, u32[]{:S(2)}) collective-permute-start(bf16[4,16,8,256]{3,2,1,0:T(8,128)(2,1)S(1)} %get-tuple-element.97), channel_id=1, source_target_pairs={{0,16},{2,18},{4,20},{6,22},{8,24},{10,26},{12,28},{14,30},{16,0},... | collective-permute-start | bytes 786440 | tf_op jit(solution)/shard_map/ppermute | solution.py:374
  513.2 29.8 %collective-permute-start.24 = (bf16[4,16,8,256]{3,2,1,0:T(8,128)(2,1)S(1)}, bf16[4,16,8,256]{3,2,1,0:T(8,128)(2,1)S(1)}, u32[]{:S(2)}, u32[]{:S(2)}) collective-permute-start(bf16[4,16,8,256]{3,2,1,0:T(8,128)(2,1)S(1)} %get-tuple-element.100), channel_id=1, source_target_pairs={{0,8},{2,10},{4,12},{6,14},{8,16},{10,18},{12,20},{14,22},{16,24},... | collective-permute-start | bytes 786440 | tf_op jit(solution)/shard_map/ppermute | solution.py:374
  513.5 40.8 %collective-permute-start.23 = (bf16[4,16,8,256]{3,2,1,0:T(8,128)(2,1)S(1)}, bf16[4,16,8,256]{3,2,1,0:T(8,128)(2,1)S(1)}, u32[]{:S(2)}, u32[]{:S(2)}) collective-permute-start(bf16[4,16,8,256]{3,2,1,0:T(8,128)(2,1)S(1)} %get-tuple-element.101), channel_id=1, source_target_pairs={{0,16},{2,18},{4,20},{6,22},{8,24},{10,26},{12,28},{14,30},{16,0},... | collective-permute-start | bytes 786440 | tf_op jit(solution)/shard_map/ppermute | solution.py:374
  516.8 58.7 %collective-permute-start.22 = (bf16[4,16,8,256]{3,2,1,0:T(8,128)(2,1)S(1)}, bf16[4,16,8,256]{3,2,1,0:T(8,128)(2,1)S(1)}, u32[]{:S(2)}, u32[]{:S(2)}) collective-permute-start(bf16[4,16,8,256]{3,2,1,0:T(8,128)(2,1)S(1)} %get-tuple-element.102), channel_id=1, source_target_pairs={{0,24},{2,26},{4,28},{6,30},{8,0},{10,2},{12,4},{14,6},{16,8},{18,... | collective-permute-start | bytes 786440 | tf_op jit(solution)/shard_map/ppermute | solution.py:374
  518.0 64.2 %copy-start.32 = (bf16[4,16,8,256]{3,2,1,0:T(8,128)(2,1)}, bf16[4,16,8,256]{3,2,1,0:T(8,128)(2,1)S(1)}, u32[]{:S(2)}) copy-start(bf16[4,16,8,256]{3,2,1,0:T(8,128)(2,1)S(1)} %collective-permute-done.28.rest_3_) | copy-start | bytes 786436
  518.0 115.1 %collective-permute-start.41 = (bf16[16,128,256]{2,1,0:T(8,128)(2,1)}, bf16[16,128,256]{2,1,0:T(8,128)(2,1)}, u32[]{:S(2)}, u32[]{:S(2)}) collective-permute-start(bf16[16,128,256]{2,1,0:T(8,128)(2,1)} %get-tuple-element.80), channel_id=1, source_target_pairs={{0,1},{1,0},{2,3},{3,2},{4,5},{5,4},{6,7},{7,6},{8,9},{9,8},{10,11... | collective-permute-start | bytes 3145736 | tf_op jit(solution)/shard_map/ppermute | solution.py:364
  526.1 56.1 %copy-start.33 = (bf16[4,16,8,256]{3,2,1,0:T(8,128)(2,1)}, bf16[4,16,8,256]{3,2,1,0:T(8,128)(2,1)S(1)}, u32[]{:S(2)}) copy-start(bf16[4,16,8,256]{3,2,1,0:T(8,128)(2,1)S(1)} %collective-permute-done.27.rest_2_) | copy-start | bytes 786436
  526.1 60.0 %collective-permute-start.26 = (bf16[4,16,8,256]{3,2,1,0:T(8,128)(2,1)S(1)}, bf16[4,16,8,256]{3,2,1,0:T(8,128)(2,1)S(1)}, u32[]{:S(2)}, u32[]{:S(2)}) collective-permute-start(bf16[4,16,8,256]{3,2,1,0:T(8,128)(2,1)S(1)} %get-tuple-element.98), channel_id=1, source_target_pairs={{0,24},{2,26},{4,28},{6,30},{8,0},{10,2},{12,4},{14,6},{16,8},{18,... | collective-permute-start | bytes 786440 | tf_op jit(solution)/shard_map/ppermute | solution.py:374
  543.0 39.2 %copy-start.34 = (bf16[4,16,8,256]{3,2,1,0:T(8,128)(2,1)}, bf16[4,16,8,256]{3,2,1,0:T(8,128)(2,1)S(1)}, u32[]{:S(2)}) copy-start(bf16[4,16,8,256]{3,2,1,0:T(8,128)(2,1)S(1)} %collective-permute-done.24.rest_3_) | copy-start | bytes 786436
  543.0 49.4 %collective-permute-start.36 = (bf16[4,16,16,256]{3,2,1,0:T(8,128)(2,1)}, bf16[4,16,16,256]{3,2,1,0:T(8,128)(2,1)}, u32[]{:S(2)}, u32[]{:S(2)}) collective-permute-start(bf16[4,16,16,256]{3,2,1,0:T(8,128)(2,1)} %get-tuple-element.86), channel_id=1, source_target_pairs={{0,8},{2,10},{4,12},{6,14},{8,16},{10,18},{12,20},{14,22},{16,24},... | collective-permute-start | bytes 1572872 | tf_op jit(solution)/shard_map/ppermute | solution.py:374
  554.3 27.9 %copy-start.35 = (bf16[4,16,8,256]{3,2,1,0:T(8,128)(2,1)}, bf16[4,16,8,256]{3,2,1,0:T(8,128)(2,1)S(1)}, u32[]{:S(2)}) copy-start(bf16[4,16,8,256]{3,2,1,0:T(8,128)(2,1)S(1)} %collective-permute-done.23.rest_2_) | copy-start | bytes 786436
  554.3 45.1 %collective-permute-start.35 = (bf16[4,16,16,256]{3,2,1,0:T(8,128)(2,1)}, bf16[4,16,16,256]{3,2,1,0:T(8,128)(2,1)}, u32[]{:S(2)}, u32[]{:S(2)}) collective-permute-start(bf16[4,16,16,256]{3,2,1,0:T(8,128)(2,1)} %get-tuple-element.87), channel_id=1, source_target_pairs={{0,16},{2,18},{4,20},{6,22},{8,24},{10,26},{12,28},{14,30},{16,0},... | collective-permute-start | bytes 1572872 | tf_op jit(solution)/shard_map/ppermute | solution.py:374
  575.4 50.7 %collective-permute-start.34 = (bf16[4,16,16,256]{3,2,1,0:T(8,128)(2,1)S(1)}, bf16[4,16,16,256]{3,2,1,0:T(8,128)(2,1)}, u32[]{:S(2)}, u32[]{:S(2)}) collective-permute-start(bf16[4,16,16,256]{3,2,1,0:T(8,128)(2,1)S(1)} %get-tuple-element.88), channel_id=1, source_target_pairs={{0,24},{2,26},{4,28},{6,30},{8,0},{10,2},{12,4},{14,6},{16,8},{18,... | collective-permute-start | bytes 1572872 | tf_op jit(solution)/shard_map/ppermute | solution.py:374
  586.2 127.3 %collective-permute-start.25 = (bf16[8,128,256]{2,1,0:T(8,128)(2,1)}, bf16[8,128,256]{2,1,0:T(8,128)(2,1)S(1)}, u32[]{:S(2)}, u32[]{:S(2)}) collective-permute-start(bf16[8,128,256]{2,1,0:T(8,128)(2,1)} %get-tuple-element.69), channel_id=1, source_target_pairs={{0,1},{1,0},{2,3},{3,2},{4,5},{5,4},{6,7},{7,6},{8,9},{9,8},{10,11... | collective-permute-start | bytes 1572872 | tf_op jit(solution)/shard_map/ppermute | solution.py:364
  592.4 48.7 %collective-permute-start.32 = (bf16[4,16,16,256]{3,2,1,0:T(8,128)(2,1)S(1)}, bf16[4,16,16,256]{3,2,1,0:T(8,128)(2,1)S(1)}, u32[]{:S(2)}, u32[]{:S(2)}) collective-permute-start(bf16[4,16,16,256]{3,2,1,0:T(8,128)(2,1)S(1)} %get-tuple-element.90), channel_id=1, source_target_pairs={{0,8},{2,10},{4,12},{6,14},{8,16},{10,18},{12,20},{14,22},{16,24},... | collective-permute-start | bytes 1572872 | tf_op jit(solution)/shard_map/ppermute | solution.py:374
  599.4 44.8 %collective-permute-start.31 = (bf16[4,16,16,256]{3,2,1,0:T(8,128)(2,1)S(1)}, bf16[4,16,16,256]{3,2,1,0:T(8,128)(2,1)S(1)}, u32[]{:S(2)}, u32[]{:S(2)}) collective-permute-start(bf16[4,16,16,256]{3,2,1,0:T(8,128)(2,1)S(1)} %get-tuple-element.91), channel_id=1, source_target_pairs={{0,16},{2,18},{4,20},{6,22},{8,24},{10,26},{12,28},{14,30},{16,0},... | collective-permute-start | bytes 1572872 | tf_op jit(solution)/shard_map/ppermute | solution.py:374
  626.1 22.4 %collective-permute-start.30 = (bf16[4,16,16,256]{3,2,1,0:T(8,128)(2,1)S(1)}, bf16[4,16,16,256]{3,2,1,0:T(8,128)(2,1)S(1)}, u32[]{:S(2)}, u32[]{:S(2)}) collective-permute-start(bf16[4,16,16,256]{3,2,1,0:T(8,128)(2,1)S(1)} %get-tuple-element.92), channel_id=1, source_target_pairs={{0,24},{2,26},{4,28},{6,30},{8,0},{10,2},{12,4},{14,6},{16,8},{18,... | collective-permute-start | bytes 1572872 | tf_op jit(solution)/shard_map/ppermute | solution.py:374
  633.1 8.1 %copy-start.23 = (bf16[8,128,256]{2,1,0:T(8,128)(2,1)S(1)}, bf16[8,128,256]{2,1,0:T(8,128)(2,1)}, u32[]{:S(2)}) copy-start(bf16[8,128,256]{2,1,0:T(8,128)(2,1)} %get-tuple-element.71) | copy-start | bytes 1572868
  633.1 31.2 %collective-permute-start.37 = (bf16[16,128,256]{2,1,0:T(8,128)(2,1)}, bf16[16,128,256]{2,1,0:T(8,128)(2,1)S(1)}, u32[]{:S(2)}, u32[]{:S(2)}) collective-permute-start(bf16[16,128,256]{2,1,0:T(8,128)(2,1)} %get-tuple-element.77), channel_id=1, source_target_pairs={{0,1},{1,0},{2,3},{3,2},{4,5},{5,4},{6,7},{7,6},{8,9},{9,8},{10,11... | collective-permute-start | bytes 3145736 | tf_op jit(solution)/shard_map/ppermute | solution.py:364
  641.2 62.4 %collective-permute-start.29 = (bf16[8,128,256]{2,1,0:T(8,128)(2,1)S(1)}, bf16[8,128,256]{2,1,0:T(8,128)(2,1)S(1)}, u32[]{:S(2)}, u32[]{:S(2)}) collective-permute-start(bf16[8,128,256]{2,1,0:T(8,128)(2,1)S(1)} %copy-done.23), channel_id=1, source_target_pairs={{0,1},{1,0},{2,3},{3,2},{4,5},{5,4},{6,7},{7,6},{8,9},{9,8},{10,11... | collective-permute-start | bytes 1572872 | tf_op jit(solution)/shard_map/ppermute | solution.py:364
  656.3 35.0 %collective-permute-start.33 = (bf16[16,128,256]{2,1,0:T(8,128)(2,1)}, bf16[16,128,256]{2,1,0:T(8,128)(2,1)S(1)}, u32[]{:S(2)}, u32[]{:S(2)}) collective-permute-start(bf16[16,128,256]{2,1,0:T(8,128)(2,1)} %get-tuple-element.74), channel_id=1, source_target_pairs={{0,1},{1,0},{2,3},{3,2},{4,5},{5,4},{6,7},{7,6},{8,9},{9,8},{10,11... | collective-permute-start | bytes 3145736 | tf_op jit(solution)/shard_map/ppermute | solution.py:364
  (25 other events, 66.7 us)

commit v4 on v3

--- a/solution.py
+++ b/solution.py
@@ -49,7 +49,7 @@
     return jnp.concatenate([rows * mask for mask in band_masks(rows.shape[0], first_total)], axis=1)
 
 
-def vertical_fwd_body(first_slot, info, waves, x, v, out, scratch):
+def vertical_fwd_body(first_slot, info, waves, x, v, out, dense, scratch):
     step, rows_dev = out.shape[:2]
     matrix = jnp.concatenate([v[band, 0] for band in range(COV_BANDS)], axis=1)
 
@@ -57,8 +57,8 @@
     def _(i):
         slot = first_slot + pl.program_id(0) * step + i
         first_total = waves[slot] + info[0] * rows_dev
-        rows = x[0, i].reshape(2 * rows_dev, LEVELS)
-        scratch[...] = dot(band_rows_of(rows, first_total), matrix, ((1,), (1,)))
+        dense[...] = x[0, i].reshape(2 * rows_dev, LEVELS)
+        scratch[...] = dot(band_rows_of(dense[...], first_total), matrix, ((1,), (1,)))
         for part in range(2):
             out[i, :, part * LEVELS : (part + 1) * LEVELS] = scratch[
                 pl.ds(part, rows_dev, stride=2), :
@@ -88,7 +88,10 @@
                 pl.BlockSpec((COV_BANDS, 1, LEVELS, LEVELS), lambda s, info, w: (0, column(info), 0, 0)),
             ],
             out_specs=pl.BlockSpec((step, rows_dev, 2 * LEVELS), lambda s, info, w: (s, 0, 0)),
-            scratch_shapes=[pltpu.VMEM((2 * rows_dev, LEVELS), F32)],
+            scratch_shapes=[
+                pltpu.VMEM((2 * rows_dev, LEVELS), BF16),
+                pltpu.VMEM((2 * rows_dev, LEVELS), F32),
+            ],
         ),
         out_shape=jax.ShapeDtypeStruct((slots, rows_dev, 2 * LEVELS), BF16),
         compiler_params=params("arbitrary"),

time: 724 us -> 716 us (0.989)
  Pallas kernels: 282 us -> 264 us
  waiting for transfers between devices: 261 us -> 271 us
    pallas_call x10, Pallas kernels: 85.4 us -> 67.7 us  [vertical_fwd(): pl.pallas_call(functools.partial(vertical_fwd_body, first_slot), grid_spe...]
  transfers between devices with their start and end apart: 50 -> 50, of which waited for: 22 -> 23; matrix products, arithmetic and copies ran while one was open for 4% -> 4% of each run, Pallas kernels for 38% -> 36%
where the time goes in v4:
time: 716 us; the launch traced here: 711 us
  waiting for transfers between devices  271 us (38%)
  Pallas kernels  264 us (37%)
  starting transfers between devices  102 us (14%)
  local copies, waits for them, and re-layouts  33.4 us (5%)
  blocking collectives  33.2 us (5%)
    ppermute x30, waiting for transfers between devices, far_shift(): lax.ppermute(values, 'wave', [(i, (i + shift * inner) % count) for i in r...  244 us
    pallas_call x10, Pallas kernels, vertical_fwd(): pl.pallas_call(functools.partial(vertical_fwd_body, first_slot), grid_spe...  67.7 us
    pallas_call x4, Pallas kernels, grid_stage(): pl.pallas_call(grid_body, grid=(lats,), in_specs=in_specs, out_specs=[pl....  62.2 us
    pallas_call x10, Pallas kernels, vertical_adj(): pl.pallas_call(functools.partial(vertical_adj_body, first_slot), grid_spe...  59.1 us
    ppermute x30, starting transfers between devices, far_shift(): lax.ppermute(values, 'wave', [(i, (i + shift * inner) % count) for i in r...  53.1 us
    all_to_all x8, starting transfers between devices, near_exchange(): lax.all_to_all(values, 'wave', split_axis=0, concat_axis=0, axis_index_gr...  36.9 us
    all_to_all x2, blocking collectives, near_exchange(): lax.all_to_all(values, 'wave', split_axis=0, concat_axis=0, axis_index_gr...  33.2 us
    pallas_call x5, Pallas kernels, legendre_adj(): pl.pallas_call(legendre_adj_body, grid_spec=pltpu.PrefetchScalarGridSpec(...  28.7 us
  transfers between devices with their start and end apart: 50, of which 23 were waited for; matrix products, arithmetic and copies ran while one was open for 4% of the time, Pallas kernels for 36%

profile of v4, /device:TPU:13, one launch (start us, length us, event | category | flops | bytes accessed | tf_op | source)
XLA Modules:
  0.0 711.5 jit_solution(5437447400005254055)
XLA Ops:
  2.6 5.1 vertical_fwd.17
  8.9 5.1 vertical_fwd.19
  16.0 7.8 %vertical_fwd.11 = bf16[16,128,256]{2,1,0:T(8,128)(2,1)} custom-call(s32[2]{0:T(128)} %pad_add_fusion.info, s32[16]{0:T(128)} %dynamic_slice.3.waves, bf16[2,16,128,2,512]{4,3,2,1,0:T(2,128)(2,1)} %x.19, bf16[4,4,128,128]{3,2,1,0:T(8,128)(2,1)} %v.39), custom_call_target="tpu_custom_call" | custom-call | flops 8589934592 | bytes 4194304 | tf_op jit(solution)/shard_map/vertical_fwd/pallas_call | solution.py:79
  23.9 5.1 vertical_fwd.18.own
  32.0 11.2 %collective-permute-done.1.lx = bf16[8,128,256]{2,1,0:T(8,128)(2,1)S(1)} collective-permute-done((bf16[8,128,256]{2,1,0:T(8,128)(2,1)S(1)}, bf16[8,128,256]{2,1,0:T(8,128)(2,1)S(1)}, u32[]{:S(2)}, u32[]{:S(2)}) %collective-permute-start.1) | collective-permute-done | bytes 524320 | tf_op jit(solution)/shard_map/ppermute | solution.py:367
  44.0 4.1 legendre_fwd.9
  51.8 5.1 vertical_fwd.16.own
  59.0 4.0 legendre_fwd.8
  70.7 14.8 %collective-permute-done.21 = bf16[4,16,8,256]{3,2,1,0:T(8,128)(2,1)S(1)} collective-permute-done((bf16[4,16,8,256]{3,2,1,0:T(8,128)(2,1)}, bf16[4,16,8,256]{3,2,1,0:T(8,128)(2,1)S(1)}, u32[]{:S(2)}, u32[]{:S(2)}) %collective-permute-start.21) | collective-permute-done | bytes 262176 | tf_op jit(solution)/shard_map/ppermute | solution.py:377
  86.6 4.2 all-to-all-start.4
  90.8 8.0 %vertical_fwd.10.own = bf16[16,128,256]{2,1,0:T(8,128)(2,1)} custom-call(s32[2]{0:T(128)} %pad_add_fusion.info, s32[16]{0:T(128)} %dynamic_slice.3.waves, bf16[2,16,128,2,512]{4,3,2,1,0:T(2,128)(2,1)} %x.19, bf16[4,4,128,128]{3,2,1,0:T(8,128)(2,1)} %v.39), custom_call_target="tpu_custom_call" | custom-call | flops 8589934592 | bytes 4194304 | tf_op jit(solution)/shard_map/vertical_fwd/pallas_call | solution.py:79
  100.9 6.7 legendre_fwd.5
  107.7 4.8 collective-permute-start.4
  112.5 4.1 all-to-all-start.3
  116.6 8.0 %vertical_fwd.13 = bf16[16,128,256]{2,1,0:T(8,128)(2,1)} custom-call(s32[2]{0:T(128)} %pad_add_fusion.info, s32[16]{0:T(128)} %dynamic_slice.3.waves, bf16[2,16,128,2,512]{4,3,2,1,0:T(2,128)(2,1)} %x.19, bf16[4,4,128,128]{3,2,1,0:T(8,128)(2,1)} %v.39), custom_call_target="tpu_custom_call" | custom-call | flops 8589934592 | bytes 4194304 | tf_op jit(solution)/shard_map/vertical_fwd/pallas_call | solution.py:79
  125.7 26.9 %collective-permute-done.4 = bf16[4,16,16,256]{3,2,1,0:T(8,128)(2,1)} collective-permute-done((bf16[4,16,16,256]{3,2,1,0:T(8,128)(2,1)}, bf16[4,16,16,256]{3,2,1,0:T(8,128)(2,1)}, u32[]{:S(2)}, u32[]{:S(2)}) %collective-permute-start.4) | collective-permute-done | bytes 524320 | tf_op jit(solution)/shard_map/ppermute | solution.py:377
  152.6 4.7 collective-permute-done.5
  161.3 4.8 all-to-all-start
  166.1 7.8 %vertical_fwd.12.own = bf16[16,128,256]{2,1,0:T(8,128)(2,1)} custom-call(s32[2]{0:T(128)} %pad_add_fusion.info, s32[16]{0:T(128)} %dynamic_slice.3.waves, bf16[2,16,128,2,512]{4,3,2,1,0:T(2,128)(2,1)} %x.19, bf16[4,4,128,128]{3,2,1,0:T(8,128)(2,1)} %v.39), custom_call_target="tpu_custom_call" | custom-call | flops 8589934592 | bytes 4194304 | tf_op jit(solution)/shard_map/vertical_fwd/pallas_call | solution.py:79
  173.9 6.8 legendre_fwd.6
  182.2 7.8 %vertical_fwd.15 = bf16[16,128,256]{2,1,0:T(8,128)(2,1)} custom-call(s32[2]{0:T(128)} %pad_add_fusion.info, s32[16]{0:T(128)} %dynamic_slice.3.waves, bf16[2,16,128,2,512]{4,3,2,1,0:T(2,128)(2,1)} %x.19, bf16[4,4,128,128]{3,2,1,0:T(8,128)(2,1)} %v.39), custom_call_target="tpu_custom_call" | custom-call | flops 8589934592 | bytes 4194304 | tf_op jit(solution)/shard_map/vertical_fwd/pallas_call | solution.py:79
  194.0 31.9 %collective-permute-done.8 = bf16[4,16,16,256]{3,2,1,0:T(8,128)(2,1)S(1)} collective-permute-done((bf16[4,16,16,256]{3,2,1,0:T(8,128)(2,1)}, bf16[4,16,16,256]{3,2,1,0:T(8,128)(2,1)S(1)}, u32[]{:S(2)}, u32[]{:S(2)}) %collective-permute-start.8) | collective-permute-done | bytes 524320 | tf_op jit(solution)/shard_map/ppermute | solution.py:377
  229.1 5.4 all-to-all-start.1
  234.5 7.8 %vertical_fwd.14.own = bf16[16,128,256]{2,1,0:T(8,128)(2,1)} custom-call(s32[2]{0:T(128)} %pad_add_fusion.info, s32[16]{0:T(128)} %dynamic_slice.3.waves, bf16[2,16,128,2,512]{4,3,2,1,0:T(2,128)(2,1)} %x.19, bf16[4,4,128,128]{3,2,1,0:T(8,128)(2,1)} %v.39), custom_call_target="tpu_custom_call" | custom-call | flops 8589934592 | bytes 4194304 | tf_op jit(solution)/shard_map/vertical_fwd/pallas_call | solution.py:79
  242.3 6.7 legendre_fwd.7
  253.5 8.8 %collective-permute-done.11 = bf16[4,16,16,256]{3,2,1,0:T(8,128)(2,1)S(1)} collective-permute-done((bf16[4,16,16,256]{3,2,1,0:T(8,128)(2,1)}, bf16[4,16,16,256]{3,2,1,0:T(8,128)(2,1)S(1)}, u32[]{:S(2)}, u32[]{:S(2)}) %collective-permute-start.11) | collective-permute-done | bytes 524320 | tf_op jit(solution)/shard_map/ppermute | solution.py:377
  262.4 31.9 %collective-permute-done.12 = bf16[4,16,16,256]{3,2,1,0:T(8,128)(2,1)S(1)} collective-permute-done((bf16[4,16,16,256]{3,2,1,0:T(8,128)(2,1)}, bf16[4,16,16,256]{3,2,1,0:T(8,128)(2,1)S(1)}, u32[]{:S(2)}, u32[]{:S(2)}) %collective-permute-start.12) | collective-permute-done | bytes 524320 | tf_op jit(solution)/shard_map/ppermute | solution.py:377
  294.3 4.2 collective-permute-done.13
  301.3 4.2 all-to-all-start.2
  309.1 18.1 %fourier_tables.1 = (bf16[16,256,512]{2,1,0:T(8,128)(2,1)}, bf16[16,256,512]{2,1,0:T(8,128)(2,1)}) custom-call(s32[16]{0:T(128)} %points.1, f32[256,1]{1,0:T(8,128)} %convert_element_type.20.waves), custom_call_target="tpu_custom_call" | custom-call | flops 83886080 | bytes 8388608 | tf_op jit(solution)/shard_map/fourier_tables/pallas_call | solution.py:300
  330.0 15.5 %grid_stage.4 = (bf16[2,16,256,512]{3,2,1,0:T(8,128)(2,1)}, bf16[16,16,16,256]{3,2,1,0:T(8,128)(2,1)}) custom-call(bf16[16,16,16,256]{3,2,1,0:T(8,128)(2,1)} %bitcast.120, bf16[16,256,512]{2,1,0:T(8,128)(2,1)} %get-tuple-element.46.cosine, bf16[16,256,512]{2,1,0:T(8,128)(2,1)} %get-tuple-element.47.sine, f32[16,256,1]{2,1,0:T(8,128)} %copy.51.scale, ...), custom_call_target="tpu_custom_call" | custom-call | flops 2147483648 | bytes 12582912 | tf_op jit(solution)/shard_map/grid_stage/pallas_call | solution.py:350
  346.8 4.6 all-to-all-start.9
  351.5 15.6 %grid_stage.5 = (bf16[2,16,256,512]{3,2,1,0:T(8,128)(2,1)}, bf16[16,16,16,256]{3,2,1,0:T(8,128)(2,1)}) custom-call(bf16[16,16,16,256]{3,2,1,0:T(8,128)(2,1)} %bitcast.119, bf16[16,256,512]{2,1,0:T(8,128)(2,1)} %get-tuple-element.46.cosine, bf16[16,256,512]{2,1,0:T(8,128)(2,1)} %get-tuple-element.47.sine, ...), custom_call_target="tpu_custom_call", output_to_operand_aliasing={{0}: (5, {})} | custom-call | flops 2147483648 | bytes 12582912 | tf_op jit(solution)/shard_map/grid_stage/pallas_call | solution.py:350
  367.0 15.5 %grid_stage.6 = (bf16[2,16,256,512]{3,2,1,0:T(8,128)(2,1)}, bf16[16,16,16,256]{3,2,1,0:T(8,128)(2,1)}) custom-call(bf16[16,16,16,256]{3,2,1,0:T(8,128)(2,1)} %bitcast.14.by_lat, bf16[16,256,512]{2,1,0:T(8,128)(2,1)} %get-tuple-element.46.cosine, bf16[16,256,512]{2,1,0:T(8,128)(2,1)} %get-tuple-element.47.sine, ...), custom_call_target="tpu_custom_call", output_to_operand_aliasing={{0}: (5, {})} | custom-call | flops 2147483648 | bytes 12582912 | tf_op jit(solution)/shard_map/grid_stage/pallas_call | solution.py:350
  382.6 15.5 %grid_stage.7 = (bf16[2,16,256,512]{3,2,1,0:T(8,128)(2,1)}, bf16[16,16,16,256]{3,2,1,0:T(8,128)(2,1)}) custom-call(bf16[16,16,16,256]{3,2,1,0:T(8,128)(2,1)} %bitcast.118, bf16[16,256,512]{2,1,0:T(8,128)(2,1)} %get-tuple-element.46.cosine, bf16[16,256,512]{2,1,0:T(8,128)(2,1)} %get-tuple-element.47.sine, ...), custom_call_target="tpu_custom_call", output_to_operand_aliasing={{0}: (5, {})} | custom-call | flops 2147483648 | bytes 12582912 | tf_op jit(solution)/shard_map/grid_stage/pallas_call | solution.py:350
  399.8 15.7 %all_to_all.50 = bf16[4,4,16,8,256]{4,3,2,1,0:T(8,128)(2,1)S(1)} all-to-all(bf16[4,4,16,8,256]{4,3,2,1,0:T(8,128)(2,1)S(1)} %bitcast.122), channel_id=1, replica_groups={{0,2,4,6},{8,10,12,14},{16,18,20,22},{24,26,28,30},{1,3,5,7},{9,11,13,1..., dimensions={0} | all-to-all | bytes 2097152 | tf_op jit(solution)/shard_map/all_to_all | solution.py:372
  415.5 17.5 %all_to_all.51 = bf16[4,4,16,8,256]{4,3,2,1,0:T(8,128)(2,1)} all-to-all(bf16[4,4,16,8,256]{4,3,2,1,0:T(8,128)(2,1)S(1)} %bitcast.121), channel_id=1, replica_groups={{0,2,4,6},{8,10,12,14},{16,18,20,22},{24,26,28,30},{1,3,5,7},{9,11,13,1..., dimensions={0} | all-to-all | bytes 2097152 | tf_op jit(solution)/shard_map/all_to_all | solution.py:372
  433.1 5.4 all-to-all-start.8
  442.4 11.6 %collective-permute-done.40.rest_3_ = bf16[4,16,16,256]{3,2,1,0:T(8,128)(2,1)S(1)} collective-permute-done((bf16[4,16,16,256]{3,2,1,0:T(8,128)(2,1)S(1)}, bf16[4,16,16,256]{3,2,1,0:T(8,128)(2,1)S(1)}, u32[]{:S(2)}, u32[]{:S(2)}) %collective-permute-start.40) | collective-permute-done | bytes 524320 | tf_op jit(solution)/shard_map/ppermute | solution.py:377
  454.0 31.8 %collective-permute-done.39.rest_2_ = bf16[4,16,16,256]{3,2,1,0:T(8,128)(2,1)S(1)} collective-permute-done((bf16[4,16,16,256]{3,2,1,0:T(8,128)(2,1)S(1)}, bf16[4,16,16,256]{3,2,1,0:T(8,128)(2,1)S(1)}, u32[]{:S(2)}, u32[]{:S(2)}) %collective-permute-start.39) | collective-permute-done | bytes 524320 | tf_op jit(solution)/shard_map/ppermute | solution.py:377
  487.2 6.9 legendre_adj.9
  495.4 4.1 all-to-all-start.7
  511.6 7.0 collective-permute-done.27.rest_2_
  518.6 16.7 %collective-permute-start.26 = (bf16[4,16,8,256]{3,2,1,0:T(8,128)(2,1)S(1)}, bf16[4,16,8,256]{3,2,1,0:T(8,128)(2,1)S(1)}, u32[]{:S(2)}, u32[]{:S(2)}) collective-permute-start(bf16[4,16,8,256]{3,2,1,0:T(8,128)(2,1)S(1)} %get-tuple-element.98), channel_id=1, source_target_pairs={{0,24},{2,26},{4,28},{6,30},{8,0},{10,2},{12,4},{14,6},{16,8},{18,... | collective-permute-start | bytes 786440 | tf_op jit(solution)/shard_map/ppermute | solution.py:377
  537.6 9.1 %collective-permute-done.23.rest_2_ = bf16[4,16,8,256]{3,2,1,0:T(8,128)(2,1)S(1)} collective-permute-done((bf16[4,16,8,256]{3,2,1,0:T(8,128)(2,1)S(1)}, bf16[4,16,8,256]{3,2,1,0:T(8,128)(2,1)S(1)}, u32[]{:S(2)}, u32[]{:S(2)}) %collective-permute-start.23) | collective-permute-done | bytes 262176 | tf_op jit(solution)/shard_map/ppermute | solution.py:377
  549.8 18.0 %collective-permute-done.22.rest_1_ = bf16[4,16,8,256]{3,2,1,0:T(8,128)(2,1)S(1)} collective-permute-done((bf16[4,16,8,256]{3,2,1,0:T(8,128)(2,1)S(1)}, bf16[4,16,8,256]{3,2,1,0:T(8,128)(2,1)S(1)}, u32[]{:S(2)}, u32[]{:S(2)}) %collective-permute-start.22) | collective-permute-done | bytes 262176 | tf_op jit(solution)/shard_map/ppermute | solution.py:377
  567.8 6.8 vertical_adj.10.rest_0_
  574.7 4.0 legendre_adj.5
  579.9 3.9 legendre_adj.6
  586.3 5.5 collective-permute-done.35.rest_2_
  594.9 23.7 %collective-permute-done.34.rest_1_ = bf16[4,16,16,256]{3,2,1,0:T(8,128)(2,1)} collective-permute-done((bf16[4,16,16,256]{3,2,1,0:T(8,128)(2,1)S(1)}, bf16[4,16,16,256]{3,2,1,0:T(8,128)(2,1)}, u32[]{:S(2)}, u32[]{:S(2)}) %collective-permute-start.34) | collective-permute-done | bytes 524320 | tf_op jit(solution)/shard_map/ppermute | solution.py:377
  618.5 7.0 legendre_adj.8
  626.8 6.8 vertical_adj.11.rest_0_
  636.6 4.3 collective-permute-done.30.rest_1_
  641.7 6.9 legendre_adj.7
  649.9 6.8 vertical_adj.12.rest_0_
  657.6 6.8 vertical_adj.13.rest_0_
  664.4 6.8 vertical_adj.14.rest_0_
  671.2 12.5 %collective-permute-done.33.block = bf16[16,128,256]{2,1,0:T(8,128)(2,1)S(1)} collective-permute-done((bf16[16,128,256]{2,1,0:T(8,128)(2,1)}, bf16[16,128,256]{2,1,0:T(8,128)(2,1)S(1)}, u32[]{:S(2)}, u32[]{:S(2)}) %collective-permute-start.33) | collective-permute-done | bytes 1048608 | tf_op jit(solution)/shard_map/ppermute | solution.py:367
  684.6 6.8 vertical_adj.15.rest_0_
  691.4 4.6 vertical_adj.16.rest_0_
  696.8 4.6 vertical_adj.17.rest_0_
  701.4 4.6 vertical_adj.18.rest_0_
  706.8 4.7 vertical_adj.19
  (182 shorter events, 96.9 us)
Async XLA Ops:
  0.6 306.3 %copy-start = (f32[8,256]{1,0:T(8,128)S(1)}, f32[8,256]{1,0:T(8,128)}, u32[]{:S(2)}) copy-start(f32[8,256]{1,0:T(8,128)} %param.14) | copy-start | bytes 24580
  7.7 49.2 %collective-permute-start.14 = (bf16[8,128,256]{2,1,0:T(8,128)(2,1)}, bf16[8,128,256]{2,1,0:T(8,128)(2,1)S(1)}, u32[]{:S(2)}, u32[]{:S(2)}) collective-permute-start(bf16[8,128,256]{2,1,0:T(8,128)(2,1)} %vertical_fwd.17), channel_id=1, source_target_pairs={{0,1},{1,0},{2,3},{3,2},{4,5},{5,4},{6,7},{7,6},{8,9},{9,8},{10,11... | collective-permute-start | bytes 1572872 | tf_op jit(solution)/shard_map/ppermute | solution.py:367
  14.0 17.9 %collective-permute-start.18 = (bf16[8,128,256]{2,1,0:T(8,128)(2,1)}, bf16[8,128,256]{2,1,0:T(8,128)(2,1)S(1)}, u32[]{:S(2)}, u32[]{:S(2)}) collective-permute-start(bf16[8,128,256]{2,1,0:T(8,128)(2,1)} %vertical_fwd.19), channel_id=1, source_target_pairs={{0,1},{1,0},{2,3},{3,2},{4,5},{5,4},{6,7},{7,6},{8,9},{9,8},{10,11... | collective-permute-start | bytes 1572872 | tf_op jit(solution)/shard_map/ppermute | solution.py:367
  14.5 28.7 %collective-permute-start.1 = (bf16[8,128,256]{2,1,0:T(8,128)(2,1)S(1)}, bf16[8,128,256]{2,1,0:T(8,128)(2,1)S(1)}, u32[]{:S(2)}, u32[]{:S(2)}) collective-permute-start(bf16[8,128,256]{2,1,0:T(8,128)(2,1)S(1)} %get-tuple-element.104), channel_id=1, source_target_pairs={{0,1},{1,0},{2,3},{3,2},{4,5},{5,4},{6,7},{7,6},{8,9},{9,8},{10,11... | collective-permute-start | bytes 1572872 | tf_op jit(solution)/shard_map/ppermute | solution.py:367
  15.6 42.6 %collective-permute-start = (bf16[8,128,256]{2,1,0:T(8,128)(2,1)S(1)}, bf16[8,128,256]{2,1,0:T(8,128)(2,1)S(1)}, u32[]{:S(2)}, u32[]{:S(2)}) collective-permute-start(bf16[8,128,256]{2,1,0:T(8,128)(2,1)S(1)} %get-tuple-element.105), channel_id=1, source_target_pairs={{0,1},{1,0},{2,3},{3,2},{4,5},{5,4},{6,7},{7,6},{8,9},{9,8},{10,11... | collective-permute-start | bytes 1572872 | tf_op jit(solution)/shard_map/ppermute | solution.py:367
  32.0 11.2 %copy-start.28 = (bf16[8,128,256]{2,1,0:T(8,128)(2,1)}, bf16[8,128,256]{2,1,0:T(8,128)(2,1)S(1)}, u32[]{:S(2)}) copy-start(bf16[8,128,256]{2,1,0:T(8,128)(2,1)S(1)} %collective-permute-done.18.recv) | copy-start | bytes 1572868
  48.1 15.1 %collective-permute-start.19 = (bf16[4,16,8,256]{3,2,1,0:T(8,128)(2,1)}, bf16[4,16,8,256]{3,2,1,0:T(8,128)(2,1)S(1)}, u32[]{:S(2)}, u32[]{:S(2)}) collective-permute-start(bf16[4,16,8,256]{3,2,1,0:T(8,128)(2,1)} %get-tuple-element.61), channel_id=1, source_target_pairs={{0,8},{2,10},{4,12},{6,14},{8,16},{10,18},{12,20},{14,22},{16,24},... | collective-permute-start | bytes 786440 | tf_op jit(solution)/shard_map/ppermute | solution.py:377
  49.4 20.5 %collective-permute-start.20 = (bf16[4,16,8,256]{3,2,1,0:T(8,128)(2,1)}, bf16[4,16,8,256]{3,2,1,0:T(8,128)(2,1)S(1)}, u32[]{:S(2)}, u32[]{:S(2)}) collective-permute-start(bf16[4,16,8,256]{3,2,1,0:T(8,128)(2,1)} %get-tuple-element.62), channel_id=1, source_target_pairs={{0,16},{2,18},{4,20},{6,22},{8,24},{10,26},{12,28},{14,30},{16,0},... | collective-permute-start | bytes 786440 | tf_op jit(solution)/shard_map/ppermute | solution.py:377
  50.4 35.0 %collective-permute-start.21 = (bf16[4,16,8,256]{3,2,1,0:T(8,128)(2,1)}, bf16[4,16,8,256]{3,2,1,0:T(8,128)(2,1)S(1)}, u32[]{:S(2)}, u32[]{:S(2)}) collective-permute-start(bf16[4,16,8,256]{3,2,1,0:T(8,128)(2,1)} %get-tuple-element.63), channel_id=1, source_target_pairs={{0,24},{2,26},{4,28},{6,30},{8,0},{10,2},{12,4},{14,6},{16,8},{18,... | collective-permute-start | bytes 786440 | tf_op jit(solution)/shard_map/ppermute | solution.py:377
  56.9 28.5 %copy-start.17 = (bf16[4,16,8,256]{3,2,1,0:T(8,128)(2,1)S(1)}, bf16[4,16,8,256]{3,2,1,0:T(8,128)(2,1)}, u32[]{:S(2)}) copy-start(bf16[4,16,8,256]{3,2,1,0:T(8,128)(2,1)} %get-tuple-element.60) | copy-start | bytes 786436
  57.0 44.0 %collective-permute-start.2 = (bf16[16,128,256]{2,1,0:T(8,128)(2,1)S(1)}, bf16[16,128,256]{2,1,0:T(8,128)(2,1)}, u32[]{:S(2)}, u32[]{:S(2)}) collective-permute-start(bf16[16,128,256]{2,1,0:T(8,128)(2,1)S(1)} %copy-done.20), channel_id=1, source_target_pairs={{0,1},{1,0},{2,3},{3,2},{4,5},{5,4},{6,7},{7,6},{8,9},{9,8},{10,11... | collective-permute-start | bytes 3145736 | tf_op jit(solution)/shard_map/ppermute | solution.py:367
  63.1 35.8 %collective-permute-start.15 = (bf16[4,16,8,256]{3,2,1,0:T(8,128)(2,1)}, bf16[4,16,8,256]{3,2,1,0:T(8,128)(2,1)S(1)}, u32[]{:S(2)}, u32[]{:S(2)}) collective-permute-start(bf16[4,16,8,256]{3,2,1,0:T(8,128)(2,1)} %get-tuple-element.57), channel_id=1, source_target_pairs={{0,8},{2,10},{4,12},{6,14},{8,16},{10,18},{12,20},{14,22},{16,24},... | collective-permute-start | bytes 786440 | tf_op jit(solution)/shard_map/ppermute | solution.py:377
  63.1 35.8 %collective-permute-start.16 = (bf16[4,16,8,256]{3,2,1,0:T(8,128)(2,1)}, bf16[4,16,8,256]{3,2,1,0:T(8,128)(2,1)S(1)}, u32[]{:S(2)}, u32[]{:S(2)}) collective-permute-start(bf16[4,16,8,256]{3,2,1,0:T(8,128)(2,1)} %get-tuple-element.58), channel_id=1, source_target_pairs={{0,16},{2,18},{4,20},{6,22},{8,24},{10,26},{12,28},{14,30},{16,0},... | collective-permute-start | bytes 786440 | tf_op jit(solution)/shard_map/ppermute | solution.py:377
  69.9 29.0 %collective-permute-start.17 = (bf16[4,16,8,256]{3,2,1,0:T(8,128)(2,1)}, bf16[4,16,8,256]{3,2,1,0:T(8,128)(2,1)S(1)}, u32[]{:S(2)}, u32[]{:S(2)}) collective-permute-start(bf16[4,16,8,256]{3,2,1,0:T(8,128)(2,1)} %get-tuple-element.59), channel_id=1, source_target_pairs={{0,24},{2,26},{4,28},{6,30},{8,0},{10,2},{12,4},{14,6},{16,8},{18,... | collective-permute-start | bytes 786440 | tf_op jit(solution)/shard_map/ppermute | solution.py:377
  86.6 25.9 %all-to-all-start.4 = ((bf16[4,4,16,8,256]{4,3,2,1,0:T(8,128)(2,1)}), bf16[4,4,16,8,256]{4,3,2,1,0:T(8,128)(2,1)S(1)}, u32[]{:S(2)}, u32[]{:S(2)}) async-start(bf16[4,4,16,8,256]{4,3,2,1,0:T(8,128)(2,1)} %copy.47), calls=%async_computation.4 | async-start | bytes 2097152 | tf_op jit(solution)/shard_map/all_to_all | solution.py:372
  90.8 8.0 %copy-start.11 = (bf16[8,128,256]{2,1,0:T(8,128)(2,1)S(1)}, bf16[8,128,256]{2,1,0:T(8,128)(2,1)}, u32[]{:S(2)}) copy-start(bf16[8,128,256]{2,1,0:T(8,128)(2,1)} %copy-done.10) | copy-start | bytes 1572868
  90.8 8.0 %copy-start.13 = (bf16[8,128,256]{2,1,0:T(8,128)(2,1)S(1)}, bf16[8,128,256]{2,1,0:T(8,128)(2,1)}, u32[]{:S(2)}) copy-start(bf16[8,128,256]{2,1,0:T(8,128)(2,1)} %copy-done.12) | copy-start | bytes 1572868
  107.6 18.1 %collective-permute-start.3 = (bf16[4,16,16,256]{3,2,1,0:T(8,128)(2,1)}, bf16[4,16,16,256]{3,2,1,0:T(8,128)(2,1)S(1)}, u32[]{:S(2)}, u32[]{:S(2)}) collective-permute-start(bf16[4,16,16,256]{3,2,1,0:T(8,128)(2,1)} %get-tuple-element.43), channel_id=1, source_target_pairs={{0,8},{2,10},{4,12},{6,14},{8,16},{10,18},{12,20},{14,22},{16,24},... | collective-permute-start | bytes 1572872 | tf_op jit(solution)/shard_map/ppermute | solution.py:377
  107.7 45.0 %collective-permute-start.4 = (bf16[4,16,16,256]{3,2,1,0:T(8,128)(2,1)}, bf16[4,16,16,256]{3,2,1,0:T(8,128)(2,1)}, u32[]{:S(2)}, u32[]{:S(2)}) collective-permute-start(bf16[4,16,16,256]{3,2,1,0:T(8,128)(2,1)} %get-tuple-element.44), channel_id=1, source_target_pairs={{0,16},{2,18},{4,20},{6,22},{8,24},{10,26},{12,28},{14,30},{16,0},... | collective-permute-start | bytes 1572872 | tf_op jit(solution)/shard_map/ppermute | solution.py:377
  112.5 44.8 %collective-permute-start.5 = (bf16[4,16,16,256]{3,2,1,0:T(8,128)(2,1)}, bf16[4,16,16,256]{3,2,1,0:T(8,128)(2,1)}, u32[]{:S(2)}, u32[]{:S(2)}) collective-permute-start(bf16[4,16,16,256]{3,2,1,0:T(8,128)(2,1)} %get-tuple-element.45), channel_id=1, source_target_pairs={{0,24},{2,26},{4,28},{6,30},{8,0},{10,2},{12,4},{14,6},{16,8},{18,... | collective-permute-start | bytes 1572872 | tf_op jit(solution)/shard_map/ppermute | solution.py:377
  112.5 47.8 %all-to-all-start.3 = ((bf16[4,4,16,8,256]{4,3,2,1,0:T(8,128)(2,1)}), bf16[4,4,16,8,256]{4,3,2,1,0:T(8,128)(2,1)S(1)}, u32[]{:S(2)}, u32[]{:S(2)}) async-start(bf16[4,4,16,8,256]{4,3,2,1,0:T(8,128)(2,1)} %copy.46), calls=%async_computation.3 | async-start | bytes 2097152 | tf_op jit(solution)/shard_map/all_to_all | solution.py:372
  116.6 40.7 %copy-start.14 = (bf16[4,16,16,256]{3,2,1,0:T(8,128)(2,1)S(1)}, bf16[4,16,16,256]{3,2,1,0:T(8,128)(2,1)}, u32[]{:S(2)}) copy-start(bf16[4,16,16,256]{3,2,1,0:T(8,128)(2,1)} %get-tuple-element.42) | copy-start | bytes 1572868
  124.5 49.4 %collective-permute-start.6 = (bf16[16,128,256]{2,1,0:T(8,128)(2,1)}, bf16[16,128,256]{2,1,0:T(8,128)(2,1)}, u32[]{:S(2)}, u32[]{:S(2)}) collective-permute-start(bf16[16,128,256]{2,1,0:T(8,128)(2,1)} %vertical_fwd.13), channel_id=1, source_target_pairs={{0,1},{1,0},{2,3},{3,2},{4,5},{5,4},{6,7},{7,6},{8,9},{9,8},{10,11... | collective-permute-start | bytes 3145736 | tf_op jit(solution)/shard_map/ppermute | solution.py:367
  161.3 66.4 %all-to-all-start = ((bf16[4,4,16,16,256]{4,3,2,1,0:T(8,128)(2,1)}), bf16[4,4,16,16,256]{4,3,2,1,0:T(8,128)(2,1)S(1)}, u32[]{:S(2)}, u32[]{:S(2)}) async-start(bf16[4,4,16,16,256]{4,3,2,1,0:T(8,128)(2,1)} %copy.41), calls=%async_computation | async-start | bytes 4194304 | tf_op jit(solution)/shard_map/all_to_all | solution.py:372
  180.7 13.3 %collective-permute-start.7 = (bf16[4,16,16,256]{3,2,1,0:T(8,128)(2,1)}, bf16[4,16,16,256]{3,2,1,0:T(8,128)(2,1)S(1)}, u32[]{:S(2)}, u32[]{:S(2)}) collective-permute-start(bf16[4,16,16,256]{3,2,1,0:T(8,128)(2,1)} %get-tuple-element.49), channel_id=1, source_target_pairs={{0,8},{2,10},{4,12},{6,14},{8,16},{10,18},{12,20},{14,22},{16,24},... | collective-permute-start | bytes 1572872 | tf_op jit(solution)/shard_map/ppermute | solution.py:377
  180.7 45.2 %collective-permute-start.8 = (bf16[4,16,16,256]{3,2,1,0:T(8,128)(2,1)}, bf16[4,16,16,256]{3,2,1,0:T(8,128)(2,1)S(1)}, u32[]{:S(2)}, u32[]{:S(2)}) collective-permute-start(bf16[4,16,16,256]{3,2,1,0:T(8,128)(2,1)} %get-tuple-element.50), channel_id=1, source_target_pairs={{0,16},{2,18},{4,20},{6,22},{8,24},{10,26},{12,28},{14,30},{16,0},... | collective-permute-start | bytes 1572872 | tf_op jit(solution)/shard_map/ppermute | solution.py:377
  180.7 45.2 %copy-start.15 = (bf16[4,16,16,256]{3,2,1,0:T(8,128)(2,1)S(1)}, bf16[4,16,16,256]{3,2,1,0:T(8,128)(2,1)}, u32[]{:S(2)}) copy-start(bf16[4,16,16,256]{3,2,1,0:T(8,128)(2,1)} %get-tuple-element.48) | copy-start | bytes 1572868
  180.7 45.1 %collective-permute-start.9 = (bf16[4,16,16,256]{3,2,1,0:T(8,128)(2,1)}, bf16[4,16,16,256]{3,2,1,0:T(8,128)(2,1)S(1)}, u32[]{:S(2)}, u32[]{:S(2)}) collective-permute-start(bf16[4,16,16,256]{3,2,1,0:T(8,128)(2,1)} %get-tuple-element.51), channel_id=1, source_target_pairs={{0,24},{2,26},{4,28},{6,30},{8,0},{10,2},{12,4},{14,6},{16,8},{18,... | collective-permute-start | bytes 1572872 | tf_op jit(solution)/shard_map/ppermute | solution.py:377
  190.0 52.3 %collective-permute-start.10 = (bf16[16,128,256]{2,1,0:T(8,128)(2,1)}, bf16[16,128,256]{2,1,0:T(8,128)(2,1)}, u32[]{:S(2)}, u32[]{:S(2)}) collective-permute-start(bf16[16,128,256]{2,1,0:T(8,128)(2,1)} %vertical_fwd.15), channel_id=1, source_target_pairs={{0,1},{1,0},{2,3},{3,2},{4,5},{5,4},{6,7},{7,6},{8,9},{9,8},{10,11... | collective-permute-start | bytes 3145736 | tf_op jit(solution)/shard_map/ppermute | solution.py:367
  229.1 72.2 %all-to-all-start.1 = ((bf16[4,4,16,16,256]{4,3,2,1,0:T(8,128)(2,1)}), bf16[4,4,16,16,256]{4,3,2,1,0:T(8,128)(2,1)}, u32[]{:S(2)}, u32[]{:S(2)}) async-start(bf16[4,4,16,16,256]{4,3,2,1,0:T(8,128)(2,1)} %copy.44), calls=%async_computation.1 | async-start | bytes 4194304 | tf_op jit(solution)/shard_map/all_to_all | solution.py:372
  249.1 13.3 %collective-permute-start.11 = (bf16[4,16,16,256]{3,2,1,0:T(8,128)(2,1)}, bf16[4,16,16,256]{3,2,1,0:T(8,128)(2,1)S(1)}, u32[]{:S(2)}, u32[]{:S(2)}) collective-permute-start(bf16[4,16,16,256]{3,2,1,0:T(8,128)(2,1)} %get-tuple-element.53), channel_id=1, source_target_pairs={{0,8},{2,10},{4,12},{6,14},{8,16},{10,18},{12,20},{14,22},{16,24},... | collective-permute-start | bytes 1572872 | tf_op jit(solution)/shard_map/ppermute | solution.py:377
  249.1 45.2 %collective-permute-start.12 = (bf16[4,16,16,256]{3,2,1,0:T(8,128)(2,1)}, bf16[4,16,16,256]{3,2,1,0:T(8,128)(2,1)S(1)}, u32[]{:S(2)}, u32[]{:S(2)}) collective-permute-start(bf16[4,16,16,256]{3,2,1,0:T(8,128)(2,1)} %get-tuple-element.54), channel_id=1, source_target_pairs={{0,16},{2,18},{4,20},{6,22},{8,24},{10,26},{12,28},{14,30},{16,0},... | collective-permute-start | bytes 1572872 | tf_op jit(solution)/shard_map/ppermute | solution.py:377
  252.1 46.3 %collective-permute-start.13 = (bf16[4,16,16,256]{3,2,1,0:T(8,128)(2,1)}, bf16[4,16,16,256]{3,2,1,0:T(8,128)(2,1)S(1)}, u32[]{:S(2)}, u32[]{:S(2)}) collective-permute-start(bf16[4,16,16,256]{3,2,1,0:T(8,128)(2,1)} %get-tuple-element.55), channel_id=1, source_target_pairs={{0,24},{2,26},{4,28},{6,30},{8,0},{10,2},{12,4},{14,6},{16,8},{18,... | collective-permute-start | bytes 1572872 | tf_op jit(solution)/shard_map/ppermute | solution.py:377
  301.3 44.2 %all-to-all-start.2 = ((bf16[4,4,16,16,256]{4,3,2,1,0:T(8,128)(2,1)}), bf16[4,4,16,16,256]{4,3,2,1,0:T(8,128)(2,1)S(1)}, u32[]{:S(2)}, u32[]{:S(2)}) async-start(bf16[4,4,16,16,256]{4,3,2,1,0:T(8,128)(2,1)} %copy.45), calls=%async_computation.2 | async-start | bytes 4194304 | tf_op jit(solution)/shard_map/all_to_all | solution.py:372
  346.8 53.0 %all-to-all-start.9 = ((bf16[4,4,16,16,256]{4,3,2,1,0:T(8,128)(2,1)}), bf16[4,4,16,16,256]{4,3,2,1,0:T(8,128)(2,1)}, u32[]{:S(2)}, u32[]{:S(2)}) async-start(bf16[4,4,16,16,256]{4,3,2,1,0:T(8,128)(2,1)} %bitcast.125), calls=%async_computation.9 | async-start | bytes 4194304 | tf_op jit(solution)/shard_map/all_to_all | solution.py:372
  433.1 61.1 %all-to-all-start.8 = ((bf16[4,4,16,16,256]{4,3,2,1,0:T(8,128)(2,1)}), bf16[4,4,16,16,256]{4,3,2,1,0:T(8,128)(2,1)S(1)}, u32[]{:S(2)}, u32[]{:S(2)}) async-start(bf16[4,4,16,16,256]{4,3,2,1,0:T(8,128)(2,1)} %bitcast.124), calls=%async_computation.8 | async-start | bytes 4194304 | tf_op jit(solution)/shard_map/all_to_all | solution.py:372
  440.9 13.1 %collective-permute-start.40 = (bf16[4,16,16,256]{3,2,1,0:T(8,128)(2,1)S(1)}, bf16[4,16,16,256]{3,2,1,0:T(8,128)(2,1)S(1)}, u32[]{:S(2)}, u32[]{:S(2)}) collective-permute-start(bf16[4,16,16,256]{3,2,1,0:T(8,128)(2,1)S(1)} %get-tuple-element.82), channel_id=1, source_target_pairs={{0,8},{2,10},{4,12},{6,14},{8,16},{10,18},{12,20},{14,22},{16,24},... | collective-permute-start | bytes 1572872 | tf_op jit(solution)/shard_map/ppermute | solution.py:377
  440.9 44.9 %collective-permute-start.39 = (bf16[4,16,16,256]{3,2,1,0:T(8,128)(2,1)S(1)}, bf16[4,16,16,256]{3,2,1,0:T(8,128)(2,1)S(1)}, u32[]{:S(2)}, u32[]{:S(2)}) collective-permute-start(bf16[4,16,16,256]{3,2,1,0:T(8,128)(2,1)S(1)} %get-tuple-element.83), channel_id=1, source_target_pairs={{0,16},{2,18},{4,20},{6,22},{8,24},{10,26},{12,28},{14,30},{16,0},... | collective-permute-start | bytes 1572872 | tf_op jit(solution)/shard_map/ppermute | solution.py:377
  440.9 45.5 %collective-permute-start.38 = (bf16[4,16,16,256]{3,2,1,0:T(8,128)(2,1)S(1)}, bf16[4,16,16,256]{3,2,1,0:T(8,128)(2,1)S(1)}, u32[]{:S(2)}, u32[]{:S(2)}) collective-permute-start(bf16[4,16,16,256]{3,2,1,0:T(8,128)(2,1)S(1)} %get-tuple-element.84), channel_id=1, source_target_pairs={{0,24},{2,26},{4,28},{6,30},{8,0},{10,2},{12,4},{14,6},{16,8},{18,... | collective-permute-start | bytes 1572872 | tf_op jit(solution)/shard_map/ppermute | solution.py:377
  454.0 32.4 %copy-start.29 = (bf16[4,16,16,256]{3,2,1,0:T(8,128)(2,1)}, bf16[4,16,16,256]{3,2,1,0:T(8,128)(2,1)S(1)}, u32[]{:S(2)}) copy-start(bf16[4,16,16,256]{3,2,1,0:T(8,128)(2,1)S(1)} %collective-permute-done.40.rest_3_) | copy-start | bytes 1572868
  495.4 88.3 %all-to-all-start.7 = ((bf16[4,4,16,16,256]{4,3,2,1,0:T(8,128)(2,1)}), bf16[4,4,16,16,256]{4,3,2,1,0:T(8,128)(2,1)S(1)}, u32[]{:S(2)}, u32[]{:S(2)}) async-start(bf16[4,4,16,16,256]{4,3,2,1,0:T(8,128)(2,1)} %bitcast.123), calls=%async_computation.7 | async-start | bytes 4194304 | tf_op jit(solution)/shard_map/all_to_all | solution.py:372
  499.6 9.6 %copy-start.5 = (bf16[4,4,16,16,256]{4,3,2,1,0:T(8,128)(2,1)S(1)}, bf16[4,4,16,16,256]{4,3,2,1,0:T(8,128)(2,1)}, u32[]{:S(2)}) copy-start(bf16[4,4,16,16,256]{4,3,2,1,0:T(8,128)(2,1)} %copy-done.4) | copy-start | bytes 6291460
  501.7 8.7 %collective-permute-start.28 = (bf16[4,16,8,256]{3,2,1,0:T(8,128)(2,1)S(1)}, bf16[4,16,8,256]{3,2,1,0:T(8,128)(2,1)S(1)}, u32[]{:S(2)}, u32[]{:S(2)}) collective-permute-start(bf16[4,16,8,256]{3,2,1,0:T(8,128)(2,1)S(1)} %get-tuple-element.96), channel_id=1, source_target_pairs={{0,8},{2,10},{4,12},{6,14},{8,16},{10,18},{12,20},{14,22},{16,24},... | collective-permute-start | bytes 786440 | tf_op jit(solution)/shard_map/ppermute | solution.py:377
  501.7 16.8 %collective-permute-start.27 = (bf16[4,16,8,256]{3,2,1,0:T(8,128)(2,1)S(1)}, bf16[4,16,8,256]{3,2,1,0:T(8,128)(2,1)S(1)}, u32[]{:S(2)}, u32[]{:S(2)}) collective-permute-start(bf16[4,16,8,256]{3,2,1,0:T(8,128)(2,1)S(1)} %get-tuple-element.97), channel_id=1, source_target_pairs={{0,16},{2,18},{4,20},{6,22},{8,24},{10,26},{12,28},{14,30},{16,0},... | collective-permute-start | bytes 786440 | tf_op jit(solution)/shard_map/ppermute | solution.py:377
  505.6 29.8 %collective-permute-start.24 = (bf16[4,16,8,256]{3,2,1,0:T(8,128)(2,1)S(1)}, bf16[4,16,8,256]{3,2,1,0:T(8,128)(2,1)S(1)}, u32[]{:S(2)}, u32[]{:S(2)}) collective-permute-start(bf16[4,16,8,256]{3,2,1,0:T(8,128)(2,1)S(1)} %get-tuple-element.100), channel_id=1, source_target_pairs={{0,8},{2,10},{4,12},{6,14},{8,16},{10,18},{12,20},{14,22},{16,24},... | collective-permute-start | bytes 786440 | tf_op jit(solution)/shard_map/ppermute | solution.py:377
  505.9 40.8 %collective-permute-start.23 = (bf16[4,16,8,256]{3,2,1,0:T(8,128)(2,1)S(1)}, bf16[4,16,8,256]{3,2,1,0:T(8,128)(2,1)S(1)}, u32[]{:S(2)}, u32[]{:S(2)}) collective-permute-start(bf16[4,16,8,256]{3,2,1,0:T(8,128)(2,1)S(1)} %get-tuple-element.101), channel_id=1, source_target_pairs={{0,16},{2,18},{4,20},{6,22},{8,24},{10,26},{12,28},{14,30},{16,0},... | collective-permute-start | bytes 786440 | tf_op jit(solution)/shard_map/ppermute | solution.py:377
  509.2 58.7 %collective-permute-start.22 = (bf16[4,16,8,256]{3,2,1,0:T(8,128)(2,1)S(1)}, bf16[4,16,8,256]{3,2,1,0:T(8,128)(2,1)S(1)}, u32[]{:S(2)}, u32[]{:S(2)}) collective-permute-start(bf16[4,16,8,256]{3,2,1,0:T(8,128)(2,1)S(1)} %get-tuple-element.102), channel_id=1, source_target_pairs={{0,24},{2,26},{4,28},{6,30},{8,0},{10,2},{12,4},{14,6},{16,8},{18,... | collective-permute-start | bytes 786440 | tf_op jit(solution)/shard_map/ppermute | solution.py:377
  510.4 64.2 %copy-start.32 = (bf16[4,16,8,256]{3,2,1,0:T(8,128)(2,1)}, bf16[4,16,8,256]{3,2,1,0:T(8,128)(2,1)S(1)}, u32[]{:S(2)}) copy-start(bf16[4,16,8,256]{3,2,1,0:T(8,128)(2,1)S(1)} %collective-permute-done.28.rest_3_) | copy-start | bytes 786436
  510.4 115.1 %collective-permute-start.41 = (bf16[16,128,256]{2,1,0:T(8,128)(2,1)}, bf16[16,128,256]{2,1,0:T(8,128)(2,1)}, u32[]{:S(2)}, u32[]{:S(2)}) collective-permute-start(bf16[16,128,256]{2,1,0:T(8,128)(2,1)} %get-tuple-element.80), channel_id=1, source_target_pairs={{0,1},{1,0},{2,3},{3,2},{4,5},{5,4},{6,7},{7,6},{8,9},{9,8},{10,11... | collective-permute-start | bytes 3145736 | tf_op jit(solution)/shard_map/ppermute | solution.py:367
  518.6 56.1 %copy-start.33 = (bf16[4,16,8,256]{3,2,1,0:T(8,128)(2,1)}, bf16[4,16,8,256]{3,2,1,0:T(8,128)(2,1)S(1)}, u32[]{:S(2)}) copy-start(bf16[4,16,8,256]{3,2,1,0:T(8,128)(2,1)S(1)} %collective-permute-done.27.rest_2_) | copy-start | bytes 786436
  518.6 60.0 %collective-permute-start.26 = (bf16[4,16,8,256]{3,2,1,0:T(8,128)(2,1)S(1)}, bf16[4,16,8,256]{3,2,1,0:T(8,128)(2,1)S(1)}, u32[]{:S(2)}, u32[]{:S(2)}) collective-permute-start(bf16[4,16,8,256]{3,2,1,0:T(8,128)(2,1)S(1)} %get-tuple-element.98), channel_id=1, source_target_pairs={{0,24},{2,26},{4,28},{6,30},{8,0},{10,2},{12,4},{14,6},{16,8},{18,... | collective-permute-start | bytes 786440 | tf_op jit(solution)/shard_map/ppermute | solution.py:377
  535.4 39.2 %copy-start.34 = (bf16[4,16,8,256]{3,2,1,0:T(8,128)(2,1)}, bf16[4,16,8,256]{3,2,1,0:T(8,128)(2,1)S(1)}, u32[]{:S(2)}) copy-start(bf16[4,16,8,256]{3,2,1,0:T(8,128)(2,1)S(1)} %collective-permute-done.24.rest_3_) | copy-start | bytes 786436
  535.4 49.4 %collective-permute-start.36 = (bf16[4,16,16,256]{3,2,1,0:T(8,128)(2,1)}, bf16[4,16,16,256]{3,2,1,0:T(8,128)(2,1)}, u32[]{:S(2)}, u32[]{:S(2)}) collective-permute-start(bf16[4,16,16,256]{3,2,1,0:T(8,128)(2,1)} %get-tuple-element.86), channel_id=1, source_target_pairs={{0,8},{2,10},{4,12},{6,14},{8,16},{10,18},{12,20},{14,22},{16,24},... | collective-permute-start | bytes 1572872 | tf_op jit(solution)/shard_map/ppermute | solution.py:377
  546.7 27.9 %copy-start.35 = (bf16[4,16,8,256]{3,2,1,0:T(8,128)(2,1)}, bf16[4,16,8,256]{3,2,1,0:T(8,128)(2,1)S(1)}, u32[]{:S(2)}) copy-start(bf16[4,16,8,256]{3,2,1,0:T(8,128)(2,1)S(1)} %collective-permute-done.23.rest_2_) | copy-start | bytes 786436
  546.7 45.1 %collective-permute-start.35 = (bf16[4,16,16,256]{3,2,1,0:T(8,128)(2,1)}, bf16[4,16,16,256]{3,2,1,0:T(8,128)(2,1)}, u32[]{:S(2)}, u32[]{:S(2)}) collective-permute-start(bf16[4,16,16,256]{3,2,1,0:T(8,128)(2,1)} %get-tuple-element.87), channel_id=1, source_target_pairs={{0,16},{2,18},{4,20},{6,22},{8,24},{10,26},{12,28},{14,30},{16,0},... | collective-permute-start | bytes 1572872 | tf_op jit(solution)/shard_map/ppermute | solution.py:377
  567.8 50.7 %collective-permute-start.34 = (bf16[4,16,16,256]{3,2,1,0:T(8,128)(2,1)S(1)}, bf16[4,16,16,256]{3,2,1,0:T(8,128)(2,1)}, u32[]{:S(2)}, u32[]{:S(2)}) collective-permute-start(bf16[4,16,16,256]{3,2,1,0:T(8,128)(2,1)S(1)} %get-tuple-element.88), channel_id=1, source_target_pairs={{0,24},{2,26},{4,28},{6,30},{8,0},{10,2},{12,4},{14,6},{16,8},{18,... | collective-permute-start | bytes 1572872 | tf_op jit(solution)/shard_map/ppermute | solution.py:377
  578.6 127.3 %collective-permute-start.25 = (bf16[8,128,256]{2,1,0:T(8,128)(2,1)}, bf16[8,128,256]{2,1,0:T(8,128)(2,1)S(1)}, u32[]{:S(2)}, u32[]{:S(2)}) collective-permute-start(bf16[8,128,256]{2,1,0:T(8,128)(2,1)} %get-tuple-element.69), channel_id=1, source_target_pairs={{0,1},{1,0},{2,3},{3,2},{4,5},{5,4},{6,7},{7,6},{8,9},{9,8},{10,11... | collective-permute-start | bytes 1572872 | tf_op jit(solution)/shard_map/ppermute | solution.py:367
  584.8 48.7 %collective-permute-start.32 = (bf16[4,16,16,256]{3,2,1,0:T(8,128)(2,1)S(1)}, bf16[4,16,16,256]{3,2,1,0:T(8,128)(2,1)S(1)}, u32[]{:S(2)}, u32[]{:S(2)}) collective-permute-start(bf16[4,16,16,256]{3,2,1,0:T(8,128)(2,1)S(1)} %get-tuple-element.90), channel_id=1, source_target_pairs={{0,8},{2,10},{4,12},{6,14},{8,16},{10,18},{12,20},{14,22},{16,24},... | collective-permute-start | bytes 1572872 | tf_op jit(solution)/shard_map/ppermute | solution.py:377
  591.8 44.8 %collective-permute-start.31 = (bf16[4,16,16,256]{3,2,1,0:T(8,128)(2,1)S(1)}, bf16[4,16,16,256]{3,2,1,0:T(8,128)(2,1)S(1)}, u32[]{:S(2)}, u32[]{:S(2)}) collective-permute-start(bf16[4,16,16,256]{3,2,1,0:T(8,128)(2,1)S(1)} %get-tuple-element.91), channel_id=1, source_target_pairs={{0,16},{2,18},{4,20},{6,22},{8,24},{10,26},{12,28},{14,30},{16,0},... | collective-permute-start | bytes 1572872 | tf_op jit(solution)/shard_map/ppermute | solution.py:377
  618.5 22.4 %collective-permute-start.30 = (bf16[4,16,16,256]{3,2,1,0:T(8,128)(2,1)S(1)}, bf16[4,16,16,256]{3,2,1,0:T(8,128)(2,1)S(1)}, u32[]{:S(2)}, u32[]{:S(2)}) collective-permute-start(bf16[4,16,16,256]{3,2,1,0:T(8,128)(2,1)S(1)} %get-tuple-element.92), channel_id=1, source_target_pairs={{0,24},{2,26},{4,28},{6,30},{8,0},{10,2},{12,4},{14,6},{16,8},{18,... | collective-permute-start | bytes 1572872 | tf_op jit(solution)/shard_map/ppermute | solution.py:377
  625.5 8.0 %copy-start.23 = (bf16[8,128,256]{2,1,0:T(8,128)(2,1)S(1)}, bf16[8,128,256]{2,1,0:T(8,128)(2,1)}, u32[]{:S(2)}) copy-start(bf16[8,128,256]{2,1,0:T(8,128)(2,1)} %get-tuple-element.71) | copy-start | bytes 1572868
  625.5 31.1 %collective-permute-start.37 = (bf16[16,128,256]{2,1,0:T(8,128)(2,1)}, bf16[16,128,256]{2,1,0:T(8,128)(2,1)S(1)}, u32[]{:S(2)}, u32[]{:S(2)}) collective-permute-start(bf16[16,128,256]{2,1,0:T(8,128)(2,1)} %get-tuple-element.77), channel_id=1, source_target_pairs={{0,1},{1,0},{2,3},{3,2},{4,5},{5,4},{6,7},{7,6},{8,9},{9,8},{10,11... | collective-permute-start | bytes 3145736 | tf_op jit(solution)/shard_map/ppermute | solution.py:367
  633.6 62.4 %collective-permute-start.29 = (bf16[8,128,256]{2,1,0:T(8,128)(2,1)S(1)}, bf16[8,128,256]{2,1,0:T(8,128)(2,1)S(1)}, u32[]{:S(2)}, u32[]{:S(2)}) collective-permute-start(bf16[8,128,256]{2,1,0:T(8,128)(2,1)S(1)} %copy-done.23), channel_id=1, source_target_pairs={{0,1},{1,0},{2,3},{3,2},{4,5},{5,4},{6,7},{7,6},{8,9},{9,8},{10,11... | collective-permute-start | bytes 1572872 | tf_op jit(solution)/shard_map/ppermute | solution.py:367
  648.7 35.0 %collective-permute-start.33 = (bf16[16,128,256]{2,1,0:T(8,128)(2,1)}, bf16[16,128,256]{2,1,0:T(8,128)(2,1)S(1)}, u32[]{:S(2)}, u32[]{:S(2)}) collective-permute-start(bf16[16,128,256]{2,1,0:T(8,128)(2,1)} %get-tuple-element.74), channel_id=1, source_target_pairs={{0,1},{1,0},{2,3},{3,2},{4,5},{5,4},{6,7},{7,6},{8,9},{9,8},{10,11... | collective-permute-start | bytes 3145736 | tf_op jit(solution)/shard_map/ppermute | solution.py:367
  (25 other events, 64.5 us)

commit v5 on v4

--- a/solution.py
+++ b/solution.py
@@ -314,32 +314,34 @@
 
 def grid_body(by_lat, cosine, sine, scale, weight, *rest):
     increment, adjoint = rest[-2:]
-    groups, _, slots, width = by_lat.shape
+    groups, step, slots, width = by_lat.shape
     half = width // 2
-    rows = by_lat[:, 0].reshape(groups * slots, width)
-    synthesis = dot(rows[:, :half], cosine[0], ((0,), (0,)))
-    synthesis = synthesis + dot(rows[:, half:], sine[0], ((0,), (0,)))
-    lat_scale = scale[0]
-    inc = (synthesis * lat_scale).astype(BF16)
-    increment[0, 0] = inc
-    weighted = (inc.astype(F32) * weight[0].astype(F32) * lat_scale).astype(BF16)
-    for part, table in ((0, cosine), (1, sine)):
-        total = dot(table[0], weighted, ((1,), (1,))).astype(BF16)
-        adjoint[:, 0, :, part * half : (part + 1) * half] = total.reshape(groups, slots, half)
+    for i in range(step):
+        rows = by_lat[:, i].reshape(groups * slots, width)
+        synthesis = dot(rows[:, :half], cosine[i], ((0,), (0,)))
+        synthesis = synthesis + dot(rows[:, half:], sine[i], ((0,), (0,)))
+        lat_scale = scale[i]
+        inc = (synthesis * lat_scale).astype(BF16)
+        increment[0, i] = inc
+        weighted = (inc.astype(F32) * weight[i].astype(F32) * lat_scale).astype(BF16)
+        for part, table in ((0, cosine), (1, sine)):
+            total = dot(table[i], weighted, ((1,), (1,))).astype(BF16)
+            adjoint[:, i, :, part * half : (part + 1) * half] = total.reshape(groups, slots, half)
 
 
 def grid_stage(by_lat, tables, lat_scale, obs_weight, member, sub, shape, into):
     groups, lats, slots, width = by_lat.shape
     half = width // 2
     count = groups * slots
-    table = pl.BlockSpec((1, count, LONGITUDES), lambda t: (t, 0, 0))
-    lat_rows = pl.BlockSpec((groups, 1, slots, width), lambda t: (0, t, 0, 0))
+    step = 2 if lats % 2 == 0 else 1
+    table = pl.BlockSpec((step, count, LONGITUDES), lambda t: (t, 0, 0))
+    lat_rows = pl.BlockSpec((groups, step, slots, width), lambda t: (0, t, 0, 0))
     in_specs = [
         lat_rows,
         table,
         table,
-        pl.BlockSpec((1, half, 1), lambda t: (t, sub, 0)),
-        pl.BlockSpec((1, half, LONGITUDES), lambda t: (t, sub, 0)),
+        pl.BlockSpec((step, half, 1), lambda t: (t, sub, 0)),
+        pl.BlockSpec((step, half, LONGITUDES), lambda t: (t, sub, 0)),
     ]
     operands = [by_lat, *tables, lat_scale, obs_weight]
     aliases = {}
@@ -349,10 +351,10 @@
         aliases = {5: 0}
     return pl.pallas_call(
         grid_body,
-        grid=(lats,),
+        grid=(lats // step,),
         in_specs=in_specs,
         out_specs=[
-            pl.BlockSpec((1, 1, half, LONGITUDES), lambda t: (member, t, sub, 0)),
+            pl.BlockSpec((1, step, half, LONGITUDES), lambda t: (member, t, sub, 0)),
             lat_rows,
         ],
         out_shape=[jax.ShapeDtypeStruct(shape, BF16), jax.ShapeDtypeStruct(by_lat.shape, BF16)],

time: 716 us -> 701 us (0.979)
  Pallas kernels: 264 us -> 249 us
    pallas_call x4, Pallas kernels: 62.2 us -> 47.4 us  [grid_stage(): pl.pallas_call(grid_body, grid=(lats // step,), in_specs=in_specs, out_sp...]
  transfers between devices with their start and end apart: 50 -> 50, of which waited for: 23 -> 23; matrix products, arithmetic and copies ran while one was open for 4% -> 4% of each run, Pallas kernels for 36% -> 34%
where the time goes in v5:
time: 701 us; the launch traced here: 697 us
  waiting for transfers between devices  271 us (39%)
  Pallas kernels  249 us (36%)
  starting transfers between devices  102 us (15%)
  local copies, waits for them, and re-layouts  33.4 us (5%)
  blocking collectives  33.2 us (5%)
    ppermute x30, waiting for transfers between devices, far_shift(): lax.ppermute(values, 'wave', [(i, (i + shift * inner) % count) for i in r...  244 us
    pallas_call x10, Pallas kernels, vertical_fwd(): pl.pallas_call(functools.partial(vertical_fwd_body, first_slot), grid_spe...  67.7 us
    pallas_call x10, Pallas kernels, vertical_adj(): pl.pallas_call(functools.partial(vertical_adj_body, first_slot), grid_spe...  59.1 us
    ppermute x30, starting transfers between devices, far_shift(): lax.ppermute(values, 'wave', [(i, (i + shift * inner) % count) for i in r...  53.1 us
    pallas_call x4, Pallas kernels, grid_stage(): pl.pallas_call(grid_body, grid=(lats // step,), in_specs=in_specs, out_sp...  47.4 us
    all_to_all x8, starting transfers between devices, near_exchange(): lax.all_to_all(values, 'wave', split_axis=0, concat_axis=0, axis_index_gr...  36.9 us
    all_to_all x2, blocking collectives, near_exchange(): lax.all_to_all(values, 'wave', split_axis=0, concat_axis=0, axis_index_gr...  33.2 us
    pallas_call x5, Pallas kernels, legendre_adj(): pl.pallas_call(legendre_adj_body, grid_spec=pltpu.PrefetchScalarGridSpec(...  28.7 us
  transfers between devices with their start and end apart: 50, of which 23 were waited for; matrix products, arithmetic and copies ran while one was open for 4% of the time, Pallas kernels for 34%

profile of v5, /device:TPU:13, one launch (start us, length us, event | category | flops | bytes accessed | tf_op | source)
XLA Modules:
  0.0 696.7 jit_solution(2839657846771722430)
XLA Ops:
  2.6 5.1 vertical_fwd.17
  8.9 5.1 vertical_fwd.19
  16.0 7.8 %vertical_fwd.11 = bf16[16,128,256]{2,1,0:T(8,128)(2,1)} custom-call(s32[2]{0:T(128)} %pad_add_fusion.info, s32[16]{0:T(128)} %dynamic_slice.3.waves, bf16[2,16,128,2,512]{4,3,2,1,0:T(2,128)(2,1)} %x.19, bf16[4,4,128,128]{3,2,1,0:T(8,128)(2,1)} %v.39), custom_call_target="tpu_custom_call" | custom-call | flops 8589934592 | bytes 4194304 | tf_op jit(solution)/shard_map/vertical_fwd/pallas_call | solution.py:79
  23.9 5.1 vertical_fwd.18.own
  32.0 11.2 %collective-permute-done.1.lx = bf16[8,128,256]{2,1,0:T(8,128)(2,1)S(1)} collective-permute-done((bf16[8,128,256]{2,1,0:T(8,128)(2,1)S(1)}, bf16[8,128,256]{2,1,0:T(8,128)(2,1)S(1)}, u32[]{:S(2)}, u32[]{:S(2)}) %collective-permute-start.1) | collective-permute-done | bytes 524320 | tf_op jit(solution)/shard_map/ppermute | solution.py:369
  44.0 4.1 legendre_fwd.9
  51.8 5.1 vertical_fwd.16.own
  59.0 4.0 legendre_fwd.8
  70.7 14.8 %collective-permute-done.21 = bf16[4,16,8,256]{3,2,1,0:T(8,128)(2,1)S(1)} collective-permute-done((bf16[4,16,8,256]{3,2,1,0:T(8,128)(2,1)}, bf16[4,16,8,256]{3,2,1,0:T(8,128)(2,1)S(1)}, u32[]{:S(2)}, u32[]{:S(2)}) %collective-permute-start.21) | collective-permute-done | bytes 262176 | tf_op jit(solution)/shard_map/ppermute | solution.py:379
  86.6 4.2 all-to-all-start.4
  90.8 8.0 %vertical_fwd.10.own = bf16[16,128,256]{2,1,0:T(8,128)(2,1)} custom-call(s32[2]{0:T(128)} %pad_add_fusion.info, s32[16]{0:T(128)} %dynamic_slice.3.waves, bf16[2,16,128,2,512]{4,3,2,1,0:T(2,128)(2,1)} %x.19, bf16[4,4,128,128]{3,2,1,0:T(8,128)(2,1)} %v.39), custom_call_target="tpu_custom_call" | custom-call | flops 8589934592 | bytes 4194304 | tf_op jit(solution)/shard_map/vertical_fwd/pallas_call | solution.py:79
  100.9 6.7 legendre_fwd.5
  107.7 4.8 collective-permute-start.4
  112.5 4.1 all-to-all-start.3
  116.6 8.0 %vertical_fwd.13 = bf16[16,128,256]{2,1,0:T(8,128)(2,1)} custom-call(s32[2]{0:T(128)} %pad_add_fusion.info, s32[16]{0:T(128)} %dynamic_slice.3.waves, bf16[2,16,128,2,512]{4,3,2,1,0:T(2,128)(2,1)} %x.19, bf16[4,4,128,128]{3,2,1,0:T(8,128)(2,1)} %v.39), custom_call_target="tpu_custom_call" | custom-call | flops 8589934592 | bytes 4194304 | tf_op jit(solution)/shard_map/vertical_fwd/pallas_call | solution.py:79
  125.7 26.9 %collective-permute-done.4 = bf16[4,16,16,256]{3,2,1,0:T(8,128)(2,1)} collective-permute-done((bf16[4,16,16,256]{3,2,1,0:T(8,128)(2,1)}, bf16[4,16,16,256]{3,2,1,0:T(8,128)(2,1)}, u32[]{:S(2)}, u32[]{:S(2)}) %collective-permute-start.4) | collective-permute-done | bytes 524320 | tf_op jit(solution)/shard_map/ppermute | solution.py:379
  152.6 4.7 collective-permute-done.5
  161.3 4.8 all-to-all-start
  166.1 7.8 %vertical_fwd.12.own = bf16[16,128,256]{2,1,0:T(8,128)(2,1)} custom-call(s32[2]{0:T(128)} %pad_add_fusion.info, s32[16]{0:T(128)} %dynamic_slice.3.waves, bf16[2,16,128,2,512]{4,3,2,1,0:T(2,128)(2,1)} %x.19, bf16[4,4,128,128]{3,2,1,0:T(8,128)(2,1)} %v.39), custom_call_target="tpu_custom_call" | custom-call | flops 8589934592 | bytes 4194304 | tf_op jit(solution)/shard_map/vertical_fwd/pallas_call | solution.py:79
  173.9 6.8 legendre_fwd.6
  182.2 7.8 %vertical_fwd.15 = bf16[16,128,256]{2,1,0:T(8,128)(2,1)} custom-call(s32[2]{0:T(128)} %pad_add_fusion.info, s32[16]{0:T(128)} %dynamic_slice.3.waves, bf16[2,16,128,2,512]{4,3,2,1,0:T(2,128)(2,1)} %x.19, bf16[4,4,128,128]{3,2,1,0:T(8,128)(2,1)} %v.39), custom_call_target="tpu_custom_call" | custom-call | flops 8589934592 | bytes 4194304 | tf_op jit(solution)/shard_map/vertical_fwd/pallas_call | solution.py:79
  194.0 31.9 %collective-permute-done.8 = bf16[4,16,16,256]{3,2,1,0:T(8,128)(2,1)S(1)} collective-permute-done((bf16[4,16,16,256]{3,2,1,0:T(8,128)(2,1)}, bf16[4,16,16,256]{3,2,1,0:T(8,128)(2,1)S(1)}, u32[]{:S(2)}, u32[]{:S(2)}) %collective-permute-start.8) | collective-permute-done | bytes 524320 | tf_op jit(solution)/shard_map/ppermute | solution.py:379
  229.1 5.4 all-to-all-start.1
  234.5 7.8 %vertical_fwd.14.own = bf16[16,128,256]{2,1,0:T(8,128)(2,1)} custom-call(s32[2]{0:T(128)} %pad_add_fusion.info, s32[16]{0:T(128)} %dynamic_slice.3.waves, bf16[2,16,128,2,512]{4,3,2,1,0:T(2,128)(2,1)} %x.19, bf16[4,4,128,128]{3,2,1,0:T(8,128)(2,1)} %v.39), custom_call_target="tpu_custom_call" | custom-call | flops 8589934592 | bytes 4194304 | tf_op jit(solution)/shard_map/vertical_fwd/pallas_call | solution.py:79
  242.3 6.7 legendre_fwd.7
  253.5 8.8 %collective-permute-done.11 = bf16[4,16,16,256]{3,2,1,0:T(8,128)(2,1)S(1)} collective-permute-done((bf16[4,16,16,256]{3,2,1,0:T(8,128)(2,1)}, bf16[4,16,16,256]{3,2,1,0:T(8,128)(2,1)S(1)}, u32[]{:S(2)}, u32[]{:S(2)}) %collective-permute-start.11) | collective-permute-done | bytes 524320 | tf_op jit(solution)/shard_map/ppermute | solution.py:379
  262.4 31.9 %collective-permute-done.12 = bf16[4,16,16,256]{3,2,1,0:T(8,128)(2,1)S(1)} collective-permute-done((bf16[4,16,16,256]{3,2,1,0:T(8,128)(2,1)}, bf16[4,16,16,256]{3,2,1,0:T(8,128)(2,1)S(1)}, u32[]{:S(2)}, u32[]{:S(2)}) %collective-permute-start.12) | collective-permute-done | bytes 524320 | tf_op jit(solution)/shard_map/ppermute | solution.py:379
  294.3 4.2 collective-permute-done.13
  301.3 4.2 all-to-all-start.2
  309.1 18.1 %fourier_tables.1 = (bf16[16,256,512]{2,1,0:T(8,128)(2,1)}, bf16[16,256,512]{2,1,0:T(8,128)(2,1)}) custom-call(s32[16]{0:T(128)} %points.1, f32[256,1]{1,0:T(8,128)} %convert_element_type.20.waves), custom_call_target="tpu_custom_call" | custom-call | flops 83886080 | bytes 8388608 | tf_op jit(solution)/shard_map/fourier_tables/pallas_call | solution.py:300
  330.0 11.8 %grid_stage.4 = (bf16[2,16,256,512]{3,2,1,0:T(8,128)(2,1)}, bf16[16,16,16,256]{3,2,1,0:T(8,128)(2,1)}) custom-call(bf16[16,16,16,256]{3,2,1,0:T(8,128)(2,1)} %bitcast.120, bf16[16,256,512]{2,1,0:T(8,128)(2,1)} %get-tuple-element.46.cosine, bf16[16,256,512]{2,1,0:T(8,128)(2,1)} %get-tuple-element.47.sine, f32[16,256,1]{2,1,0:T(8,128)} %copy.51.scale, ...), custom_call_target="tpu_custom_call" | custom-call | flops 2147483648 | bytes 12582912 | tf_op jit(solution)/shard_map/grid_stage/pallas_call | solution.py:352
  343.1 4.6 all-to-all-start.9
  347.8 11.8 %grid_stage.5 = (bf16[2,16,256,512]{3,2,1,0:T(8,128)(2,1)}, bf16[16,16,16,256]{3,2,1,0:T(8,128)(2,1)}) custom-call(bf16[16,16,16,256]{3,2,1,0:T(8,128)(2,1)} %bitcast.119, bf16[16,256,512]{2,1,0:T(8,128)(2,1)} %get-tuple-element.46.cosine, bf16[16,256,512]{2,1,0:T(8,128)(2,1)} %get-tuple-element.47.sine, ...), custom_call_target="tpu_custom_call", output_to_operand_aliasing={{0}: (5, {})} | custom-call | flops 2147483648 | bytes 12582912 | tf_op jit(solution)/shard_map/grid_stage/pallas_call | solution.py:352
  359.6 11.9 %grid_stage.6 = (bf16[2,16,256,512]{3,2,1,0:T(8,128)(2,1)}, bf16[16,16,16,256]{3,2,1,0:T(8,128)(2,1)}) custom-call(bf16[16,16,16,256]{3,2,1,0:T(8,128)(2,1)} %bitcast.14.by_lat, bf16[16,256,512]{2,1,0:T(8,128)(2,1)} %get-tuple-element.46.cosine, bf16[16,256,512]{2,1,0:T(8,128)(2,1)} %get-tuple-element.47.sine, ...), custom_call_target="tpu_custom_call", output_to_operand_aliasing={{0}: (5, {})} | custom-call | flops 2147483648 | bytes 12582912 | tf_op jit(solution)/shard_map/grid_stage/pallas_call | solution.py:352
  371.5 11.8 %grid_stage.7 = (bf16[2,16,256,512]{3,2,1,0:T(8,128)(2,1)}, bf16[16,16,16,256]{3,2,1,0:T(8,128)(2,1)}) custom-call(bf16[16,16,16,256]{3,2,1,0:T(8,128)(2,1)} %bitcast.118, bf16[16,256,512]{2,1,0:T(8,128)(2,1)} %get-tuple-element.46.cosine, bf16[16,256,512]{2,1,0:T(8,128)(2,1)} %get-tuple-element.47.sine, ...), custom_call_target="tpu_custom_call", output_to_operand_aliasing={{0}: (5, {})} | custom-call | flops 2147483648 | bytes 12582912 | tf_op jit(solution)/shard_map/grid_stage/pallas_call | solution.py:352
  385.0 15.7 %all_to_all.50 = bf16[4,4,16,8,256]{4,3,2,1,0:T(8,128)(2,1)S(1)} all-to-all(bf16[4,4,16,8,256]{4,3,2,1,0:T(8,128)(2,1)S(1)} %bitcast.122), channel_id=1, replica_groups={{0,2,4,6},{8,10,12,14},{16,18,20,22},{24,26,28,30},{1,3,5,7},{9,11,13,1..., dimensions={0} | all-to-all | bytes 2097152 | tf_op jit(solution)/shard_map/all_to_all | solution.py:374
  400.7 17.5 %all_to_all.51 = bf16[4,4,16,8,256]{4,3,2,1,0:T(8,128)(2,1)} all-to-all(bf16[4,4,16,8,256]{4,3,2,1,0:T(8,128)(2,1)S(1)} %bitcast.121), channel_id=1, replica_groups={{0,2,4,6},{8,10,12,14},{16,18,20,22},{24,26,28,30},{1,3,5,7},{9,11,13,1..., dimensions={0} | all-to-all | bytes 2097152 | tf_op jit(solution)/shard_map/all_to_all | solution.py:374
  418.2 5.4 all-to-all-start.8
  427.6 11.6 %collective-permute-done.40.rest_3_ = bf16[4,16,16,256]{3,2,1,0:T(8,128)(2,1)S(1)} collective-permute-done((bf16[4,16,16,256]{3,2,1,0:T(8,128)(2,1)S(1)}, bf16[4,16,16,256]{3,2,1,0:T(8,128)(2,1)S(1)}, u32[]{:S(2)}, u32[]{:S(2)}) %collective-permute-start.40) | collective-permute-done | bytes 524320 | tf_op jit(solution)/shard_map/ppermute | solution.py:379
  439.2 31.8 %collective-permute-done.39.rest_2_ = bf16[4,16,16,256]{3,2,1,0:T(8,128)(2,1)S(1)} collective-permute-done((bf16[4,16,16,256]{3,2,1,0:T(8,128)(2,1)S(1)}, bf16[4,16,16,256]{3,2,1,0:T(8,128)(2,1)S(1)}, u32[]{:S(2)}, u32[]{:S(2)}) %collective-permute-start.39) | collective-permute-done | bytes 524320 | tf_op jit(solution)/shard_map/ppermute | solution.py:379
  472.4 6.9 legendre_adj.9
  480.7 4.1 all-to-all-start.7
  496.8 7.0 %collective-permute-done.27.rest_2_ = bf16[4,16,8,256]{3,2,1,0:T(8,128)(2,1)S(1)} collective-permute-done((bf16[4,16,8,256]{3,2,1,0:T(8,128)(2,1)S(1)}, bf16[4,16,8,256]{3,2,1,0:T(8,128)(2,1)S(1)}, u32[]{:S(2)}, u32[]{:S(2)}) %collective-permute-start.27) | collective-permute-done | bytes 262176 | tf_op jit(solution)/shard_map/ppermute | solution.py:379
  503.8 16.7 %collective-permute-start.26 = (bf16[4,16,8,256]{3,2,1,0:T(8,128)(2,1)S(1)}, bf16[4,16,8,256]{3,2,1,0:T(8,128)(2,1)S(1)}, u32[]{:S(2)}, u32[]{:S(2)}) collective-permute-start(bf16[4,16,8,256]{3,2,1,0:T(8,128)(2,1)S(1)} %get-tuple-element.98), channel_id=1, source_target_pairs={{0,24},{2,26},{4,28},{6,30},{8,0},{10,2},{12,4},{14,6},{16,8},{18,... | collective-permute-start | bytes 786440 | tf_op jit(solution)/shard_map/ppermute | solution.py:379
  522.8 9.1 %collective-permute-done.23.rest_2_ = bf16[4,16,8,256]{3,2,1,0:T(8,128)(2,1)S(1)} collective-permute-done((bf16[4,16,8,256]{3,2,1,0:T(8,128)(2,1)S(1)}, bf16[4,16,8,256]{3,2,1,0:T(8,128)(2,1)S(1)}, u32[]{:S(2)}, u32[]{:S(2)}) %collective-permute-start.23) | collective-permute-done | bytes 262176 | tf_op jit(solution)/shard_map/ppermute | solution.py:379
  535.0 18.0 %collective-permute-done.22.rest_1_ = bf16[4,16,8,256]{3,2,1,0:T(8,128)(2,1)S(1)} collective-permute-done((bf16[4,16,8,256]{3,2,1,0:T(8,128)(2,1)S(1)}, bf16[4,16,8,256]{3,2,1,0:T(8,128)(2,1)S(1)}, u32[]{:S(2)}, u32[]{:S(2)}) %collective-permute-start.22) | collective-permute-done | bytes 262176 | tf_op jit(solution)/shard_map/ppermute | solution.py:379
  553.0 6.8 vertical_adj.10.rest_0_
  559.9 4.0 legendre_adj.5
  565.1 3.9 legendre_adj.6
  571.5 5.5 collective-permute-done.35.rest_2_
  580.1 23.7 %collective-permute-done.34.rest_1_ = bf16[4,16,16,256]{3,2,1,0:T(8,128)(2,1)} collective-permute-done((bf16[4,16,16,256]{3,2,1,0:T(8,128)(2,1)S(1)}, bf16[4,16,16,256]{3,2,1,0:T(8,128)(2,1)}, u32[]{:S(2)}, u32[]{:S(2)}) %collective-permute-start.34) | collective-permute-done | bytes 524320 | tf_op jit(solution)/shard_map/ppermute | solution.py:379
  603.7 7.0 legendre_adj.8
  612.0 6.8 vertical_adj.11.rest_0_
  621.8 4.3 collective-permute-done.30.rest_1_
  626.9 6.9 legendre_adj.7
  635.0 6.8 vertical_adj.12.rest_0_
  642.8 6.8 vertical_adj.13.rest_0_
  649.6 6.8 vertical_adj.14.rest_0_
  656.4 12.5 %collective-permute-done.33.block = bf16[16,128,256]{2,1,0:T(8,128)(2,1)S(1)} collective-permute-done((bf16[16,128,256]{2,1,0:T(8,128)(2,1)}, bf16[16,128,256]{2,1,0:T(8,128)(2,1)S(1)}, u32[]{:S(2)}, u32[]{:S(2)}) %collective-permute-start.33) | collective-permute-done | bytes 1048608 | tf_op jit(solution)/shard_map/ppermute | solution.py:369
  669.8 6.8 vertical_adj.15.rest_0_
  676.6 4.6 vertical_adj.16.rest_0_
  682.0 4.6 vertical_adj.17.rest_0_
  686.6 4.6 vertical_adj.18.rest_0_
  692.0 4.7 vertical_adj.19
  (182 shorter events, 96.9 us)
Async XLA Ops:
  0.6 306.3 %copy-start = (f32[8,256]{1,0:T(8,128)S(1)}, f32[8,256]{1,0:T(8,128)}, u32[]{:S(2)}) copy-start(f32[8,256]{1,0:T(8,128)} %param.14) | copy-start | bytes 24580
  7.7 49.2 %collective-permute-start.14 = (bf16[8,128,256]{2,1,0:T(8,128)(2,1)}, bf16[8,128,256]{2,1,0:T(8,128)(2,1)S(1)}, u32[]{:S(2)}, u32[]{:S(2)}) collective-permute-start(bf16[8,128,256]{2,1,0:T(8,128)(2,1)} %vertical_fwd.17), channel_id=1, source_target_pairs={{0,1},{1,0},{2,3},{3,2},{4,5},{5,4},{6,7},{7,6},{8,9},{9,8},{10,11... | collective-permute-start | bytes 1572872 | tf_op jit(solution)/shard_map/ppermute | solution.py:369
  14.0 17.9 %collective-permute-start.18 = (bf16[8,128,256]{2,1,0:T(8,128)(2,1)}, bf16[8,128,256]{2,1,0:T(8,128)(2,1)S(1)}, u32[]{:S(2)}, u32[]{:S(2)}) collective-permute-start(bf16[8,128,256]{2,1,0:T(8,128)(2,1)} %vertical_fwd.19), channel_id=1, source_target_pairs={{0,1},{1,0},{2,3},{3,2},{4,5},{5,4},{6,7},{7,6},{8,9},{9,8},{10,11... | collective-permute-start | bytes 1572872 | tf_op jit(solution)/shard_map/ppermute | solution.py:369
  14.5 28.7 %collective-permute-start.1 = (bf16[8,128,256]{2,1,0:T(8,128)(2,1)S(1)}, bf16[8,128,256]{2,1,0:T(8,128)(2,1)S(1)}, u32[]{:S(2)}, u32[]{:S(2)}) collective-permute-start(bf16[8,128,256]{2,1,0:T(8,128)(2,1)S(1)} %get-tuple-element.104), channel_id=1, source_target_pairs={{0,1},{1,0},{2,3},{3,2},{4,5},{5,4},{6,7},{7,6},{8,9},{9,8},{10,11... | collective-permute-start | bytes 1572872 | tf_op jit(solution)/shard_map/ppermute | solution.py:369
  15.6 42.6 %collective-permute-start = (bf16[8,128,256]{2,1,0:T(8,128)(2,1)S(1)}, bf16[8,128,256]{2,1,0:T(8,128)(2,1)S(1)}, u32[]{:S(2)}, u32[]{:S(2)}) collective-permute-start(bf16[8,128,256]{2,1,0:T(8,128)(2,1)S(1)} %get-tuple-element.105), channel_id=1, source_target_pairs={{0,1},{1,0},{2,3},{3,2},{4,5},{5,4},{6,7},{7,6},{8,9},{9,8},{10,11... | collective-permute-start | bytes 1572872 | tf_op jit(solution)/shard_map/ppermute | solution.py:369
  32.0 11.2 %copy-start.28 = (bf16[8,128,256]{2,1,0:T(8,128)(2,1)}, bf16[8,128,256]{2,1,0:T(8,128)(2,1)S(1)}, u32[]{:S(2)}) copy-start(bf16[8,128,256]{2,1,0:T(8,128)(2,1)S(1)} %collective-permute-done.18.recv) | copy-start | bytes 1572868
  48.1 15.1 %collective-permute-start.19 = (bf16[4,16,8,256]{3,2,1,0:T(8,128)(2,1)}, bf16[4,16,8,256]{3,2,1,0:T(8,128)(2,1)S(1)}, u32[]{:S(2)}, u32[]{:S(2)}) collective-permute-start(bf16[4,16,8,256]{3,2,1,0:T(8,128)(2,1)} %get-tuple-element.61), channel_id=1, source_target_pairs={{0,8},{2,10},{4,12},{6,14},{8,16},{10,18},{12,20},{14,22},{16,24},... | collective-permute-start | bytes 786440 | tf_op jit(solution)/shard_map/ppermute | solution.py:379
  49.4 20.5 %collective-permute-start.20 = (bf16[4,16,8,256]{3,2,1,0:T(8,128)(2,1)}, bf16[4,16,8,256]{3,2,1,0:T(8,128)(2,1)S(1)}, u32[]{:S(2)}, u32[]{:S(2)}) collective-permute-start(bf16[4,16,8,256]{3,2,1,0:T(8,128)(2,1)} %get-tuple-element.62), channel_id=1, source_target_pairs={{0,16},{2,18},{4,20},{6,22},{8,24},{10,26},{12,28},{14,30},{16,0},... | collective-permute-start | bytes 786440 | tf_op jit(solution)/shard_map/ppermute | solution.py:379
  50.4 35.0 %collective-permute-start.21 = (bf16[4,16,8,256]{3,2,1,0:T(8,128)(2,1)}, bf16[4,16,8,256]{3,2,1,0:T(8,128)(2,1)S(1)}, u32[]{:S(2)}, u32[]{:S(2)}) collective-permute-start(bf16[4,16,8,256]{3,2,1,0:T(8,128)(2,1)} %get-tuple-element.63), channel_id=1, source_target_pairs={{0,24},{2,26},{4,28},{6,30},{8,0},{10,2},{12,4},{14,6},{16,8},{18,... | collective-permute-start | bytes 786440 | tf_op jit(solution)/shard_map/ppermute | solution.py:379
  56.9 28.5 %copy-start.17 = (bf16[4,16,8,256]{3,2,1,0:T(8,128)(2,1)S(1)}, bf16[4,16,8,256]{3,2,1,0:T(8,128)(2,1)}, u32[]{:S(2)}) copy-start(bf16[4,16,8,256]{3,2,1,0:T(8,128)(2,1)} %get-tuple-element.60) | copy-start | bytes 786436
  57.0 44.0 %collective-permute-start.2 = (bf16[16,128,256]{2,1,0:T(8,128)(2,1)S(1)}, bf16[16,128,256]{2,1,0:T(8,128)(2,1)}, u32[]{:S(2)}, u32[]{:S(2)}) collective-permute-start(bf16[16,128,256]{2,1,0:T(8,128)(2,1)S(1)} %copy-done.20), channel_id=1, source_target_pairs={{0,1},{1,0},{2,3},{3,2},{4,5},{5,4},{6,7},{7,6},{8,9},{9,8},{10,11... | collective-permute-start | bytes 3145736 | tf_op jit(solution)/shard_map/ppermute | solution.py:369
  63.1 35.8 %collective-permute-start.15 = (bf16[4,16,8,256]{3,2,1,0:T(8,128)(2,1)}, bf16[4,16,8,256]{3,2,1,0:T(8,128)(2,1)S(1)}, u32[]{:S(2)}, u32[]{:S(2)}) collective-permute-start(bf16[4,16,8,256]{3,2,1,0:T(8,128)(2,1)} %get-tuple-element.57), channel_id=1, source_target_pairs={{0,8},{2,10},{4,12},{6,14},{8,16},{10,18},{12,20},{14,22},{16,24},... | collective-permute-start | bytes 786440 | tf_op jit(solution)/shard_map/ppermute | solution.py:379
  63.1 35.8 %collective-permute-start.16 = (bf16[4,16,8,256]{3,2,1,0:T(8,128)(2,1)}, bf16[4,16,8,256]{3,2,1,0:T(8,128)(2,1)S(1)}, u32[]{:S(2)}, u32[]{:S(2)}) collective-permute-start(bf16[4,16,8,256]{3,2,1,0:T(8,128)(2,1)} %get-tuple-element.58), channel_id=1, source_target_pairs={{0,16},{2,18},{4,20},{6,22},{8,24},{10,26},{12,28},{14,30},{16,0},... | collective-permute-start | bytes 786440 | tf_op jit(solution)/shard_map/ppermute | solution.py:379
  69.9 29.0 %collective-permute-start.17 = (bf16[4,16,8,256]{3,2,1,0:T(8,128)(2,1)}, bf16[4,16,8,256]{3,2,1,0:T(8,128)(2,1)S(1)}, u32[]{:S(2)}, u32[]{:S(2)}) collective-permute-start(bf16[4,16,8,256]{3,2,1,0:T(8,128)(2,1)} %get-tuple-element.59), channel_id=1, source_target_pairs={{0,24},{2,26},{4,28},{6,30},{8,0},{10,2},{12,4},{14,6},{16,8},{18,... | collective-permute-start | bytes 786440 | tf_op jit(solution)/shard_map/ppermute | solution.py:379
  86.6 25.9 %all-to-all-start.4 = ((bf16[4,4,16,8,256]{4,3,2,1,0:T(8,128)(2,1)}), bf16[4,4,16,8,256]{4,3,2,1,0:T(8,128)(2,1)S(1)}, u32[]{:S(2)}, u32[]{:S(2)}) async-start(bf16[4,4,16,8,256]{4,3,2,1,0:T(8,128)(2,1)} %copy.47), calls=%async_computation.4 | async-start | bytes 2097152 | tf_op jit(solution)/shard_map/all_to_all | solution.py:374
  90.8 8.0 %copy-start.11 = (bf16[8,128,256]{2,1,0:T(8,128)(2,1)S(1)}, bf16[8,128,256]{2,1,0:T(8,128)(2,1)}, u32[]{:S(2)}) copy-start(bf16[8,128,256]{2,1,0:T(8,128)(2,1)} %copy-done.10) | copy-start | bytes 1572868
  90.8 8.0 %copy-start.13 = (bf16[8,128,256]{2,1,0:T(8,128)(2,1)S(1)}, bf16[8,128,256]{2,1,0:T(8,128)(2,1)}, u32[]{:S(2)}) copy-start(bf16[8,128,256]{2,1,0:T(8,128)(2,1)} %copy-done.12) | copy-start | bytes 1572868
  107.6 18.1 %collective-permute-start.3 = (bf16[4,16,16,256]{3,2,1,0:T(8,128)(2,1)}, bf16[4,16,16,256]{3,2,1,0:T(8,128)(2,1)S(1)}, u32[]{:S(2)}, u32[]{:S(2)}) collective-permute-start(bf16[4,16,16,256]{3,2,1,0:T(8,128)(2,1)} %get-tuple-element.43), channel_id=1, source_target_pairs={{0,8},{2,10},{4,12},{6,14},{8,16},{10,18},{12,20},{14,22},{16,24},... | collective-permute-start | bytes 1572872 | tf_op jit(solution)/shard_map/ppermute | solution.py:379
  107.7 45.0 %collective-permute-start.4 = (bf16[4,16,16,256]{3,2,1,0:T(8,128)(2,1)}, bf16[4,16,16,256]{3,2,1,0:T(8,128)(2,1)}, u32[]{:S(2)}, u32[]{:S(2)}) collective-permute-start(bf16[4,16,16,256]{3,2,1,0:T(8,128)(2,1)} %get-tuple-element.44), channel_id=1, source_target_pairs={{0,16},{2,18},{4,20},{6,22},{8,24},{10,26},{12,28},{14,30},{16,0},... | collective-permute-start | bytes 1572872 | tf_op jit(solution)/shard_map/ppermute | solution.py:379
  112.5 44.8 %collective-permute-start.5 = (bf16[4,16,16,256]{3,2,1,0:T(8,128)(2,1)}, bf16[4,16,16,256]{3,2,1,0:T(8,128)(2,1)}, u32[]{:S(2)}, u32[]{:S(2)}) collective-permute-start(bf16[4,16,16,256]{3,2,1,0:T(8,128)(2,1)} %get-tuple-element.45), channel_id=1, source_target_pairs={{0,24},{2,26},{4,28},{6,30},{8,0},{10,2},{12,4},{14,6},{16,8},{18,... | collective-permute-start | bytes 1572872 | tf_op jit(solution)/shard_map/ppermute | solution.py:379
  112.5 47.8 %all-to-all-start.3 = ((bf16[4,4,16,8,256]{4,3,2,1,0:T(8,128)(2,1)}), bf16[4,4,16,8,256]{4,3,2,1,0:T(8,128)(2,1)S(1)}, u32[]{:S(2)}, u32[]{:S(2)}) async-start(bf16[4,4,16,8,256]{4,3,2,1,0:T(8,128)(2,1)} %copy.46), calls=%async_computation.3 | async-start | bytes 2097152 | tf_op jit(solution)/shard_map/all_to_all | solution.py:374
  116.6 40.7 %copy-start.14 = (bf16[4,16,16,256]{3,2,1,0:T(8,128)(2,1)S(1)}, bf16[4,16,16,256]{3,2,1,0:T(8,128)(2,1)}, u32[]{:S(2)}) copy-start(bf16[4,16,16,256]{3,2,1,0:T(8,128)(2,1)} %get-tuple-element.42) | copy-start | bytes 1572868
  124.5 49.4 %collective-permute-start.6 = (bf16[16,128,256]{2,1,0:T(8,128)(2,1)}, bf16[16,128,256]{2,1,0:T(8,128)(2,1)}, u32[]{:S(2)}, u32[]{:S(2)}) collective-permute-start(bf16[16,128,256]{2,1,0:T(8,128)(2,1)} %vertical_fwd.13), channel_id=1, source_target_pairs={{0,1},{1,0},{2,3},{3,2},{4,5},{5,4},{6,7},{7,6},{8,9},{9,8},{10,11... | collective-permute-start | bytes 3145736 | tf_op jit(solution)/shard_map/ppermute | solution.py:369
  161.3 66.4 %all-to-all-start = ((bf16[4,4,16,16,256]{4,3,2,1,0:T(8,128)(2,1)}), bf16[4,4,16,16,256]{4,3,2,1,0:T(8,128)(2,1)S(1)}, u32[]{:S(2)}, u32[]{:S(2)}) async-start(bf16[4,4,16,16,256]{4,3,2,1,0:T(8,128)(2,1)} %copy.41), calls=%async_computation | async-start | bytes 4194304 | tf_op jit(solution)/shard_map/all_to_all | solution.py:374
  180.7 13.3 %collective-permute-start.7 = (bf16[4,16,16,256]{3,2,1,0:T(8,128)(2,1)}, bf16[4,16,16,256]{3,2,1,0:T(8,128)(2,1)S(1)}, u32[]{:S(2)}, u32[]{:S(2)}) collective-permute-start(bf16[4,16,16,256]{3,2,1,0:T(8,128)(2,1)} %get-tuple-element.49), channel_id=1, source_target_pairs={{0,8},{2,10},{4,12},{6,14},{8,16},{10,18},{12,20},{14,22},{16,24},... | collective-permute-start | bytes 1572872 | tf_op jit(solution)/shard_map/ppermute | solution.py:379
  180.7 45.2 %collective-permute-start.8 = (bf16[4,16,16,256]{3,2,1,0:T(8,128)(2,1)}, bf16[4,16,16,256]{3,2,1,0:T(8,128)(2,1)S(1)}, u32[]{:S(2)}, u32[]{:S(2)}) collective-permute-start(bf16[4,16,16,256]{3,2,1,0:T(8,128)(2,1)} %get-tuple-element.50), channel_id=1, source_target_pairs={{0,16},{2,18},{4,20},{6,22},{8,24},{10,26},{12,28},{14,30},{16,0},... | collective-permute-start | bytes 1572872 | tf_op jit(solution)/shard_map/ppermute | solution.py:379
  180.7 45.2 %copy-start.15 = (bf16[4,16,16,256]{3,2,1,0:T(8,128)(2,1)S(1)}, bf16[4,16,16,256]{3,2,1,0:T(8,128)(2,1)}, u32[]{:S(2)}) copy-start(bf16[4,16,16,256]{3,2,1,0:T(8,128)(2,1)} %get-tuple-element.48) | copy-start | bytes 1572868
  180.7 45.1 %collective-permute-start.9 = (bf16[4,16,16,256]{3,2,1,0:T(8,128)(2,1)}, bf16[4,16,16,256]{3,2,1,0:T(8,128)(2,1)S(1)}, u32[]{:S(2)}, u32[]{:S(2)}) collective-permute-start(bf16[4,16,16,256]{3,2,1,0:T(8,128)(2,1)} %get-tuple-element.51), channel_id=1, source_target_pairs={{0,24},{2,26},{4,28},{6,30},{8,0},{10,2},{12,4},{14,6},{16,8},{18,... | collective-permute-start | bytes 1572872 | tf_op jit(solution)/shard_map/ppermute | solution.py:379
  190.0 52.3 %collective-permute-start.10 = (bf16[16,128,256]{2,1,0:T(8,128)(2,1)}, bf16[16,128,256]{2,1,0:T(8,128)(2,1)}, u32[]{:S(2)}, u32[]{:S(2)}) collective-permute-start(bf16[16,128,256]{2,1,0:T(8,128)(2,1)} %vertical_fwd.15), channel_id=1, source_target_pairs={{0,1},{1,0},{2,3},{3,2},{4,5},{5,4},{6,7},{7,6},{8,9},{9,8},{10,11... | collective-permute-start | bytes 3145736 | tf_op jit(solution)/shard_map/ppermute | solution.py:369
  229.1 72.2 %all-to-all-start.1 = ((bf16[4,4,16,16,256]{4,3,2,1,0:T(8,128)(2,1)}), bf16[4,4,16,16,256]{4,3,2,1,0:T(8,128)(2,1)}, u32[]{:S(2)}, u32[]{:S(2)}) async-start(bf16[4,4,16,16,256]{4,3,2,1,0:T(8,128)(2,1)} %copy.44), calls=%async_computation.1 | async-start | bytes 4194304 | tf_op jit(solution)/shard_map/all_to_all | solution.py:374
  249.1 13.3 %collective-permute-start.11 = (bf16[4,16,16,256]{3,2,1,0:T(8,128)(2,1)}, bf16[4,16,16,256]{3,2,1,0:T(8,128)(2,1)S(1)}, u32[]{:S(2)}, u32[]{:S(2)}) collective-permute-start(bf16[4,16,16,256]{3,2,1,0:T(8,128)(2,1)} %get-tuple-element.53), channel_id=1, source_target_pairs={{0,8},{2,10},{4,12},{6,14},{8,16},{10,18},{12,20},{14,22},{16,24},... | collective-permute-start | bytes 1572872 | tf_op jit(solution)/shard_map/ppermute | solution.py:379
  249.1 45.2 %collective-permute-start.12 = (bf16[4,16,16,256]{3,2,1,0:T(8,128)(2,1)}, bf16[4,16,16,256]{3,2,1,0:T(8,128)(2,1)S(1)}, u32[]{:S(2)}, u32[]{:S(2)}) collective-permute-start(bf16[4,16,16,256]{3,2,1,0:T(8,128)(2,1)} %get-tuple-element.54), channel_id=1, source_target_pairs={{0,16},{2,18},{4,20},{6,22},{8,24},{10,26},{12,28},{14,30},{16,0},... | collective-permute-start | bytes 1572872 | tf_op jit(solution)/shard_map/ppermute | solution.py:379
  252.1 46.3 %collective-permute-start.13 = (bf16[4,16,16,256]{3,2,1,0:T(8,128)(2,1)}, bf16[4,16,16,256]{3,2,1,0:T(8,128)(2,1)S(1)}, u32[]{:S(2)}, u32[]{:S(2)}) collective-permute-start(bf16[4,16,16,256]{3,2,1,0:T(8,128)(2,1)} %get-tuple-element.55), channel_id=1, source_target_pairs={{0,24},{2,26},{4,28},{6,30},{8,0},{10,2},{12,4},{14,6},{16,8},{18,... | collective-permute-start | bytes 1572872 | tf_op jit(solution)/shard_map/ppermute | solution.py:379
  301.3 40.5 %all-to-all-start.2 = ((bf16[4,4,16,16,256]{4,3,2,1,0:T(8,128)(2,1)}), bf16[4,4,16,16,256]{4,3,2,1,0:T(8,128)(2,1)S(1)}, u32[]{:S(2)}, u32[]{:S(2)}) async-start(bf16[4,4,16,16,256]{4,3,2,1,0:T(8,128)(2,1)} %copy.45), calls=%async_computation.2 | async-start | bytes 4194304 | tf_op jit(solution)/shard_map/all_to_all | solution.py:374
  343.1 41.9 %all-to-all-start.9 = ((bf16[4,4,16,16,256]{4,3,2,1,0:T(8,128)(2,1)}), bf16[4,4,16,16,256]{4,3,2,1,0:T(8,128)(2,1)}, u32[]{:S(2)}, u32[]{:S(2)}) async-start(bf16[4,4,16,16,256]{4,3,2,1,0:T(8,128)(2,1)} %bitcast.125), calls=%async_computation.9 | async-start | bytes 4194304 | tf_op jit(solution)/shard_map/all_to_all | solution.py:374
  418.2 61.1 %all-to-all-start.8 = ((bf16[4,4,16,16,256]{4,3,2,1,0:T(8,128)(2,1)}), bf16[4,4,16,16,256]{4,3,2,1,0:T(8,128)(2,1)S(1)}, u32[]{:S(2)}, u32[]{:S(2)}) async-start(bf16[4,4,16,16,256]{4,3,2,1,0:T(8,128)(2,1)} %bitcast.124), calls=%async_computation.8 | async-start | bytes 4194304 | tf_op jit(solution)/shard_map/all_to_all | solution.py:374
  426.1 13.1 %collective-permute-start.40 = (bf16[4,16,16,256]{3,2,1,0:T(8,128)(2,1)S(1)}, bf16[4,16,16,256]{3,2,1,0:T(8,128)(2,1)S(1)}, u32[]{:S(2)}, u32[]{:S(2)}) collective-permute-start(bf16[4,16,16,256]{3,2,1,0:T(8,128)(2,1)S(1)} %get-tuple-element.82), channel_id=1, source_target_pairs={{0,8},{2,10},{4,12},{6,14},{8,16},{10,18},{12,20},{14,22},{16,24},... | collective-permute-start | bytes 1572872 | tf_op jit(solution)/shard_map/ppermute | solution.py:379
  426.1 44.9 %collective-permute-start.39 = (bf16[4,16,16,256]{3,2,1,0:T(8,128)(2,1)S(1)}, bf16[4,16,16,256]{3,2,1,0:T(8,128)(2,1)S(1)}, u32[]{:S(2)}, u32[]{:S(2)}) collective-permute-start(bf16[4,16,16,256]{3,2,1,0:T(8,128)(2,1)S(1)} %get-tuple-element.83), channel_id=1, source_target_pairs={{0,16},{2,18},{4,20},{6,22},{8,24},{10,26},{12,28},{14,30},{16,0},... | collective-permute-start | bytes 1572872 | tf_op jit(solution)/shard_map/ppermute | solution.py:379
  426.1 45.5 %collective-permute-start.38 = (bf16[4,16,16,256]{3,2,1,0:T(8,128)(2,1)S(1)}, bf16[4,16,16,256]{3,2,1,0:T(8,128)(2,1)S(1)}, u32[]{:S(2)}, u32[]{:S(2)}) collective-permute-start(bf16[4,16,16,256]{3,2,1,0:T(8,128)(2,1)S(1)} %get-tuple-element.84), channel_id=1, source_target_pairs={{0,24},{2,26},{4,28},{6,30},{8,0},{10,2},{12,4},{14,6},{16,8},{18,... | collective-permute-start | bytes 1572872 | tf_op jit(solution)/shard_map/ppermute | solution.py:379
  439.2 32.4 %copy-start.29 = (bf16[4,16,16,256]{3,2,1,0:T(8,128)(2,1)}, bf16[4,16,16,256]{3,2,1,0:T(8,128)(2,1)S(1)}, u32[]{:S(2)}) copy-start(bf16[4,16,16,256]{3,2,1,0:T(8,128)(2,1)S(1)} %collective-permute-done.40.rest_3_) | copy-start | bytes 1572868
  480.7 88.3 %all-to-all-start.7 = ((bf16[4,4,16,16,256]{4,3,2,1,0:T(8,128)(2,1)}), bf16[4,4,16,16,256]{4,3,2,1,0:T(8,128)(2,1)S(1)}, u32[]{:S(2)}, u32[]{:S(2)}) async-start(bf16[4,4,16,16,256]{4,3,2,1,0:T(8,128)(2,1)} %bitcast.123), calls=%async_computation.7 | async-start | bytes 4194304 | tf_op jit(solution)/shard_map/all_to_all | solution.py:374
  484.8 9.6 %copy-start.5 = (bf16[4,4,16,16,256]{4,3,2,1,0:T(8,128)(2,1)S(1)}, bf16[4,4,16,16,256]{4,3,2,1,0:T(8,128)(2,1)}, u32[]{:S(2)}) copy-start(bf16[4,4,16,16,256]{4,3,2,1,0:T(8,128)(2,1)} %copy-done.4) | copy-start | bytes 6291460
  486.9 8.7 %collective-permute-start.28 = (bf16[4,16,8,256]{3,2,1,0:T(8,128)(2,1)S(1)}, bf16[4,16,8,256]{3,2,1,0:T(8,128)(2,1)S(1)}, u32[]{:S(2)}, u32[]{:S(2)}) collective-permute-start(bf16[4,16,8,256]{3,2,1,0:T(8,128)(2,1)S(1)} %get-tuple-element.96), channel_id=1, source_target_pairs={{0,8},{2,10},{4,12},{6,14},{8,16},{10,18},{12,20},{14,22},{16,24},... | collective-permute-start | bytes 786440 | tf_op jit(solution)/shard_map/ppermute | solution.py:379
  486.9 16.8 %collective-permute-start.27 = (bf16[4,16,8,256]{3,2,1,0:T(8,128)(2,1)S(1)}, bf16[4,16,8,256]{3,2,1,0:T(8,128)(2,1)S(1)}, u32[]{:S(2)}, u32[]{:S(2)}) collective-permute-start(bf16[4,16,8,256]{3,2,1,0:T(8,128)(2,1)S(1)} %get-tuple-element.97), channel_id=1, source_target_pairs={{0,16},{2,18},{4,20},{6,22},{8,24},{10,26},{12,28},{14,30},{16,0},... | collective-permute-start | bytes 786440 | tf_op jit(solution)/shard_map/ppermute | solution.py:379
  490.8 29.8 %collective-permute-start.24 = (bf16[4,16,8,256]{3,2,1,0:T(8,128)(2,1)S(1)}, bf16[4,16,8,256]{3,2,1,0:T(8,128)(2,1)S(1)}, u32[]{:S(2)}, u32[]{:S(2)}) collective-permute-start(bf16[4,16,8,256]{3,2,1,0:T(8,128)(2,1)S(1)} %get-tuple-element.100), channel_id=1, source_target_pairs={{0,8},{2,10},{4,12},{6,14},{8,16},{10,18},{12,20},{14,22},{16,24},... | collective-permute-start | bytes 786440 | tf_op jit(solution)/shard_map/ppermute | solution.py:379
  491.1 40.8 %collective-permute-start.23 = (bf16[4,16,8,256]{3,2,1,0:T(8,128)(2,1)S(1)}, bf16[4,16,8,256]{3,2,1,0:T(8,128)(2,1)S(1)}, u32[]{:S(2)}, u32[]{:S(2)}) collective-permute-start(bf16[4,16,8,256]{3,2,1,0:T(8,128)(2,1)S(1)} %get-tuple-element.101), channel_id=1, source_target_pairs={{0,16},{2,18},{4,20},{6,22},{8,24},{10,26},{12,28},{14,30},{16,0},... | collective-permute-start | bytes 786440 | tf_op jit(solution)/shard_map/ppermute | solution.py:379
  494.4 58.7 %collective-permute-start.22 = (bf16[4,16,8,256]{3,2,1,0:T(8,128)(2,1)S(1)}, bf16[4,16,8,256]{3,2,1,0:T(8,128)(2,1)S(1)}, u32[]{:S(2)}, u32[]{:S(2)}) collective-permute-start(bf16[4,16,8,256]{3,2,1,0:T(8,128)(2,1)S(1)} %get-tuple-element.102), channel_id=1, source_target_pairs={{0,24},{2,26},{4,28},{6,30},{8,0},{10,2},{12,4},{14,6},{16,8},{18,... | collective-permute-start | bytes 786440 | tf_op jit(solution)/shard_map/ppermute | solution.py:379
  495.6 64.2 %copy-start.32 = (bf16[4,16,8,256]{3,2,1,0:T(8,128)(2,1)}, bf16[4,16,8,256]{3,2,1,0:T(8,128)(2,1)S(1)}, u32[]{:S(2)}) copy-start(bf16[4,16,8,256]{3,2,1,0:T(8,128)(2,1)S(1)} %collective-permute-done.28.rest_3_) | copy-start | bytes 786436
  495.6 115.1 %collective-permute-start.41 = (bf16[16,128,256]{2,1,0:T(8,128)(2,1)}, bf16[16,128,256]{2,1,0:T(8,128)(2,1)}, u32[]{:S(2)}, u32[]{:S(2)}) collective-permute-start(bf16[16,128,256]{2,1,0:T(8,128)(2,1)} %get-tuple-element.80), channel_id=1, source_target_pairs={{0,1},{1,0},{2,3},{3,2},{4,5},{5,4},{6,7},{7,6},{8,9},{9,8},{10,11... | collective-permute-start | bytes 3145736 | tf_op jit(solution)/shard_map/ppermute | solution.py:369
  503.8 56.1 %copy-start.33 = (bf16[4,16,8,256]{3,2,1,0:T(8,128)(2,1)}, bf16[4,16,8,256]{3,2,1,0:T(8,128)(2,1)S(1)}, u32[]{:S(2)}) copy-start(bf16[4,16,8,256]{3,2,1,0:T(8,128)(2,1)S(1)} %collective-permute-done.27.rest_2_) | copy-start | bytes 786436
  503.8 60.1 %collective-permute-start.26 = (bf16[4,16,8,256]{3,2,1,0:T(8,128)(2,1)S(1)}, bf16[4,16,8,256]{3,2,1,0:T(8,128)(2,1)S(1)}, u32[]{:S(2)}, u32[]{:S(2)}) collective-permute-start(bf16[4,16,8,256]{3,2,1,0:T(8,128)(2,1)S(1)} %get-tuple-element.98), channel_id=1, source_target_pairs={{0,24},{2,26},{4,28},{6,30},{8,0},{10,2},{12,4},{14,6},{16,8},{18,... | collective-permute-start | bytes 786440 | tf_op jit(solution)/shard_map/ppermute | solution.py:379
  520.6 39.2 %copy-start.34 = (bf16[4,16,8,256]{3,2,1,0:T(8,128)(2,1)}, bf16[4,16,8,256]{3,2,1,0:T(8,128)(2,1)S(1)}, u32[]{:S(2)}) copy-start(bf16[4,16,8,256]{3,2,1,0:T(8,128)(2,1)S(1)} %collective-permute-done.24.rest_3_) | copy-start | bytes 786436
  520.6 49.4 %collective-permute-start.36 = (bf16[4,16,16,256]{3,2,1,0:T(8,128)(2,1)}, bf16[4,16,16,256]{3,2,1,0:T(8,128)(2,1)}, u32[]{:S(2)}, u32[]{:S(2)}) collective-permute-start(bf16[4,16,16,256]{3,2,1,0:T(8,128)(2,1)} %get-tuple-element.86), channel_id=1, source_target_pairs={{0,8},{2,10},{4,12},{6,14},{8,16},{10,18},{12,20},{14,22},{16,24},... | collective-permute-start | bytes 1572872 | tf_op jit(solution)/shard_map/ppermute | solution.py:379
  531.9 27.9 %copy-start.35 = (bf16[4,16,8,256]{3,2,1,0:T(8,128)(2,1)}, bf16[4,16,8,256]{3,2,1,0:T(8,128)(2,1)S(1)}, u32[]{:S(2)}) copy-start(bf16[4,16,8,256]{3,2,1,0:T(8,128)(2,1)S(1)} %collective-permute-done.23.rest_2_) | copy-start | bytes 786436
  531.9 45.1 %collective-permute-start.35 = (bf16[4,16,16,256]{3,2,1,0:T(8,128)(2,1)}, bf16[4,16,16,256]{3,2,1,0:T(8,128)(2,1)}, u32[]{:S(2)}, u32[]{:S(2)}) collective-permute-start(bf16[4,16,16,256]{3,2,1,0:T(8,128)(2,1)} %get-tuple-element.87), channel_id=1, source_target_pairs={{0,16},{2,18},{4,20},{6,22},{8,24},{10,26},{12,28},{14,30},{16,0},... | collective-permute-start | bytes 1572872 | tf_op jit(solution)/shard_map/ppermute | solution.py:379
  553.0 50.7 %collective-permute-start.34 = (bf16[4,16,16,256]{3,2,1,0:T(8,128)(2,1)S(1)}, bf16[4,16,16,256]{3,2,1,0:T(8,128)(2,1)}, u32[]{:S(2)}, u32[]{:S(2)}) collective-permute-start(bf16[4,16,16,256]{3,2,1,0:T(8,128)(2,1)S(1)} %get-tuple-element.88), channel_id=1, source_target_pairs={{0,24},{2,26},{4,28},{6,30},{8,0},{10,2},{12,4},{14,6},{16,8},{18,... | collective-permute-start | bytes 1572872 | tf_op jit(solution)/shard_map/ppermute | solution.py:379
  563.8 127.3 %collective-permute-start.25 = (bf16[8,128,256]{2,1,0:T(8,128)(2,1)}, bf16[8,128,256]{2,1,0:T(8,128)(2,1)S(1)}, u32[]{:S(2)}, u32[]{:S(2)}) collective-permute-start(bf16[8,128,256]{2,1,0:T(8,128)(2,1)} %get-tuple-element.69), channel_id=1, source_target_pairs={{0,1},{1,0},{2,3},{3,2},{4,5},{5,4},{6,7},{7,6},{8,9},{9,8},{10,11... | collective-permute-start | bytes 1572872 | tf_op jit(solution)/shard_map/ppermute | solution.py:369
  570.0 48.7 %collective-permute-start.32 = (bf16[4,16,16,256]{3,2,1,0:T(8,128)(2,1)S(1)}, bf16[4,16,16,256]{3,2,1,0:T(8,128)(2,1)S(1)}, u32[]{:S(2)}, u32[]{:S(2)}) collective-permute-start(bf16[4,16,16,256]{3,2,1,0:T(8,128)(2,1)S(1)} %get-tuple-element.90), channel_id=1, source_target_pairs={{0,8},{2,10},{4,12},{6,14},{8,16},{10,18},{12,20},{14,22},{16,24},... | collective-permute-start | bytes 1572872 | tf_op jit(solution)/shard_map/ppermute | solution.py:379
  577.0 44.8 %collective-permute-start.31 = (bf16[4,16,16,256]{3,2,1,0:T(8,128)(2,1)S(1)}, bf16[4,16,16,256]{3,2,1,0:T(8,128)(2,1)S(1)}, u32[]{:S(2)}, u32[]{:S(2)}) collective-permute-start(bf16[4,16,16,256]{3,2,1,0:T(8,128)(2,1)S(1)} %get-tuple-element.91), channel_id=1, source_target_pairs={{0,16},{2,18},{4,20},{6,22},{8,24},{10,26},{12,28},{14,30},{16,0},... | collective-permute-start | bytes 1572872 | tf_op jit(solution)/shard_map/ppermute | solution.py:379
  603.7 22.4 %collective-permute-start.30 = (bf16[4,16,16,256]{3,2,1,0:T(8,128)(2,1)S(1)}, bf16[4,16,16,256]{3,2,1,0:T(8,128)(2,1)S(1)}, u32[]{:S(2)}, u32[]{:S(2)}) collective-permute-start(bf16[4,16,16,256]{3,2,1,0:T(8,128)(2,1)S(1)} %get-tuple-element.92), channel_id=1, source_target_pairs={{0,24},{2,26},{4,28},{6,30},{8,0},{10,2},{12,4},{14,6},{16,8},{18,... | collective-permute-start | bytes 1572872 | tf_op jit(solution)/shard_map/ppermute | solution.py:379
  610.7 8.0 %copy-start.23 = (bf16[8,128,256]{2,1,0:T(8,128)(2,1)S(1)}, bf16[8,128,256]{2,1,0:T(8,128)(2,1)}, u32[]{:S(2)}) copy-start(bf16[8,128,256]{2,1,0:T(8,128)(2,1)} %get-tuple-element.71) | copy-start | bytes 1572868
  610.7 31.1 %collective-permute-start.37 = (bf16[16,128,256]{2,1,0:T(8,128)(2,1)}, bf16[16,128,256]{2,1,0:T(8,128)(2,1)S(1)}, u32[]{:S(2)}, u32[]{:S(2)}) collective-permute-start(bf16[16,128,256]{2,1,0:T(8,128)(2,1)} %get-tuple-element.77), channel_id=1, source_target_pairs={{0,1},{1,0},{2,3},{3,2},{4,5},{5,4},{6,7},{7,6},{8,9},{9,8},{10,11... | collective-permute-start | bytes 3145736 | tf_op jit(solution)/shard_map/ppermute | solution.py:369
  618.8 62.4 %collective-permute-start.29 = (bf16[8,128,256]{2,1,0:T(8,128)(2,1)S(1)}, bf16[8,128,256]{2,1,0:T(8,128)(2,1)S(1)}, u32[]{:S(2)}, u32[]{:S(2)}) collective-permute-start(bf16[8,128,256]{2,1,0:T(8,128)(2,1)S(1)} %copy-done.23), channel_id=1, source_target_pairs={{0,1},{1,0},{2,3},{3,2},{4,5},{5,4},{6,7},{7,6},{8,9},{9,8},{10,11... | collective-permute-start | bytes 1572872 | tf_op jit(solution)/shard_map/ppermute | solution.py:369
  633.9 35.0 %collective-permute-start.33 = (bf16[16,128,256]{2,1,0:T(8,128)(2,1)}, bf16[16,128,256]{2,1,0:T(8,128)(2,1)S(1)}, u32[]{:S(2)}, u32[]{:S(2)}) collective-permute-start(bf16[16,128,256]{2,1,0:T(8,128)(2,1)} %get-tuple-element.74), channel_id=1, source_target_pairs={{0,1},{1,0},{2,3},{3,2},{4,5},{5,4},{6,7},{7,6},{8,9},{9,8},{10,11... | collective-permute-start | bytes 3145736 | tf_op jit(solution)/shard_map/ppermute | solution.py:369
  (25 other events, 64.5 us)
